TPU v7x, 128 devices: a whole 4x4x4 slice. The times are simulated.
128 devices in a mesh: sub: 16 (over z, y), fsdp: 8 (over x, core).
Axes of the slice: x: 4, y: 4, z: 4, core: 2. Of those that a mesh axis runs over, the one named last changes fastest.
Arguments:
- x_in: bfloat16 [128, 192, 1536], P(('sub', 'fsdp'))
- w_q: bfloat16 [2, 1536, 12, 128], P(None, ('sub', 'fsdp'))
- w_k: bfloat16 [2, 1536, 2, 128], P(None, ('sub', 'fsdp'))
- w_v: bfloat16 [2, 1536, 2, 128], P(None, ('sub', 'fsdp'))
- w_o: bfloat16 [2, 1536, 12, 128], P(None, ('sub', 'fsdp'))
- w_up: bfloat16 [2, 1536, 8960], P(None, ('sub', 'fsdp'))
- w_down: bfloat16 [2, 8960, 1536], P(None, ('sub', 'fsdp'))
- grad_out: bfloat16 [128, 192, 1536], P(('sub', 'fsdp'))
Outputs:
- output 1: bfloat16 [128, 192, 1536], P(('sub', 'fsdp'))
- output 2: bfloat16 [128, 192, 1536], P(('sub', 'fsdp'))
- output 3: float32 [2, 1536, 12, 128], P(None, ('sub', 'fsdp'))
- output 4: float32 [2, 1536, 2, 128], P(None, ('sub', 'fsdp'))
- output 5: float32 [2, 1536, 2, 128], P(None, ('sub', 'fsdp'))
- output 6: float32 [2, 1536, 12, 128], P(None, ('sub', 'fsdp'))
- output 7: float32 [2, 1536, 8960], P(None, ('sub', 'fsdp'))
- output 8: float32 [2, 8960, 1536], P(None, ('sub', 'fsdp'))
All inputs are finite; a program needn't handle non-finite values.
Results may differ from a plain program's by a relative error of at most 0.02.
Values are sent between devices in bfloat16 or wider.
A program may use at most 1 GiB of HBM per device.

v0:
```python
import jax
import jax.numpy as jnp
from jax import lax
from jax.sharding import PartitionSpec as P

AXES = ("sub", "fsdp")
EPS = 1e-6
MASK_FILL = -1e30


def rms_norm(values):
    return values * lax.rsqrt(jnp.mean(values * values, axis=-1, keepdims=True) + EPS)


def norm_bf16(x_loc):
    return rms_norm(x_loc.astype(jnp.float32)).astype(jnp.bfloat16)


def norm_back(x_loc, grad_norm):
    _, pull_back = jax.vjp(rms_norm, x_loc.astype(jnp.float32))
    return pull_back(grad_norm)[0]


def mixed(form, left, right):
    return jnp.einsum(form, left, right, preferred_element_type=jnp.float32)


def grouped(weight, kv_heads):
    width, heads, head_dim = weight.shape
    return weight.reshape(width, kv_heads, heads // kv_heads, head_dim)


def attn_inner(x_loc, q_weight, k_weight, v_weight):
    kv_heads = k_weight.shape[1]
    scale = k_weight.shape[2] ** -0.5
    normed = norm_bf16(x_loc)
    q_act = mixed("bsd,dkge->bskge", normed, grouped(q_weight, kv_heads)).astype(jnp.bfloat16)
    k_act = mixed("bsd,dke->bske", normed, k_weight).astype(jnp.bfloat16)
    v_act = mixed("bsd,dke->bske", normed, v_weight).astype(jnp.bfloat16)
    scores = mixed("bskge,btke->bkgst", q_act, k_act) * scale
    positions = jnp.arange(x_loc.shape[1])
    causal = positions[:, None] >= positions[None, :]
    p_float = jax.nn.softmax(jnp.where(causal, scores, MASK_FILL), axis=-1)
    p_bf16 = p_float.astype(jnp.bfloat16)
    o_act = mixed("bkgst,btke->bskge", p_bf16, v_act).astype(jnp.bfloat16)
    return normed, q_act, k_act, v_act, p_float, p_bf16, o_act


def attn_forward(x_loc, q_weight, k_weight, v_weight, o_weight):
    o_act = attn_inner(x_loc, q_weight, k_weight, v_weight)[6]
    proj = mixed("bskge,dkge->bsd", o_act, grouped(o_weight, k_weight.shape[1]))
    return (x_loc.astype(jnp.float32) + proj).astype(jnp.bfloat16)


def attn_backward(x_loc, q_weight, k_weight, v_weight, o_weight, grad_y):
    kv_heads = k_weight.shape[1]
    scale = k_weight.shape[2] ** -0.5
    normed, q_act, k_act, v_act, p_float, p_bf16, o_act = attn_inner(x_loc, q_weight, k_weight, v_weight)
    d_o_w = mixed("bsd,bskge->dkge", grad_y, o_act).reshape(o_weight.shape)
    d_o = mixed("bsd,dkge->bskge", grad_y, grouped(o_weight, kv_heads)).astype(jnp.bfloat16)
    d_p = mixed("bskge,btke->bkgst", d_o, v_act)
    d_v = mixed("bkgst,bskge->btke", p_bf16, d_o).astype(jnp.bfloat16)
    d_s = p_float * (d_p - jnp.sum(p_float * d_p, axis=-1, keepdims=True))
    ds_bf16 = (d_s * scale).astype(jnp.bfloat16)
    d_q = mixed("bkgst,btke->bskge", ds_bf16, k_act).astype(jnp.bfloat16)
    d_k = mixed("bkgst,bskge->btke", ds_bf16, q_act).astype(jnp.bfloat16)
    d_q_w = mixed("bsd,bskge->dkge", normed, d_q).reshape(q_weight.shape)
    d_k_w = mixed("bsd,bske->dke", normed, d_k)
    d_v_w = mixed("bsd,bske->dke", normed, d_v)
    d_norm = (mixed("bskge,dkge->bsd", d_q, grouped(q_weight, kv_heads))
              + mixed("bske,dke->bsd", d_k, k_weight)
              + mixed("bske,dke->bsd", d_v, v_weight))
    grad_x = (grad_y.astype(jnp.float32) + norm_back(x_loc, d_norm)).astype(jnp.bfloat16)
    return grad_x, d_q_w, d_k_w, d_v_w, d_o_w


def mlp_forward(x_loc, up_weight, down_weight):
    normed = norm_bf16(x_loc)
    gelu_act = jax.nn.gelu(mixed("bsd,df->bsf", normed, up_weight)).astype(jnp.bfloat16)
    proj = mixed("bsf,fd->bsd", gelu_act, down_weight)
    return (x_loc.astype(jnp.float32) + proj).astype(jnp.bfloat16)


def mlp_backward(x_loc, up_weight, down_weight, grad_y):
    normed = norm_bf16(x_loc)
    gelu_f32, gelu_pull = jax.vjp(jax.nn.gelu, mixed("bsd,df->bsf", normed, up_weight))
    gelu_act = gelu_f32.astype(jnp.bfloat16)
    d_down = mixed("bsf,bsd->fd", gelu_act, grad_y)
    d_hid = gelu_pull(mixed("bsd,fd->bsf", grad_y, down_weight))[0].astype(jnp.bfloat16)
    d_up = mixed("bsd,bsf->df", normed, d_hid)
    d_norm = mixed("bsf,df->bsd", d_hid, up_weight)
    grad_x = (grad_y.astype(jnp.float32) + norm_back(x_loc, d_norm)).astype(jnp.bfloat16)
    return grad_x, d_up, d_down


def gather_all(shard):
    return lax.all_gather(shard, AXES, axis=0, tiled=True)


def scatter_sum(grad_full):
    return lax.psum_scatter(grad_full, AXES, scatter_dimension=0, tiled=True)


def solution(mesh):
    row_spec = P(AXES)
    weight_spec = P(None, AXES)

    def body(x_loc, w_q, w_k, w_v, w_o, w_up, w_down, grad_out):
        pairs = w_q.shape[0]
        carry_x = x_loc
        layer_inputs = []
        mlp_copies = []
        for layer in range(pairs):
            attn_full = [gather_all(weight[layer]) for weight in (w_q, w_k, w_v, w_o)]
            layer_inputs.append(carry_x)
            carry_x = attn_forward(carry_x, attn_full[0], attn_full[1], attn_full[2], attn_full[3])
            up_copy = lax.all_gather(w_up[layer], "fsdp", axis=0, tiled=True)
            down_copy = lax.all_gather(w_down[layer], "fsdp", axis=0, tiled=True)
            mlp_copies.append((up_copy, down_copy))
            up_full = lax.all_gather(up_copy, "sub", axis=0, tiled=True)
            down_full = lax.all_gather(down_copy, "sub", axis=0, tiled=True)
            layer_inputs.append(carry_x)
            carry_x = mlp_forward(carry_x, up_full, down_full)
        y_loc = carry_x
        grad_x = grad_out
        grad_lists = ([], [], [], [], [], [])
        for layer in reversed(range(pairs)):
            up_copy, down_copy, grad_x = lax.optimization_barrier(
                (mlp_copies[layer][0], mlp_copies[layer][1], grad_x))
            up_full = lax.all_gather(up_copy, "sub", axis=0, tiled=True)
            down_full = lax.all_gather(down_copy, "sub", axis=0, tiled=True)
            grad_x, d_up, d_down = mlp_backward(layer_inputs[2 * layer + 1], up_full, down_full, grad_x)
            grad_lists[4].append(scatter_sum(d_up))
            grad_lists[5].append(scatter_sum(d_down))
            attn_shards, grad_x = lax.optimization_barrier(
                ([weight[layer] for weight in (w_q, w_k, w_v, w_o)], grad_x))
            attn_full = [gather_all(shard) for shard in attn_shards]
            attn_grads = attn_backward(layer_inputs[2 * layer], attn_full[0], attn_full[1], attn_full[2],
                                       attn_full[3], grad_x)
            grad_x = attn_grads[0]
            for index in range(4):
                grad_lists[index].append(scatter_sum(attn_grads[index + 1]))
        return (y_loc, grad_x) + tuple(jnp.stack(grad_list[::-1]) for grad_list in grad_lists)

    return jax.shard_map(body, mesh=mesh, in_specs=(row_spec,) + (weight_spec,) * 6 + (row_spec,),
                         out_specs=(row_spec, row_spec) + (weight_spec,) * 6, check_vma=False)
```

profile of v0, /device:TPU:1, one launch (start us, length us, event | category | flops | bytes accessed | tf_op | source)
XLA Modules:
  0.0 3820.8 jit_solution(17678962324908272438)
XLA Ops:
  16.1 26.4 all-gather.61.cloned.1.call-done
  46.2 27.2 all-gather.57.cloned.1.call-done
  76.8 27.5 all-gather.73.cloned.1.call-done
  107.9 27.1 all-gather.69.cloned.1.call-done
  141.0 36.5 all-gather.1
  177.8 34.5 all-gather.9
  212.3 33.8 all-gather.8
  246.1 34.9 all-gather
  281.1 6.2 copy.103
  293.4 52.2 %all-gather.67.cloned.1.call-done = bf16[1,1536,12,128]{3,2,0,1:T(8,128)(2,1)} async-done(((bf16[1,12,12,128]{3,2,0,1:T(8,128)(2,1)}), bf16[1,1536,12,128]{3,2,0,1:T(8,128)(2,1)}) %all-gather.67.cloned.1.call-update) | async-done | bytes 4718608 | tf_op jit(solution)/shard_map/all_gather | solution.py:97
  351.7 62.7 %all-gather.55.cloned.1.call-done = bf16[1,1536,12,128]{3,2,0,1:T(8,128)(2,1)} async-done(((bf16[1,12,12,128]{3,2,0,1:T(8,128)(2,1)}), bf16[1,1536,12,128]{3,2,0,1:T(8,128)(2,1)}) %all-gather.55.cloned.1.call-update) | async-done | bytes 4718608 | tf_op jit(solution)/shard_map/all_gather | solution.py:97
  414.4 6.1 copy.92
  432.5 147.1 %all-gather.63.cloned.1.call-done = bf16[1,8960,1536]{2,1,0:T(8,128)(2,1)} async-done(((bf16[1,560,1536]{2,1,0:T(8,128)(2,1)}), bf16[1,8960,1536]{2,1,0:T(8,128)(2,1)}) %all-gather.63.cloned.1.call-update) | async-done | bytes 27525136 | tf_op jit(solution)/shard_map/all_gather | solution.py:121
  579.6 167.9 %all-gather.59.cloned.1.call-done = bf16[1,1536,8960]{2,1,0:T(8,128)(2,1)} async-done(((bf16[1,96,8960]{2,1,0:T(8,128)(2,1)}), bf16[1,1536,8960]{2,1,0:T(8,128)(2,1)}) %all-gather.59.cloned.1.call-update) | async-done | bytes 27525136 | tf_op jit(solution)/shard_map/all_gather | solution.py:120
  747.5 21.7 multiply_reduce_fusion.1
  786.8 128.7 %all-gather.39.cloned.1.call-done = bf16[1536,8960]{1,0:T(8,128)(2,1)} async-done(((bf16[96,8960]{1,0:T(8,128)(2,1)}), bf16[1536,8960]{1,0:T(8,128)(2,1)}) %all-gather.39.cloned.1.call-update) | async-done | bytes 27525136 | tf_op jit(solution)/shard_map/all_gather | solution.py:130
  915.5 14.7 fusion.333
  930.2 153.2 %all-gather.37.cloned.1.call-done = bf16[8960,1536]{1,0:T(8,128)(2,1)} async-done(((bf16[560,1536]{1,0:T(8,128)(2,1)}), bf16[8960,1536]{1,0:T(8,128)(2,1)}) %all-gather.37.cloned.1.call-update) | async-done | bytes 27525136 | tf_op jit(solution)/shard_map/all_gather | solution.py:131
  1083.4 17.7 fusion.16
  1101.1 16.1 fusion.198
  1124.9 36.9 all_gather.102
  1162.1 34.4 all_gather.104
  1205.0 54.2 %all-gather.43.cloned.1.call-done = bf16[1536,12,128]{2,1,0:T(8,128)(2,1)} async-done(((bf16[12,12,128]{2,1,0:T(8,128)(2,1)}), bf16[1536,12,128]{2,1,0:T(8,128)(2,1)}) %all-gather.43.cloned.1.call-update) | async-done | bytes 4718608 | tf_op jit(solution)/shard_map/all_gather | solution.py:97
  1275.2 162.6 %all-gather.47.cloned.1.call-done = bf16[1536,8960]{1,0:T(8,128)(2,1)} async-done(((bf16[96,8960]{1,0:T(8,128)(2,1)}), bf16[1536,8960]{1,0:T(8,128)(2,1)}) %all-gather.47.cloned.1.call-update) | async-done | bytes 27525136 | tf_op jit(solution)/shard_map/all_gather | solution.py:130
  1437.8 14.6 fusion.339
  1452.3 153.3 %all-gather.45.cloned.1.call-done = bf16[8960,1536]{1,0:T(8,128)(2,1)} async-done(((bf16[560,1536]{1,0:T(8,128)(2,1)}), bf16[8960,1536]{1,0:T(8,128)(2,1)}) %all-gather.45.cloned.1.call-update) | async-done | bytes 27525136 | tf_op jit(solution)/shard_map/all_gather | solution.py:131
  1605.6 17.7 fusion.23
  1623.3 16.6 fusion.193
  1651.3 23.2 fusion.337
  1675.8 23.2 fusion.331
  1700.6 6.6 copy.133
  1707.7 6.8 copy.131
  1725.7 36.9 all_gather.108
  1763.1 34.8 all_gather.110
  1798.2 6.2 copy.122
  1813.3 6.8 copy.132
  1822.9 6.8 copy.130
  1842.4 23.1 fusion.61
  1865.5 408.3 %fusion.1 = f32[72,1536]{1,0:T(8,128)S(1)} fusion(f32[8960,1536]{1,0:T(8,128)} %fusion.61), kind=kCustom, calls=%all-reduce-scatter.1 | all-reduce-scatter fusion | flops 14155777 | bytes 55492608
  2282.5 23.1 fusion.60
  2305.6 412.9 %fusion = f32[72,1536]{1,0:T(8,128)S(1)} fusion(f32[8960,1536]{1,0:T(8,128)} %fusion.60), kind=kCustom, calls=%all-reduce-scatter | all-reduce-scatter fusion | flops 14155777 | bytes 55492608
  2724.7 94.5 %all-gather.71.cloned.1.call-done = bf16[1,1536,8960]{2,1,0:T(8,128)(2,1)} async-done(((bf16[1,96,8960]{2,1,0:T(8,128)(2,1)}), bf16[1,1536,8960]{2,1,0:T(8,128)(2,1)}) %all-gather.71.cloned.1.call-update) | async-done | bytes 27525136 | tf_op jit(solution)/shard_map/all_gather | solution.py:120
  2819.2 22.2 fusion.150
  2841.5 12.2 concatenate.1
  2856.0 7.0 collective-permute-done.3
  2863.0 11.2 concatenate
  2883.5 311.8 %all-reduce.18.cloned.1.call-done = f32[1536,8960]{1,0:T(8,128)} async-done(((f32[1536,8960]{1,0:T(8,128)}), f32[1536,8960]{1,0:T(8,128)}) %all-reduce.18.cloned.1.call-update) | async-done | bytes 55050256
  3196.5 604.7 %all-reduce.20.cloned.1.call-done = (f32[1536,12,128]{2,0,1:T(8,128)}, f32[1536,12,128]{2,0,1:T(8,128)}, f32[1536,2,128]{2,1,0:T(2,128)}, f32[1536,2,128]{2,1,0:...) async-done(((f32[1536,12,128]{2,0,1:T(8,128)}, ...) | async-done | bytes 99090448
  (303 shorter events, 190.3 us)
Async XLA Ops:
  7.2 35.4 all-gather.61.cloned.1.call-start
  10.1 63.3 %all-gather.57.cloned.1.call-start = ((), (), s32[]{:S(2)}) async-start(), calls=%async_computation.10 | async-start | bytes 3870720 | tf_op jit(solution)/shard_map/all_gather | solution.py:117
  11.7 92.6 %all-gather.73.cloned.1.call-start = ((), (), s32[]{:S(2)}) async-start(), calls=%async_computation.18 | async-start | bytes 3870720 | tf_op jit(solution)/shard_map/all_gather | solution.py:118
  12.4 122.6 %all-gather.69.cloned.1.call-start = ((), (), s32[]{:S(2)}) async-start(), calls=%async_computation.16 | async-start | bytes 3870720 | tf_op jit(solution)/shard_map/all_gather | solution.py:117
  13.0 268.1 %all-gather.65.cloned.1.call-start = ((), (), s32[]{:S(2)}) async-start(), calls=%async_computation.14 | async-start | bytes 6340608 | tf_op jit(solution)/shard_map/all_gather | solution.py:97
  13.8 273.4 %all-gather.53.cloned.1.call-start = ((), (), s32[]{:S(2)}) async-start(), calls=%async_computation.8 | async-start | bytes 6340608 | tf_op jit(solution)/shard_map/all_gather | solution.py:97
  14.5 331.1 %all-gather.67.cloned.1.call-start = ((), (), s32[]{:S(2)}) async-start(), calls=%async_computation.15 | async-start | bytes 6340608 | tf_op jit(solution)/shard_map/all_gather | solution.py:97
  15.3 399.1 %all-gather.55.cloned.1.call-start = ((), (), s32[]{:S(2)}) async-start(), calls=%async_computation.9 | async-start | bytes 6340608 | tf_op jit(solution)/shard_map/all_gather | solution.py:97
  16.1 563.5 %all-gather.63.cloned.1.call-start = ((), (), s32[]{:S(2)}) async-start(), calls=%async_computation.13 | async-start | bytes 29245440 | tf_op jit(solution)/shard_map/all_gather | solution.py:121
  46.2 701.3 %all-gather.59.cloned.1.call-start = ((), (), s32[]{:S(2)}) async-start(), calls=%async_computation.11 | async-start | bytes 29245440 | tf_op jit(solution)/shard_map/all_gather | solution.py:120
  76.8 838.7 %all-gather.39.cloned.1.call-start = ((), (), s32[]{:S(2)}) async-start(), calls=%async_computation.1 | async-start | bytes 29245440 | tf_op jit(solution)/shard_map/all_gather | solution.py:130
  138.5 944.9 %all-gather.37.cloned.1.call-start = ((), (), s32[]{:S(2)}) async-start(), calls=%async_computation | async-start | bytes 29245440 | tf_op jit(solution)/shard_map/all_gather | solution.py:131
  139.1 1057.8 %all-gather.41.cloned.1.call-start = ((), (), s32[]{:S(2)}) async-start(), calls=%async_computation.2 | async-start | bytes 6340608 | tf_op jit(solution)/shard_map/all_gather | solution.py:97
  139.5 1127.6 %copy-start.22 = (pred[192,192]{0,1:T(8,128)(4,1)}, pred[192,192]{0,1:T(8,128)(4,1)S(1)}, u32[]{:S(2)}) copy-start(pred[192,192]{0,1:T(8,128)(4,1)S(1)} %iota_compare_fusion) | copy-start | bytes 110596
  140.3 284.6 %copy-start.51 = (f32[192]{0:T(256)}, f32[192]{0:T(256)S(1)}, u32[]{:S(2)}) copy-start(f32[192]{0:T(256)S(1)} %fusion.307) | copy-start | bytes 2308
  432.4 336.7 %copy-start.8 = (f32[1,192,1536]{2,1,0:T(8,128)}, f32[1,192,1536]{2,1,0:T(8,128)S(1)}, u32[]{:S(2)}) copy-start(f32[1,192,1536]{2,1,0:T(8,128)S(1)} %get-tuple-element.100) | copy-start | bytes 3538948
  432.4 336.7 %copy-start.59 = (f32[192]{0:T(256)}, f32[192]{0:T(256)S(1)}, u32[]{:S(2)}) copy-start(f32[192]{0:T(256)S(1)} %get-tuple-element.99) | copy-start | bytes 2308
  432.5 336.7 %copy-start.48 = (f32[192]{0:T(256)}, f32[192]{0:T(256)S(1)}, u32[]{:S(2)}) copy-start(f32[192]{0:T(256)S(1)} %fusion.308) | copy-start | bytes 2308
  786.8 314.3 %copy-start.5 = (f32[1,192,1536]{2,1,0:T(8,128)}, f32[1,192,1536]{2,1,0:T(8,128)S(1)}, u32[]{:S(2)}) copy-start(f32[1,192,1536]{2,1,0:T(8,128)S(1)} %get-tuple-element.106) | copy-start | bytes 3538948
  786.8 330.4 %copy-start.46 = (f32[192]{0:T(256)}, f32[192]{0:T(256)S(1)}, u32[]{:S(2)}) copy-start(f32[192]{0:T(256)S(1)} %fusion.310) | copy-start | bytes 2308
  915.5 167.9 %copy-start.35 = (bf16[1,192,1536]{2,1,0:T(8,128)(2,1)S(1)}, bf16[1,192,1536]{2,1,0:T(8,128)(2,1)}, u32[]{:S(2)}) copy-start(bf16[1,192,1536]{2,1,0:T(8,128)(2,1)} %param.15) | copy-start | bytes 1769476
  1120.3 138.9 %all-gather.43.cloned.1.call-start = ((), (), s32[]{:S(2)}) async-start(), calls=%async_computation.3 | async-start | bytes 6340608 | tf_op jit(solution)/shard_map/all_gather | solution.py:97
  1120.9 316.9 %all-gather.47.cloned.1.call-start = ((), (), s32[]{:S(2)}) async-start(), calls=%async_computation.5 | async-start | bytes 29245440 | tf_op jit(solution)/shard_map/all_gather | solution.py:130
  1123.5 38.3 %copy-start.13 = (bf16[1,192,1536]{2,1,0:T(8,128)(2,1)S(1)}, bf16[1,192,1536]{2,1,0:T(8,128)(2,1)}, u32[]{:S(2)}) copy-start(bf16[1,192,1536]{2,1,0:T(8,128)(2,1)} %copy-done.12) | copy-start | bytes 1769476
  1161.8 39.1 %copy-start.28 = (bf16[1536,2,128]{2,1,0:T(2,128)(2,1)}, bf16[1536,2,128]{2,1,0:T(2,128)(2,1)S(1)}, u32[]{:S(2)}) copy-start(bf16[1536,2,128]{2,1,0:T(2,128)(2,1)S(1)} %all_gather.102) | copy-start | bytes 2359300
  1196.9 69.4 %copy-start.60 = (bf16[192,2,128,1]{2,0,3,1:T(8,128)(2,1)}, bf16[192,2,128,1]{2,0,3,1:T(8,128)(2,1)S(1)}, u32[]{:S(2)}) copy-start(bf16[192,2,128,1]{2,0,3,1:T(8,128)(2,1)S(1)} %fusion.222) | copy-start | bytes 294916
  1205.0 58.2 %copy-start.16 = (bf16[1,192,1536]{2,1,0:T(8,128)(2,1)S(1)}, bf16[1,192,1536]{2,1,0:T(8,128)(2,1)}, u32[]{:S(2)}) copy-start(bf16[1,192,1536]{2,1,0:T(8,128)(2,1)} %fusion.178) | copy-start | bytes 1769476
  1274.5 163.2 %copy-start.9 = (f32[1,192,1536]{2,1,0:T(8,128)S(1)}, f32[1,192,1536]{2,1,0:T(8,128)}, u32[]{:S(2)}) copy-start(f32[1,192,1536]{2,1,0:T(8,128)} %copy-done.8) | copy-start | bytes 3538948
  1274.5 331.1 %all-gather.45.cloned.1.call-start = ((), (), s32[]{:S(2)}) async-start(), calls=%async_computation.4 | async-start | bytes 29245440 | tf_op jit(solution)/shard_map/all_gather | solution.py:131
  1275.1 523.1 %all-gather.49.cloned.1.call-start = ((), (), s32[]{:S(2)}) async-start(), calls=%async_computation.6 | async-start | bytes 6340608 | tf_op jit(solution)/shard_map/all_gather | solution.py:97
  1643.3 161.1 %all-gather.51.cloned.1.call-start = ((), (), s32[]{:S(2)}) async-start(), calls=%async_computation.7 | async-start | bytes 6340608 | tf_op jit(solution)/shard_map/all_gather | solution.py:97
  1643.9 1080.8 %all-gather.75.cloned.1.call-start = ((), (), s32[]{:S(2)}) async-start(), calls=%async_computation.19 | async-start | bytes 29245440 | tf_op jit(solution)/shard_map/all_gather | solution.py:121
  1647.6 1171.6 %all-gather.71.cloned.1.call-start = ((), (), s32[]{:S(2)}) async-start(), calls=%async_computation.17 | async-start | bytes 29245440 | tf_op jit(solution)/shard_map/all_gather | solution.py:120
  1651.1 1544.1 %all-reduce.18.cloned.1.call-start = ((), (), s32[]{:S(2)}) async-start(), calls=%async_computation.20 | async-start | bytes 110100480
  1674.6 2126.6 %all-reduce.20.cloned.1.call-start = ((), (), s32[]{:S(2)}) async-start(), calls=%async_computation.21 | async-start | bytes 198180864
  1720.6 42.1 %copy-start.2 = (bf16[1,192,1536]{2,1,0:T(8,128)(2,1)S(1)}, bf16[1,192,1536]{2,1,0:T(8,128)(2,1)}, u32[]{:S(2)}) copy-start(bf16[1,192,1536]{2,1,0:T(8,128)(2,1)} %param.8) | copy-start | bytes 1769476
  1720.6 42.1 %copy-start.52 = (f32[192]{0:T(256)S(1)}, f32[192]{0:T(256)}, u32[]{:S(2)}) copy-start(f32[192]{0:T(256)} %copy-done.51) | copy-start | bytes 2308
  1865.5 417.0 %copy-start.20 = (bf16[1,192,1536]{2,1,0:T(8,128)(2,1)S(1)}, bf16[1,192,1536]{2,1,0:T(8,128)(2,1)}, u32[]{:S(2)}) copy-start(bf16[1,192,1536]{2,1,0:T(8,128)(2,1)} %fusion.180) | copy-start | bytes 1769476
  2274.5 448.3 %collective-permute-start.6 = (f32[72,1536]{1,0:T(8,128)S(1)}, f32[72,1536]{1,0:T(8,128)}, u32[]{:S(2)}, u32[]{:S(2)}) collective-permute-start(f32[72,1536]{1,0:T(8,128)S(1)} %fusion.1), channel_id=1, source_target_pairs={{0,3},{1,4},{2,5},{3,6},{4,7},{5,8},{6,9},{7,10},{8,11},{9,12},{10... | collective-permute-start | bytes 1327112
  2276.5 564.9 %collective-permute-start.5 = (f32[72,1536]{1,0:T(8,128)S(1)}, f32[72,1536]{1,0:T(8,128)}, u32[]{:S(2)}, u32[]{:S(2)}) collective-permute-start(f32[72,1536]{1,0:T(8,128)S(1)} %fusion.1), channel_id=1, source_target_pairs={{0,2},{1,3},{2,4},{3,5},{4,6},{5,7},{6,8},{7,9},{8,10},{9,11},{10,... | collective-permute-start | bytes 1327112
  2278.6 562.9 %collective-permute-start.4 = (f32[72,1536]{1,0:T(8,128)S(1)}, f32[72,1536]{1,0:T(8,128)}, u32[]{:S(2)}, u32[]{:S(2)}) collective-permute-start(f32[72,1536]{1,0:T(8,128)S(1)} %fusion.1), channel_id=1, source_target_pairs={{0,1},{1,2},{2,3},{3,4},{4,5},{5,6},{6,7},{7,8},{8,9},{9,10},{10,1... | collective-permute-start | bytes 1327112
  2280.5 440.1 %collective-permute-start.7 = (f32[38,1536]{1,0:T(8,128)}, f32[38,1536]{1,0:T(8,128)}, u32[]{:S(2)}, u32[]{:S(2)}) collective-permute-start(f32[38,1536]{1,0:T(8,128)} %slice.57), channel_id=1, source_target_pairs={{0,4},{1,5},{2,6},{3,7},{4,8},{5,9},{6,10},{7,11},{8,12},{9,13},{1... | collective-permute-start | bytes 700424
  2305.6 513.6 %copy-start.7 = (f32[1,192,1536]{2,1,0:T(8,128)S(1)}, f32[1,192,1536]{2,1,0:T(8,128)}, u32[]{:S(2)}) copy-start(f32[1,192,1536]{2,1,0:T(8,128)} %copy-done.5) | copy-start | bytes 3538948
  2305.6 513.6 %copy-start.47 = (f32[192]{0:T(256)S(1)}, f32[192]{0:T(256)}, u32[]{:S(2)}) copy-start(f32[192]{0:T(256)} %copy-done.46) | copy-start | bytes 2308
  2718.5 144.5 %collective-permute-start.2 = (f32[72,1536]{1,0:T(8,128)S(1)}, f32[72,1536]{1,0:T(8,128)}, u32[]{:S(2)}, u32[]{:S(2)}) collective-permute-start(f32[72,1536]{1,0:T(8,128)S(1)} %fusion), channel_id=1, source_target_pairs={{0,3},{1,4},{2,5},{3,6},{4,7},{5,8},{6,9},{7,10},{8,11},{9,12},{10... | collective-permute-start | bytes 1327112
  2720.6 142.4 %collective-permute-start.1 = (f32[72,1536]{1,0:T(8,128)S(1)}, f32[72,1536]{1,0:T(8,128)}, u32[]{:S(2)}, u32[]{:S(2)}) collective-permute-start(f32[72,1536]{1,0:T(8,128)S(1)} %fusion), channel_id=1, source_target_pairs={{0,2},{1,3},{2,4},{3,5},{4,6},{5,7},{6,8},{7,9},{8,10},{9,11},{10,... | collective-permute-start | bytes 1327112
  2722.7 140.3 %collective-permute-start = (f32[72,1536]{1,0:T(8,128)S(1)}, f32[72,1536]{1,0:T(8,128)}, u32[]{:S(2)}, u32[]{:S(2)}) collective-permute-start(f32[72,1536]{1,0:T(8,128)S(1)} %fusion), channel_id=1, source_target_pairs={{0,1},{1,2},{2,3},{3,4},{4,5},{5,6},{6,7},{7,8},{8,9},{9,10},{10,1... | collective-permute-start | bytes 1327112
  2853.6 9.4 collective-permute-start.3
  (46 other events, 240.5 us)
Sparse Core Ops, SparseCore 0:
  10.3 32.2 all-gather.60
  44.8 28.5 all-gather.56
  75.7 28.5 all-gather.72
  106.4 28.5 all-gather.68
  138.6 68.4 all-gather.64
  210.0 66.1 all-gather.52
  279.8 65.6 all-gather.66
  348.7 65.6 all-gather.54
  416.5 163.0 all-gather.62
  581.6 165.8 all-gather.58
  749.6 165.8 all-gather.38
  917.5 165.8 all-gather.36
  1120.4 69.1 all-gather.40
  1193.1 66.0 all-gather.42
  1274.7 163.0 all-gather.46
  1439.8 165.8 all-gather.44
  1643.5 68.4 all-gather.48
  1715.0 66.0 all-gather.50
  1783.2 494.2 all-gather.74
  2279.5 539.6 all-gather.70
  2824.8 370.3 all-reduce.17
  3201.7 599.4 all-reduce.19
where the time goes:
time: 3830 us; the launch traced here: 3820 us
  waiting for transfers between devices  2210 us (58%)
  blocking collectives  1100 us (29%)
  matrix products  307 us (8%)
  local copies, waits for them, and re-layouts  150 us (4%)
    unnamed x32, waiting for transfers between devices  927 us
    unnamed x2, blocking collectives  821 us
    all_gather x4, waiting for transfers between devices, body(): up_full = lax.all_gather(up_copy, 'sub', axis=0, tiled=True)  554 us
    all_gather x4, waiting for transfers between devices, body(): down_full = lax.all_gather(down_copy, 'sub', axis=0, tiled=True)  454 us
    dot_general x54, matrix products, mixed(): return jnp.einsum(form, left, right, preferred_element_type=jnp.float32)  307 us
    all_gather x8, blocking collectives, gather_all(): return lax.all_gather(shard, AXES, axis=0, tiled=True)  283 us
    all_gather x8, waiting for transfers between devices, gather_all(): return lax.all_gather(shard, AXES, axis=0, tiled=True)  169 us
  transfers between devices with their start and end apart: 30, of which 17 were waited for; matrix products, arithmetic and copies ran while one was open for 31% of the time, Pallas kernels for 0%

commit v1 on v0

v1 whole, which is shorter than its diff:
```python
import jax
import jax.numpy as jnp
from jax import lax
from jax.sharding import Mesh, PartitionSpec as P

CHIP_AXES = ("z", "y", "x")
ALL_AXES = ("z", "y", "x", "c")
EPS = 1e-6
MASK_FILL = -1e30
BLOCK = 72


def rms_norm(values):
    return values * lax.rsqrt(jnp.mean(values * values, axis=-1, keepdims=True) + EPS)


def norm_bf16(x_loc):
    return rms_norm(x_loc.astype(jnp.float32)).astype(jnp.bfloat16)


def norm_back(x_loc, grad_norm):
    _, pull_back = jax.vjp(rms_norm, x_loc.astype(jnp.float32))
    return pull_back(grad_norm)[0]


def mixed(form, left, right):
    return jnp.einsum(form, left, right, preferred_element_type=jnp.float32)


def attn_inner(x_loc, halves, kv_heads, heads, head_dim):
    seq = x_loc.shape[0]
    q_width, kv_width = heads * head_dim, kv_heads * head_dim
    normed = norm_bf16(x_loc)
    qk = mixed("sd,dw->sw", normed, halves[0]).astype(jnp.bfloat16)
    v_act = mixed("sd,dw->sw", normed, halves[1][:, :kv_width]).astype(jnp.bfloat16)
    q_act = qk[:, :q_width].reshape(seq, kv_heads, heads // kv_heads, head_dim)
    k_act = qk[:, q_width:].reshape(seq, kv_heads, head_dim)
    v_act = v_act.reshape(seq, kv_heads, head_dim)
    scores = mixed("skge,tke->kgst", q_act, k_act) * (head_dim ** -0.5)
    positions = jnp.arange(seq)
    causal = positions[:, None] >= positions[None, :]
    p_float = jax.nn.softmax(jnp.where(causal, scores, MASK_FILL), axis=-1)
    p_bf16 = p_float.astype(jnp.bfloat16)
    o_act = mixed("kgst,tke->skge", p_bf16, v_act).astype(jnp.bfloat16)
    return normed, q_act, k_act, v_act, p_float, p_bf16, o_act.reshape(seq, q_width)


def attn_forward(x_loc, halves, dims):
    o_act = attn_inner(x_loc, halves, *dims)[6]
    proj = mixed("sw,dw->sd", o_act, halves[1][:, dims[0] * dims[2]:])
    return (x_loc.astype(jnp.float32) + proj).astype(jnp.bfloat16)


def attn_backward(x_loc, halves, dims, grad_y):
    kv_heads, heads, head_dim = dims
    seq = x_loc.shape[0]
    q_width, kv_width = heads * head_dim, kv_heads * head_dim
    normed, q_act, k_act, v_act, p_float, p_bf16, o_act = attn_inner(x_loc, halves, *dims)
    d_o_w = mixed("sd,sw->dw", grad_y, o_act)
    d_o = mixed("sd,dw->sw", grad_y, halves[1][:, kv_width:]).astype(jnp.bfloat16)
    d_o = d_o.reshape(seq, kv_heads, heads // kv_heads, head_dim)
    d_p = mixed("skge,tke->kgst", d_o, v_act)
    d_v = mixed("kgst,skge->tke", p_bf16, d_o).astype(jnp.bfloat16)
    d_s = p_float * (d_p - jnp.sum(p_float * d_p, axis=-1, keepdims=True))
    ds_bf16 = (d_s * (head_dim ** -0.5)).astype(jnp.bfloat16)
    d_q = mixed("kgst,tke->skge", ds_bf16, k_act).astype(jnp.bfloat16)
    d_k = mixed("kgst,skge->tke", ds_bf16, q_act).astype(jnp.bfloat16)
    d_qk = jnp.concatenate([d_q.reshape(seq, q_width), d_k.reshape(seq, kv_width)], axis=1)
    d_v = d_v.reshape(seq, kv_width)
    d_qk_w = mixed("sd,sw->dw", normed, d_qk)
    d_v_w = mixed("sd,sw->dw", normed, d_v)
    d_norm = mixed("sw,dw->sd", d_qk, halves[0]) + mixed("sw,dw->sd", d_v, halves[1][:, :kv_width])
    grad_x = (grad_y.astype(jnp.float32) + norm_back(x_loc, d_norm)).astype(jnp.bfloat16)
    grads = jnp.stack([d_qk_w.astype(jnp.bfloat16),
                       jnp.concatenate([d_v_w.astype(jnp.bfloat16), d_o_w.astype(jnp.bfloat16)], axis=1)])
    return grad_x, grads


def mlp_hidden(normed, up_halves):
    return jnp.concatenate([mixed("sd,df->sf", normed, up_halves[0]),
                            mixed("sd,df->sf", normed, up_halves[1])], axis=1)


def core_scatter(grad_halves):
    return lax.psum_scatter(grad_halves, "c", scatter_dimension=0, tiled=True)[0]


def solution(mesh):
    mesh4 = Mesh(mesh.devices.reshape(4, 4, 4, 2), ALL_AXES)
    row_spec = P(ALL_AXES)
    weight_spec = P(None, ALL_AXES)

    def body(x_in, w_q, w_k, w_v, w_o, w_up, w_down, grad_out):
        pairs, rows, heads, head_dim = w_q.shape
        kv_heads = w_k.shape[2]
        dims = (kv_heads, heads, head_dim)
        q_width, kv_width = heads * head_dim, kv_heads * head_dim
        half_w = q_width + kv_width
        ff_rows = w_down.shape[1]
        ff = w_up.shape[2]
        blocks = ff // ff_rows
        half_f = blocks * BLOCK // 2
        core = lax.axis_index("c")
        x_loc, g_loc = x_in[0], grad_out[0]

        attn_sh = jnp.concatenate([w_q.reshape(pairs, rows, q_width), w_k.reshape(pairs, rows, kv_width),
                                   w_v.reshape(pairs, rows, kv_width), w_o.reshape(pairs, rows, q_width)], axis=2)
        up_sh = jnp.pad(w_up.reshape(pairs, rows, blocks, ff_rows),
                        ((0, 0), (0, 0), (0, 0), (0, BLOCK - ff_rows))).reshape(pairs, rows, 2 * half_f)
        both = jnp.concatenate([attn_sh[:, :, :half_w], up_sh[:, :, :half_f],
                                attn_sh[:, :, half_w:], up_sh[:, :, half_f:]], axis=2)
        both = lax.all_gather(both, "c", axis=1, tiled=True)
        mine = lax.dynamic_slice_in_dim(both, core * (half_w + half_f), half_w + half_f, axis=2)
        attn_half, up_half = mine[:, :, :half_w], mine[:, :, half_w:]
        down_sh = jnp.pad(w_down, ((0, 0), (0, BLOCK - ff_rows), (0, 0)))

        def gather_halves(part):
            chip = lax.all_gather(part, CHIP_AXES, axis=0, tiled=True)
            return lax.all_gather(chip[None], "c", axis=0, tiled=True)

        def gather_down(part):
            return lax.all_gather(part, ALL_AXES, axis=0, tiled=True)

        def after(value, *deps):
            return lax.optimization_barrier((value,) + deps)[0]

        carry = x_loc
        inputs = []
        kept = []
        up_gate, down_gate = None, None
        for layer in range(pairs):
            attn_w = gather_halves(attn_half[layer])
            up_part = up_half[layer] if up_gate is None else after(up_half[layer], up_gate)
            up_w = gather_halves(up_part)
            down_part = after(down_sh[layer], up_w) if down_gate is None else after(down_sh[layer], up_w, down_gate)
            down_w = gather_down(down_part)
            inputs.append(carry)
            carry = attn_forward(carry, attn_w, dims)
            inputs.append(carry)
            normed = norm_bf16(carry)
            gelu_act = jax.nn.gelu(mlp_hidden(normed, up_w)).astype(jnp.bfloat16)
            up_gate = gelu_act
            proj = mixed("sf,fd->sd", gelu_act, down_w)
            carry = (carry.astype(jnp.float32) + proj).astype(jnp.bfloat16)
            down_gate = carry
            kept.append((attn_w, up_w, down_w))
        y_loc = carry

        grad_x = g_loc
        attn_out, up_out, down_out = [], [], []
        gate = None
        for layer in reversed(range(pairs)):
            if layer == pairs - 1:
                attn_w, up_w, down_w = kept[layer]
            else:
                down_w = gather_down(after(down_sh[layer], gate))
                up_w = gather_halves(after(up_half[layer], gate))
                attn_w = gather_halves(after(attn_half[layer], gate))
            mlp_x = inputs[2 * layer + 1]
            normed = norm_bf16(mlp_x)
            gelu_f32, gelu_pull = jax.vjp(jax.nn.gelu, mlp_hidden(normed, up_w))
            gelu_act = gelu_f32.astype(jnp.bfloat16)
            d_down = mixed("sf,sd->fd", gelu_act, grad_x).astype(jnp.bfloat16)
            d_hid = gelu_pull(mixed("sd,fd->sf", grad_x, down_w))[0].astype(jnp.bfloat16)
            d_up = jnp.stack([mixed("sd,sf->df", normed, d_hid[:, :half_f]).astype(jnp.bfloat16),
                              mixed("sd,sf->df", normed, d_hid[:, half_f:]).astype(jnp.bfloat16)])
            d_norm = mixed("sf,df->sd", d_hid[:, :half_f], up_w[0]) + mixed("sf,df->sd", d_hid[:, half_f:], up_w[1])
            grad_x = (grad_x.astype(jnp.float32) + norm_back(mlp_x, d_norm)).astype(jnp.bfloat16)
            gate = grad_x
            down_out.append(lax.psum_scatter(d_down, ALL_AXES, scatter_dimension=0, tiled=True))
            up_out.append(lax.psum_scatter(core_scatter(d_up), CHIP_AXES, scatter_dimension=0, tiled=True))
            grad_x, d_attn = attn_backward(inputs[2 * layer], attn_w, dims, grad_x)
            attn_out.append(lax.psum_scatter(core_scatter(d_attn), CHIP_AXES, scatter_dimension=0, tiled=True))

        down_grad = jnp.stack(down_out[::-1])[:, :ff_rows].astype(jnp.float32)
        merged = jnp.concatenate([jnp.stack(attn_out[::-1]), jnp.stack(up_out[::-1])], axis=2)
        merged = lax.all_gather(merged[:, :, None], "c", axis=2, tiled=True)
        merged = lax.dynamic_slice_in_dim(merged, core * rows, rows, axis=1).astype(jnp.float32)
        attn_grad = jnp.concatenate([merged[:, :, 0, :half_w], merged[:, :, 1, :half_w]], axis=2)
        up_grad = jnp.concatenate([merged[:, :, 0, half_w:], merged[:, :, 1, half_w:]], axis=2)
        up_grad = up_grad.reshape(pairs, rows, blocks, BLOCK)[:, :, :, :ff_rows].reshape(pairs, rows, ff)
        splits = [q_width, q_width + kv_width, q_width + 2 * kv_width]
        d_q, d_k, d_v, d_o = jnp.split(attn_grad, splits, axis=2)
        return (y_loc[None], grad_x[None],
                d_q.reshape(w_q.shape), d_k.reshape(w_k.shape), d_v.reshape(w_v.shape), d_o.reshape(w_o.shape),
                up_grad, down_grad)

    return jax.shard_map(body, mesh=mesh4, in_specs=(row_spec,) + (weight_spec,) * 6 + (row_spec,),
                         out_specs=(row_spec, row_spec) + (weight_spec,) * 6, check_vma=False)
```

time: 3830 us -> 2760 us (0.72)
  blocking collectives: 1100 us -> 0 us
  local copies, waits for them, and re-layouts: 150 us -> 58.5 us
  waiting for transfers between devices: 2210 us -> 2300 us
  other arithmetic: 16.2 us -> 60.7 us
    reduce_scatter x0 -> x10, waiting for transfers between devices: none -> 1420 us  [the longest x2 517 us: body(): lax.psum_scatter(d_down, ALL_AXES, scatter_dimension=0, tiled=True)]
    unnamed x32 -> x27, waiting for transfers between devices: 927 us -> 2.88 us
    unnamed x2 -> x0, blocking collectives: 821 us -> none
    all_gather x20 -> x17, waiting for transfers between devices: 1280 us -> 871 us  [the longest x6 485 us: gather_halves(): chip = lax.all_gather(part, CHIP_AXES, axis=0, tiled=True)]
    all_gather x8 -> x0, blocking collectives: 283 us -> none  [gather_all(): return lax.all_gather(shard, AXES, axis=0, tiled=True)]
    all_gather x16 -> x1, local copies, waits for them, and re-layouts: 67 us -> 1.57 us  [body(): merged = lax.all_gather(merged[:, :, None], 'c', axis=2, tiled=True)]
    another operation x8 -> x6, other arithmetic: 3.13 us -> 49.2 us  [the longest x2 38.9 us: body(): jnp.stack([mixed('sd,sf->df', normed, d_hid[:, :half_f]).astype(jnp.bfloa...]
    dot_general x54 -> x51, matrix products: 307 us -> 308 us  [mixed(): return jnp.einsum(form, left, right, preferred_element_type=jnp.float32)]
  transfers between devices with their start and end apart: 30 -> 27, of which waited for: 17 -> 22; matrix products, arithmetic and copies ran while one was open for 31% -> 13% of each run, Pallas kernels for 0% -> 0%
where the time goes in v1:
time: 2760 us; the launch traced here: 2750 us
  waiting for transfers between devices  2300 us (83%)
  matrix products  316 us (11%)
  other arithmetic  60.7 us (2%)
  local copies, waits for them, and re-layouts  58.5 us (2%)
    reduce_scatter x2, waiting for transfers between devices, body(): lax.psum_scatter(d_down, ALL_AXES, scatter_dimension=0, tiled=True)  517 us
    all_gather x6, waiting for transfers between devices, gather_halves(): chip = lax.all_gather(part, CHIP_AXES, axis=0, tiled=True)  485 us
    reduce_scatter x2, waiting for transfers between devices, body(): lax.psum_scatter(core_scatter(d_up), CHIP_AXES, scatter_dimension=0, tile...  475 us
    reduce_scatter x2, waiting for transfers between devices, body(): lax.psum_scatter(core_scatter(d_attn), CHIP_AXES, scatter_dimension=0, ti...  400 us
    dot_general x51, matrix products, mixed(): return jnp.einsum(form, left, right, preferred_element_type=jnp.float32)  308 us
    all_gather x3, waiting for transfers between devices, gather_down(): return lax.all_gather(part, ALL_AXES, axis=0, tiled=True)  258 us
    all_gather x6, waiting for transfers between devices, gather_halves(): return lax.all_gather(chip[None], 'c', axis=0, tiled=True)  101 us
  transfers between devices with their start and end apart: 27, of which 22 were waited for; matrix products, arithmetic and copies ran while one was open for 13% of the time, Pallas kernels for 0%

profile of v1, /device:TPU:1, one launch (start us, length us, event | category | flops | bytes accessed | tf_op | source)
XLA Modules:
  0.0 2750.6 jit_solution(8757714711632903702)
XLA Ops:
  16.0 15.6 all-gather.28.cloned.1.call-done
  36.7 67.8 %all-gather.42.cloned.1.call-done = bf16[1,1536,1792]{2,1,0:T(8,128)(2,1)} async-done(((bf16[1,24,1792]{2,1,0:T(8,128)(2,1)}), bf16[1,1536,1792]{2,1,0:T(8,128)(2,1)}) %all-gather.42.cloned.1.call-update) | async-done | bytes 5505040 | tf_op jit(solution)/shard_map/all_gather | solution.py:118
  104.6 98.5 %all-gather.46.cloned.1.call-done = bf16[1,1536,4608]{2,1,0:T(8,128)(2,1)} async-done(((bf16[1,24,4608]{2,1,0:T(8,128)(2,1)}), bf16[1,1536,4608]{2,1,0:T(8,128)(2,1)}) %all-gather.46.cloned.1.call-update) | async-done | bytes 14155792 | tf_op jit(solution)/shard_map/all_gather | solution.py:118
  205.2 26.5 all-gather.44.cloned.1.call-done
  252.8 30.2 %all-gather.48.cloned.1.call-done = bf16[2,1536,4608]{2,1,0:T(8,128)(2,1)} async-done(((bf16[1,1536,4608]{2,1,0:T(8,128)(2,1)}), bf16[2,1536,4608]{2,1,0:T(8,128)(2,1)}) %all-gather.48.cloned.1.call-update) | async-done | bytes 28311568 | tf_op jit(solution)/shard_map/all_gather | solution.py:119
  283.0 6.6 fusion.9
  289.6 6.6 fusion.10
  300.8 54.9 %all-gather.50.cloned.1.call-done = bf16[1,1536,1792]{2,1,0:T(8,128)(2,1)} async-done(((bf16[1,24,1792]{2,1,0:T(8,128)(2,1)}), bf16[1,1536,1792]{2,1,0:T(8,128)(2,1)}) %all-gather.50.cloned.1.call-update) | async-done | bytes 5505040 | tf_op jit(solution)/shard_map/all_gather | solution.py:118
  355.8 98.5 %all-gather.32.cloned.1.call-done = bf16[1536,4608]{1,0:T(8,128)(2,1)} async-done(((bf16[24,4608]{1,0:T(8,128)(2,1)}), bf16[1536,4608]{1,0:T(8,128)(2,1)}) %all-gather.32.cloned.1.call-update) | async-done | bytes 14155792 | tf_op jit(solution)/shard_map/all_gather | solution.py:118
  454.9 100.4 %all-gather.30.cloned.1.call-done = bf16[9216,1536]{1,0:T(8,128)(2,1)} async-done(((bf16[72,1536]{1,0:T(8,128)(2,1)}), bf16[9216,1536]{1,0:T(8,128)(2,1)}) %all-gather.30.cloned.1.call-update) | async-done | bytes 28311568 | tf_op jit(solution)/shard_map/all_gather | solution.py:122
  555.3 13.3 fusion.146
  569.3 13.9 all-gather.52.cloned.1.call-done
  603.7 30.8 %all-gather.54.cloned.1.call-done = bf16[3072,4608]{1,0:T(8,128)(2,1)} async-done(((bf16[1536,4608]{1,0:T(8,128)(2,1)}), bf16[3072,4608]{1,0:T(8,128)(2,1)}) %all-gather.54.cloned.1.call-update) | async-done | bytes 28311568 | tf_op jit(solution)/shard_map/all_gather | solution.py:119
  634.5 9.7 fusion.19
  644.2 9.8 fusion.23
  653.9 83.3 %all-gather.34.cloned.1.call-done = bf16[9216,1536]{1,0:T(8,128)(2,1)} async-done(((bf16[72,1536]{1,0:T(8,128)(2,1)}), bf16[9216,1536]{1,0:T(8,128)(2,1)}) %all-gather.34.cloned.1.call-update) | async-done | bytes 28311568 | tf_op jit(solution)/shard_map/all_gather | solution.py:122
  737.2 19.5 fusion.33
  756.7 11.5 fusion.21
  768.2 11.1 multiply_reduce_fusion.1
  782.0 66.9 %all-gather.40.cloned.1.call-done = bf16[1536,1792]{1,0:T(8,128)(2,1)} async-done(((bf16[24,1792]{1,0:T(8,128)(2,1)}), bf16[1536,1792]{1,0:T(8,128)(2,1)}) %all-gather.40.cloned.1.call-update) | async-done | bytes 5505040 | tf_op jit(solution)/shard_map/all_gather | solution.py:118
  848.9 98.5 %all-gather.38.cloned.1.call-done = bf16[1536,4608]{1,0:T(8,128)(2,1)} async-done(((bf16[24,4608]{1,0:T(8,128)(2,1)}), bf16[1536,4608]{1,0:T(8,128)(2,1)}) %all-gather.38.cloned.1.call-update) | async-done | bytes 14155792 | tf_op jit(solution)/shard_map/all_gather | solution.py:118
  954.3 5.6 fusion.131
  962.9 5.0 fusion.169
  979.4 8.8 fusion.8
  988.2 7.1 fusion.7
  995.3 19.5 pad_maximum_fusion.1
  1035.6 9.7 fusion.11
  1045.3 9.8 fusion.15
  1055.1 74.2 %all-gather.36.cloned.1.call-done = bf16[9216,1536]{1,0:T(8,128)(2,1)} async-done(((bf16[72,1536]{1,0:T(8,128)(2,1)}), bf16[9216,1536]{1,0:T(8,128)(2,1)}) %all-gather.36.cloned.1.call-update) | async-done | bytes 28311568 | tf_op jit(solution)/shard_map/all_gather | solution.py:122
  1129.3 18.5 fusion.40
  1147.8 8.4 fusion.13
  1156.3 8.5 multiply_reduce_fusion
  1171.2 5.6 fusion.132
  1179.8 5.0 fusion.168
  1196.2 9.0 fusion.6
  1205.2 7.1 fusion.5
  1212.3 19.5 pad_maximum_fusion
  1234.0 31.6 %reduce-scatter.19.cloned.1.call-done = bf16[1,1536,4608]{2,1,0:T(8,128)(2,1)} async-done(((bf16[2,1536,4608]{2,1,0:T(8,128)(2,1)}), bf16[1,1536,4608]{2,1,0:T(8,128)(2,1)}) %reduce-scatter.19.cloned.1.call-update) | async-done | bytes 14155792 | tf_op jit(solution)/shard_map/reduce_scatter | solution.py:85
  1266.7 16.1 convolution_convert_fusion
  1283.8 16.1 convolution_convert_fusion.1
  1301.2 18.0 fusion.107
  1323.9 171.5 %reduce-scatter.17.cloned.1.call-done = bf16[24,1792]{1,0:T(8,128)(2,1)} async-done(((bf16[1536,1792]{1,0:T(8,128)(2,1)}), bf16[24,1792]{1,0:T(8,128)(2,1)}) %reduce-scatter.17.cloned.1.call-update) | async-done | bytes 86032 | tf_op jit(solution)/shard_map/reduce_scatter | solution.py:173
  1495.4 237.6 %reduce-scatter.25.cloned.1.call-done = bf16[24,4608]{1,0:T(8,128)(2,1)} async-done(((bf16[1536,4608]{1,0:T(8,128)(2,1)}), bf16[24,4608]{1,0:T(8,128)(2,1)}) %reduce-scatter.25.cloned.1.call-update) | async-done | bytes 221200 | tf_op jit(solution)/shard_map/reduce_scatter | solution.py:171
  1732.9 228.3 %reduce-scatter.13.cloned.1.call-done = bf16[24,1792]{1,0:T(8,128)(2,1)} async-done(((bf16[1536,1792]{1,0:T(8,128)(2,1)}), bf16[24,1792]{1,0:T(8,128)(2,1)}) %reduce-scatter.13.cloned.1.call-update) | async-done | bytes 86032 | tf_op jit(solution)/shard_map/reduce_scatter | solution.py:173
  1961.2 237.3 %reduce-scatter.21.cloned.1.call-done = bf16[24,4608]{1,0:T(8,128)(2,1)} async-done(((bf16[1536,4608]{1,0:T(8,128)(2,1)}), bf16[24,4608]{1,0:T(8,128)(2,1)}) %reduce-scatter.21.cloned.1.call-update) | async-done | bytes 221200 | tf_op jit(solution)/shard_map/reduce_scatter | solution.py:171
  2203.4 255.9 %reduce-scatter.29.cloned.1.call-done = bf16[72,1536]{1,0:T(8,128)(2,1)} async-done(((bf16[9216,1536]{1,0:T(8,128)(2,1)}), bf16[72,1536]{1,0:T(8,128)(2,1)}) %reduce-scatter.29.cloned.1.call-update) | async-done | bytes 221200 | tf_op jit(solution)/shard_map/reduce_scatter | solution.py:170
  2459.3 260.7 %reduce-scatter.27.cloned.1.call-done = bf16[72,1536]{1,0:T(8,128)(2,1)} async-done(((bf16[9216,1536]{1,0:T(8,128)(2,1)}), bf16[72,1536]{1,0:T(8,128)(2,1)}) %reduce-scatter.27.cloned.1.call-update) | async-done | bytes 221200 | tf_op jit(solution)/shard_map/reduce_scatter | solution.py:170
  2722.7 11.2 all-gather.60.cloned.1.call-done
  (283 shorter events, 155.5 us)
Async XLA Ops:
  7.2 7.4 copy-start.36
  7.2 7.7 copy-start.33
  7.2 24.5 all-gather.28.cloned.1.call-start
  16.0 88.5 %all-gather.42.cloned.1.call-start = ((), (), s32[]{:S(2)}) async-start(), calls=%async_computation.27 | async-start | bytes 5591040 | tf_op jit(solution)/shard_map/all_gather | solution.py:118
  33.7 169.4 %all-gather.46.cloned.1.call-start = ((), (), s32[]{:S(2)}) async-start(), calls=%async_computation.29 | async-start | bytes 14376960 | tf_op jit(solution)/shard_map/all_gather | solution.py:118
  36.7 195.1 %all-gather.44.cloned.1.call-start = ((), (), s32[]{:S(2)}) async-start(), calls=%async_computation.28 | async-start | bytes 16515072 | tf_op jit(solution)/shard_map/all_gather | solution.py:119
  104.5 178.5 %all-gather.48.cloned.1.call-start = ((), (), s32[]{:S(2)}) async-start(), calls=%async_computation.30 | async-start | bytes 42467328 | tf_op jit(solution)/shard_map/all_gather | solution.py:119
  203.1 152.6 %all-gather.50.cloned.1.call-start = ((), (), s32[]{:S(2)}) async-start(), calls=%async_computation.31 | async-start | bytes 5591040 | tf_op jit(solution)/shard_map/all_gather | solution.py:118
  203.8 250.4 %all-gather.32.cloned.1.call-start = ((), (), s32[]{:S(2)}) async-start(), calls=%async_computation.12 | async-start | bytes 14376960 | tf_op jit(solution)/shard_map/all_gather | solution.py:118
  204.2 389.3 %copy-start.34 = (pred[192,192]{0,1:T(8,128)(4,1)}, pred[192,192]{0,1:T(8,128)(4,1)S(1)}, u32[]{:S(2)}) copy-start(pred[192,192]{0,1:T(8,128)(4,1)S(1)} %iota_compare_fusion) | copy-start | bytes 110596
  204.4 27.3 copy-start.39
  204.4 34.8 %copy-start.41 = (f32[192]{0:T(256)}, f32[192]{0:T(256)S(1)}, u32[]{:S(2)}) copy-start(f32[192]{0:T(256)S(1)} %fusion.251) | copy-start | bytes 2308
  252.1 303.2 %copy-start.8 = (f32[192,1536]{1,0:T(8,128)}, f32[192,1536]{1,0:T(8,128)S(1)}, u32[]{:S(2)}) copy-start(f32[192,1536]{1,0:T(8,128)S(1)} %get-tuple-element.65) | copy-start | bytes 3538948
  252.6 37.0 %copy-start.37 = (f32[192]{0:T(256)}, f32[192]{0:T(256)S(1)}, u32[]{:S(2)}) copy-start(f32[192]{0:T(256)S(1)} %fusion.252) | copy-start | bytes 2308
  252.8 36.8 %copy-start.1 = (bf16[192,1536]{1,0:T(8,128)(2,1)}, bf16[192,1536]{1,0:T(8,128)(2,1)S(1)}, u32[]{:S(2)}) copy-start(bf16[192,1536]{1,0:T(8,128)(2,1)S(1)} %multiply_convert_fusion.4) | copy-start | bytes 1769476
  299.8 255.5 %all-gather.30.cloned.1.call-start = ((), (), s32[]{:S(2)}) async-start(), calls=%async_computation.11 | async-start | bytes 28532736 | tf_op jit(solution)/shard_map/all_gather | solution.py:122
  300.8 282.5 %all-gather.52.cloned.1.call-start = ((), (), s32[]{:S(2)}) async-start(), calls=%async_computation.32 | async-start | bytes 16515072 | tf_op jit(solution)/shard_map/all_gather | solution.py:119
  355.7 278.8 %all-gather.54.cloned.1.call-start = ((), (), s32[]{:S(2)}) async-start(), calls=%async_computation.33 | async-start | bytes 42467328 | tf_op jit(solution)/shard_map/all_gather | solution.py:119
  454.3 282.9 %all-gather.34.cloned.1.call-start = ((), (), s32[]{:S(2)}) async-start(), calls=%async_computation.13 | async-start | bytes 28532736 | tf_op jit(solution)/shard_map/all_gather | solution.py:122
  568.6 23.8 copy-start.15
  568.6 280.2 %all-gather.40.cloned.1.call-start = ((), (), s32[]{:S(2)}) async-start(), calls=%async_computation.16 | async-start | bytes 5591040 | tf_op jit(solution)/shard_map/all_gather | solution.py:118
  583.2 7.7 copy-start.13
  603.5 175.8 %copy-start.6 = (f32[192,1536]{1,0:T(8,128)}, f32[192,1536]{1,0:T(8,128)S(1)}, u32[]{:S(2)}) copy-start(f32[192,1536]{1,0:T(8,128)S(1)} %get-tuple-element.71) | copy-start | bytes 3538948
  644.2 93.0 %copy-start.25 = (bf16[1,192,1536]{2,1,0:T(8,128)(2,1)S(1)}, bf16[1,192,1536]{2,1,0:T(8,128)(2,1)}, u32[]{:S(2)}) copy-start(bf16[1,192,1536]{2,1,0:T(8,128)(2,1)} %param.15) | copy-start | bytes 1769476
  756.7 11.5 copy-start.10
  781.1 166.3 %all-gather.38.cloned.1.call-start = ((), (), s32[]{:S(2)}) async-start(), calls=%async_computation.15 | async-start | bytes 14376960 | tf_op jit(solution)/shard_map/all_gather | solution.py:118
  781.9 240.6 %all-gather.58.cloned.1.call-start = ((), (), s32[]{:S(2)}) async-start(), calls=%async_computation.35 | async-start | bytes 16515072 | tf_op jit(solution)/shard_map/all_gather | solution.py:119
  848.9 186.7 %all-gather.56.cloned.1.call-start = ((), (), s32[]{:S(2)}) async-start(), calls=%async_computation.34 | async-start | bytes 42467328 | tf_op jit(solution)/shard_map/all_gather | solution.py:119
  947.5 181.8 %all-gather.36.cloned.1.call-start = ((), (), s32[]{:S(2)}) async-start(), calls=%async_computation.14 | async-start | bytes 28532736 | tf_op jit(solution)/shard_map/all_gather | solution.py:122
  948.0 283.8 %reduce-scatter.15.cloned.1.call-start = ((), (), s32[]{:S(2)}) async-start(), calls=%async_computation.19 | async-start | bytes 16515072 | tf_op jit(solution)/shard_map/reduce_scatter | solution.py:85
  979.3 253.2 %reduce-scatter.23.cloned.1.call-start = ((), (), s32[]{:S(2)}) async-start(), calls=%async_computation.23 | async-start | bytes 42467328 | tf_op jit(solution)/shard_map/reduce_scatter | solution.py:85
  979.4 8.8 copy-start.11
  1014.8 218.5 %reduce-scatter.11.cloned.1.call-start = ((), (), s32[]{:S(2)}) async-start(), calls=%async_computation.17 | async-start | bytes 16515072 | tf_op jit(solution)/shard_map/reduce_scatter | solution.py:85
  1022.5 142.4 %copy-start.18 = (bf16[192,1536]{1,0:T(8,128)(2,1)}, bf16[192,1536]{1,0:T(8,128)(2,1)S(1)}, u32[]{:S(2)}) copy-start(bf16[192,1536]{1,0:T(8,128)(2,1)S(1)} %fusion.141) | copy-start | bytes 1769476
  1147.8 8.4 copy-start.9
  1156.2 8.6 copy-start.44
  1156.3 8.6 copy-start.38
  1171.2 8.5 copy-start.47
  1196.1 69.5 %reduce-scatter.19.cloned.1.call-start = ((), (), s32[]{:S(2)}) async-start(), calls=%async_computation.21 | async-start | bytes 42467328 | tf_op jit(solution)/shard_map/reduce_scatter | solution.py:85
  1196.2 9.0 copy-start.12
  1231.8 263.6 %reduce-scatter.17.cloned.1.call-start = ((), (), s32[]{:S(2)}) async-start(), calls=%async_computation.20 | async-start | bytes 5591040 | tf_op jit(solution)/shard_map/reduce_scatter | solution.py:173
  1232.5 500.4 %reduce-scatter.25.cloned.1.call-start = ((), (), s32[]{:S(2)}) async-start(), calls=%async_computation.24 | async-start | bytes 14376960 | tf_op jit(solution)/shard_map/reduce_scatter | solution.py:171
  1233.3 728.0 %reduce-scatter.13.cloned.1.call-start = ((), (), s32[]{:S(2)}) async-start(), calls=%async_computation.18 | async-start | bytes 5591040 | tf_op jit(solution)/shard_map/reduce_scatter | solution.py:173
  1234.0 964.5 %reduce-scatter.21.cloned.1.call-start = ((), (), s32[]{:S(2)}) async-start(), calls=%async_computation.22 | async-start | bytes 14376960 | tf_op jit(solution)/shard_map/reduce_scatter | solution.py:171
  1265.7 1193.6 %reduce-scatter.29.cloned.1.call-start = ((), (), s32[]{:S(2)}) async-start(), calls=%async_computation.26 | async-start | bytes 28532736 | tf_op jit(solution)/shard_map/reduce_scatter | solution.py:170
  1282.8 1437.2 %reduce-scatter.27.cloned.1.call-start = ((), (), s32[]{:S(2)}) async-start(), calls=%async_computation.25 | async-start | bytes 28532736 | tf_op jit(solution)/shard_map/reduce_scatter | solution.py:170
  1299.9 1433.9 %all-gather.60.cloned.1.call-start = ((), (), s32[]{:S(2)}) async-start(), calls=%async_computation.36 | async-start | bytes 1843200 | tf_op jit(solution)/shard_map/all_gather | solution.py:177
  1323.9 878.3 %copy-start.40 = (f32[192]{0:T(256)S(1)}, f32[192]{0:T(256)}, u32[]{:S(2)}) copy-start(f32[192]{0:T(256)} %copy-done.39) | copy-start | bytes 2308
  (28 other events, 80.5 us)
Sparse Core Ops, SparseCore 0:
  16.1 15.5 all-gather.27
  35.0 69.4 all-gather.41
  107.8 95.2 all-gather.45
  204.6 27.0 all-gather.43
  233.2 49.7 all-gather.47
  286.2 69.4 all-gather.49
  359.0 95.2 all-gather.31
  457.3 97.9 all-gather.29
  557.0 26.2 all-gather.51
  584.7 49.7 all-gather.53
  638.1 99.0 all-gather.33
  781.2 67.5 all-gather.39
  852.2 95.2 all-gather.37
  948.9 27.0 all-gather.57
  977.6 49.7 all-gather.55
  1030.2 99.0 all-gather.35
  1131.5 19.7 reduce-scatter.14
  1153.6 35.6 reduce-scatter.22
  1196.3 19.7 reduce-scatter.10
  1231.9 33.6 reduce-scatter.18
  1270.1 225.2 reduce-scatter.16
  1500.1 232.8 reduce-scatter.24
  1737.4 223.7 reduce-scatter.12
  1965.8 232.6 reduce-scatter.20
  2204.0 255.2 reduce-scatter.28
  2464.6 255.3 reduce-scatter.26
  2722.0 11.7 all-gather.59

commit v2 on v1

v2 whole, which is shorter than its diff:
```python
import functools

import jax
import jax.numpy as jnp
from jax import lax
from jax.experimental import pallas as pl
from jax.experimental.pallas import tpu as pltpu
from jax.sharding import Mesh, PartitionSpec as P

MESH = pl.DeviceIdType.MESH
ALL_AXES = ("z", "y", "x", "c")
CORE_MAJOR = ("c", "z", "y", "x")
EPS = 1e-6
MASK_FILL = -1e30


DIMS = ("z", "y", "x")
ORDERS = (("x", "y", "z"), ("y", "z", "x"), ("z", "x", "y"))
COLS = 256
ROWS = 24
LAG = 2


def _block(color, stage, position):
    dims = tuple(dim for dim in DIMS if dim not in ORDERS[color][:stage])
    return tuple(position if dim == ORDERS[color][stage] else slice(None) for dim in dims)


def grad_kernel(segments, n_chunks, n_in, *refs):
    arrays, out_ref = refs[:n_in], refs[n_in]
    (lhs, rhs, outgo, peer, sum0, sum1, sum2, sa0, ra0, sb0, rb0, sa1, ra1, sb1, rb1, sa2, ra2, sb2, rb2,
     load_sem, pair_send, pair_recv, ring_send, ring_recv, credit) = refs[n_in + 1:]
    sums = (sum0, sum1, sum2)
    half_bufs = ((sa0, ra0), (sa1, ra1), (sa2, ra2))
    full_bufs = ((sb0, rb0), (sb1, rb1), (sb2, rb2))
    core = lax.axis_index("c")
    place = {dim: lax.axis_index(dim) for dim in DIMS}
    nxt = {dim: lax.rem(place[dim] + 1, 4) for dim in DIMS}
    prv = {dim: lax.rem(place[dim] + 3, 4) for dim in DIMS}
    opp = {dim: lax.rem(place[dim] + 2, 4) for dim in DIMS}
    sibling = {"c": 1 - core}
    partners = [({dim: (nxt, prv)[way][dim]}, 2 * d + 1 - way, 2 * d + way)
                for d, dim in enumerate(DIMS) for way in range(2)]
    partners.append((sibling, 6, 6))

    barrier = pltpu.get_barrier_semaphore()
    for device, _, _ in partners:
        pl.semaphore_signal(barrier, inc=1, device_id=device, device_id_type=MESH)
    pl.semaphore_wait(barrier, len(partners))

    depth = 1 + 8 * LAG
    n_ticks = n_chunks + depth

    def load(lhs_ref, rhs_ref, slot, role):
        return (pltpu.make_async_copy(lhs_ref, lhs.at[slot, role], load_sem.at[slot, role, 0]),
                pltpu.make_async_copy(rhs_ref, rhs.at[slot, role], load_sem.at[slot, role, 1]))

    def fetch(chunk):
        slot = lax.rem(chunk, 4)
        for half in range(2):
            role = jnp.where(core == half, 0, 1)
            first = 0
            for count, lhs_name, lhs_start, rhs_name, rhs_start in segments[half]:
                @pl.when((chunk >= first) & (chunk < first + count))
                def _(first=first, lhs_name=lhs_name, lhs_start=lhs_start, rhs_name=rhs_name, rhs_start=rhs_start):
                    start = pl.multiple_of(rhs_start + (chunk - first) * COLS, COLS)
                    width = lhs.shape[-1]
                    for copy in load(arrays[lhs_name].at[:, lhs_start:lhs_start + width],
                                     arrays[rhs_name].at[:, pl.ds(start, COLS)], slot, role):
                        copy.start()
                first += count

    def pair_copy(slot):
        return pltpu.make_async_remote_copy(
            src_ref=outgo.at[slot], dst_ref=peer.at[slot], send_sem=pair_send.at[slot],
            recv_sem=pair_recv.at[slot], device_id=sibling, device_id_type=MESH)

    def multiply(chunk):
        slot = lax.rem(chunk, 4)
        for role in range(2):
            for copy in load(lhs.at[slot, role], rhs.at[slot, role], slot, role):
                copy.wait()
        quarter = lhs.shape[-1] // 4
        for role in (1, 0):
            for z in range(4):
                part = lax.dot_general(lhs[slot, role, :, quarter * z:quarter * z + quarter], rhs[slot, role],
                                       (((0,), (0,)), ((), ())), preferred_element_type=jnp.float32)
                if role == 0:
                    sum0[lax.rem(chunk, 8), z] = part.reshape(4, 4, ROWS, COLS)
                else:
                    outgo[slot, z] = part.astype(jnp.bfloat16).reshape(4, 4, ROWS, COLS)
        pair_copy(slot).start()

    def merge_pair(chunk):
        slot, lead = lax.rem(chunk, 4), lax.rem(chunk, 8)
        pair_copy(slot).wait_send()
        pair_copy(slot).wait_recv()
        for z in range(4):
            for y in range(4):
                sum0[lead, z, y] = sum0[lead, z, y] + peer[slot, z, y].astype(jnp.float32)

    def ring_copy(stage, part, slot, color, way):
        send, recv = (half_bufs, full_bufs)[part][stage]
        dim = ORDERS[color][stage]
        return pltpu.make_async_remote_copy(
            src_ref=send.at[slot, color, way], dst_ref=recv.at[slot, color, way],
            send_sem=ring_send.at[2 * stage + part, slot], recv_sem=ring_recv.at[2 * stage + part, slot],
            device_id={dim: (nxt, prv)[way][dim]}, device_id_type=MESH)

    def ring_wait(stage, part, slot):
        send, recv = (half_bufs, full_bufs)[part][stage]
        whole = pltpu.make_async_remote_copy(
            src_ref=send.at[slot], dst_ref=recv.at[slot],
            send_sem=ring_send.at[2 * stage + part, slot], recv_sem=ring_recv.at[2 * stage + part, slot],
            device_id=sibling, device_id_type=MESH)
        whole.wait_send()
        whole.wait_recv()

    def source(stage, chunk, color, position, cols):
        lead = lax.rem(chunk, 8)
        if stage == 0:
            return sum0[(lead,) + _block(color, 0, position) + (slice(8 * color, 8 * color + 8), cols)]
        return sums[stage][(lead, color) + _block(color, stage, position) + (slice(None), cols)]

    left, right, every = slice(0, COLS // 2), slice(COLS // 2, COLS), slice(0, COLS)

    def store_halves(stage, chunk):
        slot = lax.rem(chunk, 4)
        send = half_bufs[stage][0]
        for color in range(3):
            far = opp[ORDERS[color][stage]]
            send[slot, color, 0] = source(stage, chunk, color, far, left).astype(jnp.bfloat16)
            send[slot, color, 1] = source(stage, chunk, color, far, right).astype(jnp.bfloat16)

    def store_fulls(stage, chunk):
        slot = lax.rem(chunk, 4)
        ring_wait(stage, 0, slot)
        recv = half_bufs[stage][1]
        send = full_bufs[stage][0]
        lead = (slice(None),) * (len(send.shape) - 4)
        for color in range(3):
            dim = ORDERS[color][stage]
            for way, near, summed, plain in ((0, nxt, left, right), (1, prv, right, left)):
                send[(slot, color, way) + lead + (summed,)] = (
                    source(stage, chunk, color, near[dim], summed)
                    + recv[slot, color, way].astype(jnp.float32)).astype(jnp.bfloat16)
                send[(slot, color, way) + lead + (plain,)] = source(
                    stage, chunk, color, near[dim], plain).astype(jnp.bfloat16)

    def close_stage(stage, chunk):
        slot = lax.rem(chunk, 4)
        ring_wait(stage, 1, slot)
        recv = full_bufs[stage][1]
        for color in range(3):
            dim = ORDERS[color][stage]
            total = (source(stage, chunk, color, place[dim], every)
                     + recv[slot, color, 0].astype(jnp.float32)
                     + recv[slot, color, 1].astype(jnp.float32))
            if stage < 2:
                sums[stage + 1][lax.rem(chunk, 8), color] = total
            else:
                out_ref[chunk, 8 * color:8 * color + 8, :] = total

    def send_all(stage, part, chunk):
        slot = lax.rem(chunk, 4)
        for color in range(3):
            for way in range(2):
                ring_copy(stage, part, slot, color, way).start()

    def open_first(chunk):
        merge_pair(chunk)
        store_halves(0, chunk)
        send_all(0, 0, chunk)

    def middle(stage, chunk):
        store_fulls(stage, chunk)
        send_all(stage, 1, chunk)

    def turn(stage, chunk):
        close_stage(stage, chunk)
        if stage < 2:
            store_halves(stage + 1, chunk)
            send_all(stage + 1, 0, chunk)

    steps = [(0, fetch), (1 + 2 * LAG, functools.partial(middle, 0)), (1 + LAG, open_first),
             (1 + 3 * LAG, functools.partial(turn, 0)), (1 + 4 * LAG, functools.partial(middle, 1)),
             (1 + 5 * LAG, functools.partial(turn, 1)), (1 + 6 * LAG, functools.partial(middle, 2)),
             (1 + 7 * LAG, functools.partial(turn, 2)), (1, multiply)]

    def tick(now, carry):
        @pl.when(now >= 2)
        def _():
            for _, _, mine in partners:
                pl.semaphore_wait(credit.at[mine], 1)

        for lag, step in steps:
            @pl.when((now >= lag) & (now < lag + n_chunks))
            def _(lag=lag, step=step):
                step(now - lag)

        @pl.when(now < n_ticks - 2)
        def _():
            for device, theirs, _ in partners:
                pl.semaphore_signal(credit.at[theirs], inc=1, device_id=device, device_id_type=MESH)
        return carry

    lax.fori_loop(0, n_ticks, tick, 0)


def grad_scatter(arrays, segments):
    n_chunks = sum(segment[0] for segment in segments[0])
    seq = arrays[0].shape[0]
    width = 64 * ROWS
    bf16, f32 = jnp.bfloat16, jnp.float32
    half = COLS // 2
    scratch = [pltpu.VMEM((4, 2, seq, width), bf16), pltpu.VMEM((4, 2, seq, COLS), bf16),
               pltpu.VMEM((4, 4, 4, 4, ROWS, COLS), bf16), pltpu.VMEM((4, 4, 4, 4, ROWS, COLS), bf16),
               pltpu.VMEM((8, 4, 4, 4, ROWS, COLS), f32), pltpu.VMEM((8, 3, 4, 4, 8, COLS), f32),
               pltpu.VMEM((8, 3, 4, 8, COLS), f32)]
    for size in ((4, 4), (4,), ()):
        scratch += [pltpu.VMEM((4, 3, 2) + size + (8, half), bf16)] * 2
        scratch += [pltpu.VMEM((4, 3, 2) + size + (8, COLS), bf16)] * 2
    scratch += [pltpu.SemaphoreType.DMA((4, 2, 2)), pltpu.SemaphoreType.DMA((4,)), pltpu.SemaphoreType.DMA((4,)),
                pltpu.SemaphoreType.DMA((6, 4)), pltpu.SemaphoreType.DMA((6, 4)), pltpu.SemaphoreType.REGULAR((7,))]
    return pl.pallas_call(
        functools.partial(grad_kernel, segments, n_chunks, len(arrays)),
        name="grad_scatter",
        out_shape=jax.ShapeDtypeStruct((n_chunks, ROWS, COLS), f32),
        in_specs=[pl.BlockSpec(memory_space=pl.ANY)] * len(arrays),
        out_specs=pl.BlockSpec(memory_space=pltpu.VMEM),
        scratch_shapes=scratch,
        compiler_params=pltpu.CompilerParams(collective_id=0, has_side_effects=True,
                                             vmem_limit_bytes=60 * 1024 * 1024),
    )(*arrays)


def rms_norm(values):
    return values * lax.rsqrt(jnp.mean(values * values, axis=-1, keepdims=True) + EPS)


def norm_bf16(x_loc):
    return rms_norm(x_loc.astype(jnp.float32)).astype(jnp.bfloat16)


def norm_back(x_loc, grad_norm):
    _, pull_back = jax.vjp(rms_norm, x_loc.astype(jnp.float32))
    return pull_back(grad_norm)[0]


def mixed(form, left, right):
    return jnp.einsum(form, left, right, preferred_element_type=jnp.float32)


def attn_inner(x_loc, w_qk, w_v, kv_heads, heads, head_dim):
    seq = x_loc.shape[0]
    q_width = heads * head_dim
    normed = norm_bf16(x_loc)
    qk = mixed("sd,dw->sw", normed, w_qk).astype(jnp.bfloat16)
    v_act = mixed("sd,dw->sw", normed, w_v).astype(jnp.bfloat16)
    q_act = qk[:, :q_width].reshape(seq, kv_heads, heads // kv_heads, head_dim)
    k_act = qk[:, q_width:].reshape(seq, kv_heads, head_dim)
    v_act = v_act.reshape(seq, kv_heads, head_dim)
    scores = mixed("skge,tke->kgst", q_act, k_act) * (head_dim ** -0.5)
    positions = jnp.arange(seq)
    causal = positions[:, None] >= positions[None, :]
    p_float = jax.nn.softmax(jnp.where(causal, scores, MASK_FILL), axis=-1)
    p_bf16 = p_float.astype(jnp.bfloat16)
    o_act = mixed("kgst,tke->skge", p_bf16, v_act).astype(jnp.bfloat16)
    return normed, q_act, k_act, v_act, p_float, p_bf16, o_act.reshape(seq, q_width)


def attn_forward(x_loc, w_qk, w_v, w_o, dims):
    o_act = attn_inner(x_loc, w_qk, w_v, *dims)[6]
    proj = mixed("sw,dw->sd", o_act, w_o)
    return (x_loc.astype(jnp.float32) + proj).astype(jnp.bfloat16)


def attn_backward(x_loc, w_qk, w_v, w_o, dims, grad_y):
    kv_heads, heads, head_dim = dims
    seq = x_loc.shape[0]
    q_width, kv_width = heads * head_dim, kv_heads * head_dim
    normed, q_act, k_act, v_act, p_float, p_bf16, o_act = attn_inner(x_loc, w_qk, w_v, *dims)
    d_o = mixed("sd,dw->sw", grad_y, w_o).astype(jnp.bfloat16)
    d_o = d_o.reshape(seq, kv_heads, heads // kv_heads, head_dim)
    d_p = mixed("skge,tke->kgst", d_o, v_act)
    d_v = mixed("kgst,skge->tke", p_bf16, d_o).astype(jnp.bfloat16)
    d_s = p_float * (d_p - jnp.sum(p_float * d_p, axis=-1, keepdims=True))
    ds_bf16 = (d_s * (head_dim ** -0.5)).astype(jnp.bfloat16)
    d_q = mixed("kgst,tke->skge", ds_bf16, k_act).astype(jnp.bfloat16)
    d_k = mixed("kgst,skge->tke", ds_bf16, q_act).astype(jnp.bfloat16)
    d_qk = jnp.concatenate([d_q.reshape(seq, q_width), d_k.reshape(seq, kv_width)], axis=1)
    d_v = d_v.reshape(seq, kv_width)
    d_norm = mixed("sw,dw->sd", d_qk, w_qk) + mixed("sw,dw->sd", d_v, w_v)
    grad_x = (grad_y.astype(jnp.float32) + norm_back(x_loc, d_norm)).astype(jnp.bfloat16)
    return grad_x, [normed, d_qk, d_v, grad_y, o_act]


def solution(mesh):
    mesh4 = Mesh(mesh.devices.reshape(4, 4, 4, 2), ALL_AXES)
    row_spec = P(ALL_AXES)
    weight_spec = P(None, ALL_AXES)

    def body(x_in, w_q, w_k, w_v, w_o, w_up, w_down, grad_out):
        pairs, rows, heads, head_dim = w_q.shape
        kv_heads = w_k.shape[2]
        dims = (kv_heads, heads, head_dim)
        q_width, kv_width = heads * head_dim, kv_heads * head_dim
        half_w = q_width + kv_width
        ff_rows = w_down.shape[1]
        ff, width = w_up.shape[2], w_down.shape[2]
        chips = ff // ff_rows // 2
        ff_pad = 3 * ROWS
        half_f = chips * ff_pad
        core = lax.axis_index("c")
        x_loc, g_loc = x_in[0], grad_out[0]

        attn_sh = jnp.concatenate([w_q.reshape(pairs, rows, q_width), w_k.reshape(pairs, rows, kv_width),
                                   w_v.reshape(pairs, rows, kv_width), w_o.reshape(pairs, rows, q_width)], axis=2)
        up_sh = jnp.pad(w_up.reshape(pairs, rows, chips, 2, ff_rows),
                        ((0, 0), (0, 0), (0, 0), (0, 0), (0, ff_pad - ff_rows)))
        up_sh = up_sh.reshape(pairs, rows, chips, 2, 3, ROWS).transpose(0, 1, 3, 4, 2, 5)
        up_sh = up_sh.reshape(pairs, rows, 2 * half_f)
        both = jnp.concatenate([attn_sh[:, :, :half_w], up_sh[:, :, :half_f],
                                attn_sh[:, :, half_w:], up_sh[:, :, half_f:]], axis=2)
        both = lax.all_gather(both, "c", axis=1, tiled=True)
        mine = lax.dynamic_slice_in_dim(both, core * (half_w + half_f), half_w + half_f, axis=2)
        down_sh = jnp.pad(w_down, ((0, 0), (0, ff_pad - ff_rows), (0, 0)))
        down_sh = jnp.concatenate([down_sh[:, ROWS * part:ROWS * part + ROWS] for part in range(3)], axis=2)

        def gather(part):
            full = lax.all_gather(part, CORE_MAJOR, axis=0, tiled=True)
            return full.reshape(2, full.shape[0] // 2, full.shape[1])

        def after(value, *deps):
            return lax.optimization_barrier((value,) + deps)[0]

        def attn_weights(front):
            return front[0, :, :half_w], front[1, :, :kv_width], front[1, :, kv_width:half_w]

        def hidden(normed, front):
            return [mixed("sd,df->sf", normed, front[half, :, half_w:]) for half in range(2)]

        carry = x_loc
        inputs = []
        kept = []
        front_gate, down_gate = None, None
        for layer in range(pairs):
            front = gather(mine[layer] if front_gate is None else after(mine[layer], front_gate))
            down = gather(after(down_sh[layer], front) if down_gate is None
                          else after(down_sh[layer], front, down_gate))
            inputs.append(carry)
            carry = attn_forward(carry, *attn_weights(front), dims)
            inputs.append(carry)
            acts = [jax.nn.gelu(h).astype(jnp.bfloat16) for h in hidden(norm_bf16(carry), front)]
            front_gate = acts[1]
            proj = sum(mixed("sf,fd->sd", acts[half][:, width * part:width * part + width],
                             down[half, :, width * part:width * part + width])
                       for half in range(2) for part in range(3))
            carry = (carry.astype(jnp.float32) + proj).astype(jnp.bfloat16)
            down_gate = carry
            kept.append((front, down))
        y_loc = carry

        grad_x = g_loc
        outputs = []
        front_gate, down_gate = None, None
        for layer in reversed(range(pairs)):
            if layer == pairs - 1:
                front, down = kept[layer]
            else:
                down = gather(after(down_sh[layer], down_gate))
                front = gather(after(mine[layer], front_gate))
            mlp_x = inputs[2 * layer + 1]
            normed = norm_bf16(mlp_x)
            grad_y = grad_x
            acts, d_hids = [], []
            for half, h in enumerate(hidden(normed, front)):
                gelu_f32, gelu_pull = jax.vjp(jax.nn.gelu, h)
                acts.append(gelu_f32.astype(jnp.bfloat16))
                d_act = jnp.concatenate([mixed("sd,fd->sf", grad_y, down[half, :, width * part:width * part + width])
                                         for part in range(3)], axis=1)
                d_hids.append(gelu_pull(d_act)[0].astype(jnp.bfloat16))
            down_gate = d_hids[1]
            d_norm = sum(mixed("sf,df->sd", d_hids[half], front[half, :, half_w:]) for half in range(2))
            grad_x = (grad_y.astype(jnp.float32) + norm_back(mlp_x, d_norm)).astype(jnp.bfloat16)
            grad_x, attn_parts = attn_backward(inputs[2 * layer], *attn_weights(front), dims, grad_x)
            front_gate = grad_x
            outputs.append(attn_parts + [normed] + d_hids + acts + [grad_y])

        arrays, segments = [], [[], []]
        for parts in outputs[::-1]:
            base = len(arrays)
            arrays += parts
            n_at, dqk, dv, g_at, o_at, n_mlp, dh0, dh1, a0, a1, g_mlp = range(base, base + 11)
            segments[0] += [(half_w // COLS, n_at, 0, dqk, 0), (half_f // COLS, n_mlp, 0, dh0, 0)]
            segments[1] += [(kv_width // COLS, n_at, 0, dv, 0), (q_width // COLS, g_at, 0, o_at, 0),
                            (half_f // COLS, n_mlp, 0, dh1, 0)]
            for half, act in enumerate((a0, a1)):
                segments[half] += [(width // COLS, act, width * part, g_mlp, 0) for part in range(3)]
        summed = grad_scatter(arrays, segments)

        per_layer = summed.shape[0] // pairs
        wide = summed.reshape(pairs, per_layer, ROWS, COLS).transpose(0, 2, 1, 3).reshape(pairs, ROWS, -1)
        split = half_w + half_f
        down_grad = wide[:, :, split:].reshape(pairs, ROWS, 3, width).transpose(0, 2, 1, 3)
        down_grad = down_grad.reshape(pairs, ff_pad, width)[:, :ff_rows]
        merged = lax.all_gather(wide[:, :, None, :split], "c", axis=2, tiled=True)
        merged = lax.dynamic_slice_in_dim(merged, core * rows, rows, axis=1)
        attn_grad = jnp.concatenate([merged[:, :, 0, :half_w], merged[:, :, 1, :half_w]], axis=2)
        up_grad = merged[:, :, :, half_w:].reshape(pairs, rows, 2, 3, chips, ROWS).transpose(0, 1, 4, 2, 3, 5)
        up_grad = up_grad.reshape(pairs, rows, chips * 2, ff_pad)[:, :, :, :ff_rows].reshape(pairs, rows, ff)
        splits = [q_width, q_width + kv_width, q_width + 2 * kv_width]
        d_q, d_k, d_v, d_o = jnp.split(attn_grad, splits, axis=2)
        return (y_loc[None], grad_x[None],
                d_q.reshape(w_q.shape), d_k.reshape(w_k.shape), d_v.reshape(w_v.shape), d_o.reshape(w_o.shape),
                up_grad, down_grad)

    return jax.shard_map(body, mesh=mesh4, in_specs=(row_spec,) + (weight_spec,) * 6 + (row_spec,),
                         out_specs=(row_spec, row_spec) + (weight_spec,) * 6, check_vma=False)
```

time: 2760 us -> 1150 us (0.42)
  waiting for transfers between devices: 2300 us -> 481 us
  Pallas kernels: 0 us -> 264 us
  other arithmetic: 60.7 us -> 4.54 us
  matrix products: 316 us -> 288 us
    reduce_scatter x10 -> x0, waiting for transfers between devices: 1420 us -> none  [the longest x2 517 us: body(): lax.psum_scatter(d_down, ALL_AXES, scatter_dimension=0, tiled=True)]
    all_gather x16 -> x7, waiting for transfers between devices: 856 us -> 466 us  [the longest x6 466 us: gather(): full = lax.all_gather(part, CORE_MAJOR, axis=0, tiled=True)]
    pallas_call x0 -> x1, Pallas kernels: none -> 264 us  [grad_scatter(): pl.pallas_call(functools.partial(grad_kernel, segments, n_chunks, len(arr...]
    another operation x6 -> x0, other arithmetic: 49.2 us -> none  [the longest x2 38.9 us: body(): jnp.stack([mixed('sd,sf->df', normed, d_hid[:, :half_f]).astype(jnp.bfloa...]
    dot_general x51 -> x59, matrix products: 308 us -> 280 us  [mixed(): return jnp.einsum(form, left, right, preferred_element_type=jnp.float32)]
  transfers between devices with their start and end apart: 27 -> 8, of which waited for: 22 -> 7; matrix products, arithmetic and copies ran while one was open for 13% -> 18% of each run, Pallas kernels for 0% -> 0%
where the time goes in v2:
time: 1150 us; the launch traced here: 1140 us
  waiting for transfers between devices  481 us (42%)
  matrix products  288 us (25%)
  Pallas kernels  264 us (23%)
  local copies, waits for them, and re-layouts  84.5 us (7%)
  between operations  15.8 us (1%)
    all_gather x6, waiting for transfers between devices, gather(): full = lax.all_gather(part, CORE_MAJOR, axis=0, tiled=True)  466 us
    dot_general x59, matrix products, mixed(): return jnp.einsum(form, left, right, preferred_element_type=jnp.float32)  280 us
    pallas_call x1, Pallas kernels, grad_scatter(): pl.pallas_call(functools.partial(grad_kernel, segments, n_chunks, len(arr...  264 us
  transfers between devices with their start and end apart: 8, of which 7 were waited for; matrix products, arithmetic and copies ran while one was open for 18% of the time, Pallas kernels for 0%

profile of v2, /device:TPU:1, one launch (start us, length us, event | category | flops | bytes accessed | tf_op | source)
XLA Modules:
  0.0 1140.3 jit_solution(15317928084888569555)
XLA Ops:
  9.5 4.3 reshape.260
  20.6 15.6 %all-gather.11.cloned.1.call-done = bf16[2,24,12800]{2,0,1:T(2,128)(2,1)} async-done(((bf16[2,12,12800]{2,0,1:T(2,128)(2,1)}), bf16[2,24,12800]{2,0,1:T(2,128)(2,1)}) %all-gather.11.cloned.1.call-update) | async-done | bytes 1228816 | tf_op jit(solution)/shard_map/all_gather | solution.py:325
  40.7 115.6 %all-gather.23.cloned.1.call-done = bf16[1,3072,6400]{2,1,0:T(8,128)(2,1)} async-done(((bf16[1,24,6400]{2,1,0:T(8,128)(2,1)}), bf16[1,3072,6400]{2,1,0:T(8,128)(2,1)}) %all-gather.23.cloned.1.call-update) | async-done | bytes 39321616 | tf_op jit(solution)/shard_map/all_gather | solution.py:331
  157.6 3.9 fusion.124
  169.6 4.1 multiply_reduce_fusion.3
  173.9 9.8 fusion.91
  184.0 9.3 fusion.83
  193.3 63.1 %all-gather.13.cloned.1.call-done = bf16[3072,4608]{1,0:T(8,128)(2,1)} async-done(((bf16[24,4608]{1,0:T(8,128)(2,1)}), bf16[3072,4608]{1,0:T(8,128)(2,1)}) %all-gather.13.cloned.1.call-update) | async-done | bytes 28311568 | tf_op jit(solution)/shard_map/all_gather | solution.py:331
  277.7 96.5 %all-gather.15.cloned.1.call-done = bf16[3072,6400]{1,0:T(8,128)(2,1)} async-done(((bf16[24,6400]{1,0:T(8,128)(2,1)}), bf16[3072,6400]{1,0:T(8,128)(2,1)}) %all-gather.15.cloned.1.call-update) | async-done | bytes 39321616 | tf_op jit(solution)/shard_map/all_gather | solution.py:331
  375.0 4.0 fusion.123
  388.9 4.3 multiply_reduce_fusion.2
  393.3 81.4 %all-gather.17.cloned.1.call-done = bf16[3072,4608]{1,0:T(8,128)(2,1)} async-done(((bf16[24,4608]{1,0:T(8,128)(2,1)}), bf16[3072,4608]{1,0:T(8,128)(2,1)}) %all-gather.17.cloned.1.call-update) | async-done | bytes 28311568 | tf_op jit(solution)/shard_map/all_gather | solution.py:331
  474.7 4.2 fusion.108
  479.0 4.0 fusion.109
  483.0 4.0 fusion.110
  487.0 9.7 fusion.61
  497.7 4.2 fusion.111
  502.0 4.0 fusion.112
  506.0 4.0 fusion.113
  510.0 9.4 fusion.54
  520.6 8.0 fusion.7
  528.7 8.1 multiply_reduce_fusion.1
  545.4 4.9 fusion.141
  553.5 5.1 fusion.179
  561.3 4.5 fusion.16
  568.0 4.8 fusion.37
  572.8 21.2 %all-gather.19.cloned.1.call-done = bf16[3072,4608]{1,0:T(8,128)(2,1)} async-done(((bf16[24,4608]{1,0:T(8,128)(2,1)}), bf16[3072,4608]{1,0:T(8,128)(2,1)}) %all-gather.19.cloned.1.call-update) | async-done | bytes 28311568 | tf_op jit(solution)/shard_map/all_gather | solution.py:331
  594.1 5.0 fusion.24
  599.1 5.0 fusion.25
  604.1 5.0 fusion.26
  609.1 5.1 fusion.21
  614.2 5.1 fusion.22
  619.3 5.1 fusion.23
  624.4 87.7 %all-gather.21.cloned.1.call-done = bf16[3072,6400]{1,0:T(8,128)(2,1)} async-done(((bf16[24,6400]{1,0:T(8,128)(2,1)}), bf16[3072,6400]{1,0:T(8,128)(2,1)}) %all-gather.21.cloned.1.call-update) | async-done | bytes 39321616 | tf_op jit(solution)/shard_map/all_gather | solution.py:331
  714.3 4.0 fusion.122
  719.8 9.8 multiply_convert_fusion.1
  729.6 11.4 %fusion.11 = f32[192,1536]{1,0:T(8,128)} fusion(bf16[192,4608]{1,0:T(8,128)(2,1)S(1)} %get-tuple-element.45.refs_6_, bf16[2,1536,6400]{2,1,0:T(8,128)(2,1)} %bitcast.556), kind=kOutput, calls=%fused_computation.17 | convolution fusion | flops 2717908992 | bytes 17104896 | tf_op jit(solution)/shard_map/sf,df->sd/dot_general | solution.py:251
  741.1 9.7 multiply_convert_fusion
  750.8 10.8 multiply_reduce_fusion
  777.2 4.8 fusion.142
  782.0 5.6 fusion.178
  796.4 4.8 fusion.18
  811.0 264.4 %grad_scatter.1 = f32[86,24,256]{2,1,0:T(8,128)} custom-call(bf16[192,1536]{1,0:T(8,128)(2,1)} %get-tuple-element.54.refs_0_, bf16[192,1792]{1,0:T(8,128)(2,1)} %copy-done.8, bf16[192,256]{1,0:T(8,128)(2,1)} %get-tuple-element.81.refs_2_, bf16[192,1536]{1,0:T(8,128)(2,1)} %copy-done.2, bf16[192,1536]{1,0:T(8,128)(2,1)} %reshape.290.refs_4_, ...), custom_call_target="tpu_custom_call" | custom-call | tf_op jit(solution)/shard_map/grad_scatter/pallas_call | solution.py:225
  1081.8 3.8 fusion.97
  1096.2 4.3 fusion.125
  1110.6 5.0 reshape.297
  1115.6 8.5 copy.200
  1124.1 6.1 reshape.298
  (260 shorter events, 141.3 us)
Async XLA Ops:
  7.2 29.1 %all-gather.11.cloned.1.call-start = ((), (), s32[]{:S(2)}) async-start(), calls=%async_computation | async-start | bytes 1843200 | tf_op jit(solution)/shard_map/all_gather | solution.py:325
  19.5 20.2 %copy-start.26 = (bf16[2,70,1536]{2,0,1:T(2,128)(2,1)S(1)}, bf16[2,70,1536]{2,0,1:T(2,128)(2,1)}, u32[]{:S(2)}) copy-start(bf16[2,70,1536]{2,0,1:T(2,128)(2,1)} %param.14) | copy-start | bytes 1290244
  20.5 135.7 %all-gather.23.cloned.1.call-start = ((), (), s32[]{:S(2)}) async-start(), calls=%async_computation.6 | async-start | bytes 39628800 | tf_op jit(solution)/shard_map/all_gather | solution.py:331
  39.6 117.0 %copy-start.3 = (bf16[1,192,1536]{2,1,0:T(8,128)(2,1)S(1)}, bf16[1,192,1536]{2,1,0:T(8,128)(2,1)}, u32[]{:S(2)}) copy-start(bf16[1,192,1536]{2,1,0:T(8,128)(2,1)} %param.8) | copy-start | bytes 1769476
  39.6 216.7 %all-gather.13.cloned.1.call-start = ((), (), s32[]{:S(2)}) async-start(), calls=%async_computation.1 | async-start | bytes 28532736 | tf_op jit(solution)/shard_map/all_gather | solution.py:331
  156.3 218.0 %all-gather.15.cloned.1.call-start = ((), (), s32[]{:S(2)}) async-start(), calls=%async_computation.2 | async-start | bytes 39628800 | tf_op jit(solution)/shard_map/all_gather | solution.py:331
  156.6 7.2 copy-start.39
  156.8 4.7 copy-start.45
  156.8 5.4 copy-start.47
  173.7 10.0 copy-start.49
  173.7 100.4 %copy-start.5 = (f32[192,1536]{1,0:T(8,128)}, f32[192,1536]{1,0:T(8,128)S(1)}, u32[]{:S(2)}) copy-start(f32[192,1536]{1,0:T(8,128)S(1)} %get-tuple-element.64) | copy-start | bytes 3538948
  173.7 9.9 copy-start.43
  173.9 10.1 copy-start.9
  183.7 291.1 %all-gather.17.cloned.1.call-start = ((), (), s32[]{:S(2)}) async-start(), calls=%async_computation.3 | async-start | bytes 28532736 | tf_op jit(solution)/shard_map/all_gather | solution.py:331
  374.3 219.8 %all-gather.19.cloned.1.call-start = ((), (), s32[]{:S(2)}) async-start(), calls=%async_computation.4 | async-start | bytes 28532736 | tf_op jit(solution)/shard_map/all_gather | solution.py:331
  375.0 4.9 copy-start.12
  393.3 116.7 %copy-start.11 = (bf16[192,1536]{1,0:T(8,128)(2,1)}, bf16[192,1536]{1,0:T(8,128)(2,1)S(1)}, u32[]{:S(2)}) copy-start(bf16[192,1536]{1,0:T(8,128)(2,1)S(1)} %multiply_convert_fusion.4.refs_16_) | copy-start | bytes 1769476
  496.8 215.3 %all-gather.21.cloned.1.call-start = ((), (), s32[]{:S(2)}) async-start(), calls=%async_computation.5 | async-start | bytes 39628800 | tf_op jit(solution)/shard_map/all_gather | solution.py:331
  520.6 8.0 copy-start.18
  537.1 30.4 %copy-start = (bf16[192,1536]{1,0:T(8,128)(2,1)}, bf16[192,1536]{1,0:T(8,128)(2,1)S(1)}, u32[]{:S(2)}) copy-start(bf16[192,1536]{1,0:T(8,128)(2,1)S(1)} %fusion.149.refs_14_) | copy-start | bytes 1769476
  537.1 5.2 copy-start.28
  540.8 4.6 copy-start.37
  540.8 4.6 copy-start.59
  561.3 4.5 copy-start.31
  567.9 193.7 %copy-start.1 = (bf16[192,1536]{1,0:T(8,128)(2,1)}, bf16[192,1536]{1,0:T(8,128)(2,1)S(1)}, u32[]{:S(2)}) copy-start(bf16[192,1536]{1,0:T(8,128)(2,1)S(1)} %fusion.151.refs_10_) | copy-start | bytes 1769476
  568.0 536.2 %all-gather.25.cloned.1.call-start = ((), (), s32[]{:S(2)}) async-start(), calls=%async_computation.7 | async-start | bytes 3686400 | tf_op jit(solution)/shard_map/all_gather | solution.py:407
  619.3 92.8 %copy-start.4 = (bf16[1,192,1536]{2,1,0:T(8,128)(2,1)S(1)}, bf16[1,192,1536]{2,1,0:T(8,128)(2,1)}, u32[]{:S(2)}) copy-start(bf16[1,192,1536]{2,1,0:T(8,128)(2,1)} %param.8) | copy-start | bytes 1769476
  619.3 92.8 %copy-start.48 = (f32[192]{0:T(256)S(1)}, f32[192]{0:T(256)}, u32[]{:S(2)}) copy-start(f32[192]{0:T(256)} %copy-done.47) | copy-start | bytes 2308
  714.3 5.5 copy-start.10
  714.3 5.5 copy-start.55
  714.3 5.5 copy-start.56
  714.3 5.5 copy-start.57
  729.6 11.4 %copy-start.20 = (bf16[192,4608]{1,0:T(8,128)(2,1)}, bf16[192,4608]{1,0:T(8,128)(2,1)S(1)}, u32[]{:S(2)}) copy-start(bf16[192,4608]{1,0:T(8,128)(2,1)S(1)} %get-tuple-element.45.refs_6_) | copy-start | bytes 5308420
  729.6 11.5 %copy-start.52 = (f32[192,1536]{1,0:T(8,128)S(1)}, f32[192,1536]{1,0:T(8,128)}, u32[]{:S(2)}) copy-start(f32[192,1536]{1,0:T(8,128)} %fusion.21) | copy-start | bytes 3538948
  729.6 11.5 %copy-start.53 = (f32[192,1536]{1,0:T(8,128)S(1)}, f32[192,1536]{1,0:T(8,128)}, u32[]{:S(2)}) copy-start(f32[192,1536]{1,0:T(8,128)} %fusion.22) | copy-start | bytes 3538948
  729.6 11.5 %copy-start.54 = (f32[192,1536]{1,0:T(8,128)S(1)}, f32[192,1536]{1,0:T(8,128)}, u32[]{:S(2)}) copy-start(f32[192,1536]{1,0:T(8,128)} %fusion.23) | copy-start | bytes 3538948
  741.1 9.7 copy-start.6
  750.8 10.8 copy-start.21
  750.8 10.8 copy-start.50
  750.8 10.8 copy-start.44
  762.0 46.3 %copy-start.2 = (bf16[192,1536]{1,0:T(8,128)(2,1)}, bf16[192,1536]{1,0:T(8,128)(2,1)S(1)}, u32[]{:S(2)}) copy-start(bf16[192,1536]{1,0:T(8,128)(2,1)S(1)} %fusion.153.refs_3_) | copy-start | bytes 1769476
  762.0 7.1 copy-start.15
  768.1 9.1 copy-start.29
  768.1 5.6 copy-start.41
  777.2 10.4 copy-start.60
  796.4 4.8 copy-start.8
  796.4 4.8 copy-start.32
  796.4 4.8 copy-start.33
  (23 other events, 65.3 us)
Sparse Core Ops, SparseCore 0:
  20.7 15.5 all-gather.10
  39.8 116.4 all-gather.22
  159.3 97.0 all-gather.12
  259.8 114.3 all-gather.14
  377.7 97.0 all-gather.16
  496.9 97.1 all-gather.18
  597.6 114.4 all-gather.20
  1081.9 13.0 all-gather.24

commit v3 on v2

--- a/solution.py
+++ b/solution.py
@@ -234,6 +234,272 @@
     )(*arrays)
 
 
+PER_HALF = 43
+HEAD = 128
+
+
+def forward_kernel(n_layers, x_ref, shard, acts, w_out, wbuf, peer, state, normed, q_buf, k_buf, v_buf, gelu_buf, acc,
+                   ring_send, ring_recv, pair_send, pair_recv, keep_sem, credit):
+    core = lax.axis_index("c")
+    place = {dim: lax.axis_index(dim) for dim in DIMS}
+    nxt = {dim: lax.rem(place[dim] + 1, 4) for dim in DIMS}
+    prv = {dim: lax.rem(place[dim] + 3, 4) for dim in DIMS}
+    sibling = {"c": 1 - core}
+    partners = [({dim: (nxt, prv)[way][dim]}, 2 * d + 1 - way, 2 * d + way)
+                for d, dim in enumerate(DIMS) for way in range(2)]
+    partners.append((sibling, 6, 6))
+    slots = wbuf.shape[0]
+    n_chunks = n_layers * PER_HALF
+    ready = 6 * LAG
+    last_lag = ready + 2
+    n_ticks = n_chunks + last_lag
+    seq, width = x_ref.shape
+    third = 64 * ROWS
+
+    barrier = pltpu.get_barrier_semaphore()
+    for device, _, _ in partners:
+        pl.semaphore_signal(barrier, inc=1, device_id=device, device_id_type=MESH)
+    pl.semaphore_wait(barrier, len(partners))
+    state[...] = x_ref[...]
+
+    def columns(chunk):
+        return pl.ds(pl.multiple_of(lax.rem(chunk, PER_HALF) * COLS, COLS), COLS)
+
+    def spot(slot, color, stage, position, cols):
+        order = ORDERS[color]
+        index = []
+        for dim in DIMS:
+            if dim in order[:stage]:
+                index.append(slice(None))
+            else:
+                index.append(position if dim == order[stage] else place[dim])
+        return wbuf.at[(slot,) + tuple(index) + (slice(8 * color, 8 * color + 8), cols)]
+
+    halves = (slice(0, COLS // 2), slice(COLS // 2, COLS))
+
+    def send_own(stage, chunk):
+        slot, sem = lax.rem(chunk, slots), lax.rem(chunk, 4)
+        for color in range(3):
+            dim = ORDERS[color][stage]
+            here = spot(slot, color, stage, place[dim], slice(0, COLS))
+            for way in range(2):
+                source = here
+                if stage == 0:
+                    source = shard.at[chunk // PER_HALF, slice(8 * color, 8 * color + 8), columns(chunk)]
+                pltpu.make_async_remote_copy(
+                    src_ref=source, dst_ref=here, send_sem=ring_send.at[2 * stage, sem],
+                    recv_sem=ring_recv.at[2 * stage, sem],
+                    device_id={dim: (nxt, prv)[way][dim]}, device_id_type=MESH).start()
+
+    def send_far(stage, chunk):
+        slot, sem = lax.rem(chunk, slots), lax.rem(chunk, 4)
+        for color in range(3):
+            dim = ORDERS[color][stage]
+            for way in range(2):
+                block = spot(slot, color, stage, (prv, nxt)[way][dim], halves[way])
+                pltpu.make_async_remote_copy(
+                    src_ref=block, dst_ref=block, send_sem=ring_send.at[2 * stage + 1, sem],
+                    recv_sem=ring_recv.at[2 * stage + 1, sem],
+                    device_id={dim: (nxt, prv)[way][dim]}, device_id_type=MESH).start()
+
+    def arrived(part, chunk):
+        slot, sem = lax.rem(chunk, slots), lax.rem(chunk, 4)
+        block = (wbuf.at[slot, 0, 0, 0:2], wbuf.at[slot, 0, 0, 0], wbuf.at[slot, 0, 0:2], wbuf.at[slot, 0, 0],
+                 wbuf.at[slot, 0:2], wbuf.at[slot, 0])[part]
+        whole = pltpu.make_async_remote_copy(src_ref=block, dst_ref=block, send_sem=ring_send.at[part, sem],
+                                             recv_sem=ring_recv.at[part, sem], device_id=sibling,
+                                             device_id_type=MESH)
+        whole.wait_send()
+        whole.wait_recv()
+
+    def enter(chunk):
+        wbuf[lax.rem(chunk, slots), place["z"], place["y"], place["x"]] = shard[chunk // PER_HALF, :, columns(chunk)]
+        send_own(0, chunk)
+
+    def pair_copy(chunk):
+        slot = lax.rem(chunk, 4)
+        return pltpu.make_async_remote_copy(
+            src_ref=wbuf.at[lax.rem(chunk, slots)], dst_ref=peer.at[slot], send_sem=pair_send.at[slot],
+            recv_sem=pair_recv.at[slot], device_id=sibling, device_id_type=MESH)
+
+    def keep_copies(chunk):
+        slot = lax.rem(chunk, 4)
+        return (pltpu.make_async_copy(wbuf.at[lax.rem(chunk, slots)], w_out.at[core, :, :, :, :, columns(chunk)],
+                                      keep_sem.at[0, slot]),
+                pltpu.make_async_copy(peer.at[slot], w_out.at[1 - core, :, :, :, :, columns(chunk)],
+                                      keep_sem.at[1, slot]))
+
+    def exchange(chunk):
+        arrived(5, chunk)
+        pair_copy(chunk).start()
+
+    def rms(values):
+        wide = values.astype(jnp.float32)
+        return (wide * lax.rsqrt(jnp.mean(wide * wide, axis=-1, keepdims=True) + EPS)).astype(jnp.bfloat16)
+
+    def dot(left, right):
+        return jnp.dot(left, right, preferred_element_type=jnp.float32)
+
+    def dot_t(left, right):
+        return lax.dot_general(left, right, (((1,), (1,)), ((), ())), preferred_element_type=jnp.float32)
+
+    def compute(chunk):
+        layer, index = chunk // PER_HALF, lax.rem(chunk, PER_HALF)
+        pair = pair_copy(chunk)
+        pair.wait_send()
+        pair.wait_recv()
+        keeping = chunk >= n_chunks - PER_HALF
+
+        @pl.when(keeping)
+        def _():
+            for copy in keep_copies(chunk):
+                copy.start()
+
+        def weights(role):
+            block = wbuf[lax.rem(chunk, slots)] if role == 0 else peer[lax.rem(chunk, 4)]
+            return block.reshape(third, COLS)
+
+        sides = ((0, core), (1, 1 - core))
+
+        @pl.when(index == 0)
+        def _():
+            normed[...] = rms(state[...])
+
+        @pl.when(index < 3)
+        def _():
+            for role, half in sides:
+                start = pl.multiple_of(3 * COLS * half + COLS * index, COLS)
+                q_buf[:, pl.ds(start, COLS)] = dot(normed[...], weights(role)).astype(jnp.bfloat16)
+
+        @pl.when(index == 3)
+        def _():
+            for role, half in sides:
+                both = dot(normed[...], weights(role)).astype(jnp.bfloat16)
+                start = pl.multiple_of(HEAD * half, HEAD)
+                k_buf[:, pl.ds(start, HEAD)] = both[:, :HEAD]
+                v_buf[:, pl.ds(start, HEAD)] = both[:, HEAD:]
+
+        @pl.when((index >= 4) & (index < 7))
+        def _():
+            rows = lax.broadcasted_iota(jnp.int32, (seq, seq), 0)
+            cols = lax.broadcasted_iota(jnp.int32, (seq, seq), 1)
+            for role, half in sides:
+                start = pl.multiple_of(HEAD * half, HEAD)
+                key, value = k_buf[:, pl.ds(start, HEAD)], v_buf[:, pl.ds(start, HEAD)]
+                outs = []
+                for head in range(2):
+                    at = pl.multiple_of(3 * COLS * half + COLS * (index - 4) + HEAD * head, HEAD)
+                    scores = dot_t(q_buf[:, pl.ds(at, HEAD)], key) * (HEAD ** -0.5)
+                    scores = jnp.where(rows >= cols, scores, MASK_FILL)
+                    weight = jnp.exp(scores - jnp.max(scores, axis=-1, keepdims=True))
+                    prob = weight / jnp.sum(weight, axis=-1, keepdims=True)
+                    outs.append(dot(prob.astype(jnp.bfloat16), value).astype(jnp.bfloat16))
+                part = dot_t(jnp.concatenate(outs, axis=1), weights(role))
+                if role == 0:
+                    @pl.when(index == 4)
+                    def _(part=part):
+                        acc[...] = part
+
+                    @pl.when(index > 4)
+                    def _(part=part):
+                        acc[...] += part
+                else:
+                    acc[...] += part
+
+        @pl.when(index == 6)
+        def _():
+            middle = (state[...].astype(jnp.float32) + acc[...]).astype(jnp.bfloat16)
+            state[...] = middle
+            acts[2 * layer] = middle
+            normed[...] = rms(middle)
+
+        @pl.when((index >= 7) & (index < 25))
+        def _():
+            for role, half in sides:
+                hidden = dot(normed[...], weights(role))
+                start = pl.multiple_of(COLS * (index - 7), COLS)
+                gelu_buf[half, :, pl.ds(start, COLS)] = jax.nn.gelu(hidden).astype(jnp.bfloat16)
+
+        @pl.when(index >= 25)
+        def _():
+            part, block = (index - 25) // 6, lax.rem(index - 25, 6)
+            start, at = pl.multiple_of(third * part, third), pl.multiple_of(COLS * block, COLS)
+            total = sum(dot(gelu_buf[half, :, pl.ds(start, third)], weights(role)) for role, half in sides)
+
+            @pl.when(part == 0)
+            def _():
+                acc[:, pl.ds(at, COLS)] = total
+
+            @pl.when(part > 0)
+            def _():
+                acc[:, pl.ds(at, COLS)] += total
+
+        @pl.when(index == PER_HALF - 1)
+        def _():
+            result = (state[...].astype(jnp.float32) + acc[...]).astype(jnp.bfloat16)
+            state[...] = result
+            acts[2 * layer + 1] = result
+
+        @pl.when(keeping)
+        def _():
+            for copy in keep_copies(chunk):
+                copy.wait()
+
+    def forward(part, chunk):
+        arrived(part, chunk)
+        if part % 2 == 0:
+            send_far(part // 2, chunk)
+        else:
+            send_own(part // 2 + 1, chunk)
+
+    steps = [(0, enter)] + [((part + 1) * LAG, functools.partial(forward, part)) for part in range(5)]
+    steps += [(ready, exchange), (last_lag, compute)]
+
+    def tick(now, carry):
+        @pl.when(now >= 2)
+        def _():
+            for _, _, mine in partners:
+                pl.semaphore_wait(credit.at[mine], 1)
+
+        for lag, step in steps:
+            @pl.when((now >= lag) & (now < lag + n_chunks))
+            def _(lag=lag, step=step):
+                step(now - lag)
+
+        @pl.when(now < n_ticks - 2)
+        def _():
+            for device, theirs, _ in partners:
+                pl.semaphore_signal(credit.at[theirs], inc=1, device_id=device, device_id_type=MESH)
+        return carry
+
+    lax.fori_loop(0, n_ticks, tick, 0)
+
+
+def forward_stack(x_loc, shards):
+    n_layers = shards.shape[0]
+    seq, width = x_loc.shape
+    bf16, f32 = jnp.bfloat16, jnp.float32
+    slots = 6 * LAG + 4
+    chunk = (4, 4, 4, ROWS, COLS)
+    return pl.pallas_call(
+        functools.partial(forward_kernel, n_layers),
+        name="forward_stack",
+        out_shape=(jax.ShapeDtypeStruct((2 * n_layers, seq, width), bf16),
+                   jax.ShapeDtypeStruct((2, 4, 4, 4, ROWS, PER_HALF * COLS), bf16)),
+        in_specs=[pl.BlockSpec(memory_space=pltpu.VMEM)] * 2,
+        out_specs=(pl.BlockSpec(memory_space=pltpu.VMEM), pl.BlockSpec(memory_space=pl.ANY)),
+        scratch_shapes=[
+            pltpu.VMEM((slots,) + chunk, bf16), pltpu.VMEM((4,) + chunk, bf16),
+            pltpu.VMEM((seq, width), bf16), pltpu.VMEM((seq, width), bf16),
+            pltpu.VMEM((seq, 6 * COLS), bf16), pltpu.VMEM((seq, 2 * HEAD), bf16), pltpu.VMEM((seq, 2 * HEAD), bf16),
+            pltpu.VMEM((2, seq, 18 * COLS), bf16), pltpu.VMEM((seq, width), f32),
+            pltpu.SemaphoreType.DMA((6, 4)), pltpu.SemaphoreType.DMA((6, 4)), pltpu.SemaphoreType.DMA((4,)),
+            pltpu.SemaphoreType.DMA((4,)), pltpu.SemaphoreType.DMA((2, 4)), pltpu.SemaphoreType.REGULAR((7,))],
+        compiler_params=pltpu.CompilerParams(collective_id=1, has_side_effects=True,
+                                             vmem_limit_bytes=60 * 1024 * 1024),
+    )(x_loc, shards)
+
+
 def rms_norm(values):
     return values * lax.rsqrt(jnp.mean(values * values, axis=-1, keepdims=True) + EPS)
 
@@ -251,48 +517,41 @@
     return jnp.einsum(form, left, right, preferred_element_type=jnp.float32)
 
 
-def attn_inner(x_loc, w_qk, w_v, kv_heads, heads, head_dim):
+def attn_inner(x_loc, halves, heads, head_dim):
     seq = x_loc.shape[0]
-    q_width = heads * head_dim
+    group = heads // 2 * head_dim
     normed = norm_bf16(x_loc)
-    qk = mixed("sd,dw->sw", normed, w_qk).astype(jnp.bfloat16)
-    v_act = mixed("sd,dw->sw", normed, w_v).astype(jnp.bfloat16)
-    q_act = qk[:, :q_width].reshape(seq, kv_heads, heads // kv_heads, head_dim)
-    k_act = qk[:, q_width:].reshape(seq, kv_heads, head_dim)
-    v_act = v_act.reshape(seq, kv_heads, head_dim)
+    qkv = [mixed("sd,dw->sw", normed, half[:, :group + 2 * head_dim]).astype(jnp.bfloat16) for half in halves]
+    q_act = jnp.stack([part[:, :group] for part in qkv], axis=1).reshape(seq, 2, heads // 2, head_dim)
+    k_act = jnp.stack([part[:, group:group + head_dim] for part in qkv], axis=1)
+    v_act = jnp.stack([part[:, group + head_dim:] for part in qkv], axis=1)
     scores = mixed("skge,tke->kgst", q_act, k_act) * (head_dim ** -0.5)
     positions = jnp.arange(seq)
     causal = positions[:, None] >= positions[None, :]
     p_float = jax.nn.softmax(jnp.where(causal, scores, MASK_FILL), axis=-1)
     p_bf16 = p_float.astype(jnp.bfloat16)
     o_act = mixed("kgst,tke->skge", p_bf16, v_act).astype(jnp.bfloat16)
-    return normed, q_act, k_act, v_act, p_float, p_bf16, o_act.reshape(seq, q_width)
-
-
-def attn_forward(x_loc, w_qk, w_v, w_o, dims):
-    o_act = attn_inner(x_loc, w_qk, w_v, *dims)[6]
-    proj = mixed("sw,dw->sd", o_act, w_o)
-    return (x_loc.astype(jnp.float32) + proj).astype(jnp.bfloat16)
-
-
-def attn_backward(x_loc, w_qk, w_v, w_o, dims, grad_y):
-    kv_heads, heads, head_dim = dims
+    return normed, q_act, k_act, v_act, p_float, p_bf16, o_act.reshape(seq, heads * head_dim)
+
+
+def attn_backward(x_loc, halves, heads, head_dim, grad_y):
     seq = x_loc.shape[0]
-    q_width, kv_width = heads * head_dim, kv_heads * head_dim
-    normed, q_act, k_act, v_act, p_float, p_bf16, o_act = attn_inner(x_loc, w_qk, w_v, *dims)
-    d_o = mixed("sd,dw->sw", grad_y, w_o).astype(jnp.bfloat16)
-    d_o = d_o.reshape(seq, kv_heads, heads // kv_heads, head_dim)
+    group = heads // 2 * head_dim
+    inner = group + 2 * head_dim
+    normed, q_act, k_act, v_act, p_float, p_bf16, o_act = attn_inner(x_loc, halves, heads, head_dim)
+    d_o = jnp.stack([mixed("sd,dw->sw", grad_y, half[:, inner:inner + group]).astype(jnp.bfloat16)
+                     for half in halves], axis=1)
+    d_o = d_o.reshape(seq, 2, heads // 2, head_dim)
     d_p = mixed("skge,tke->kgst", d_o, v_act)
     d_v = mixed("kgst,skge->tke", p_bf16, d_o).astype(jnp.bfloat16)
     d_s = p_float * (d_p - jnp.sum(p_float * d_p, axis=-1, keepdims=True))
     ds_bf16 = (d_s * (head_dim ** -0.5)).astype(jnp.bfloat16)
     d_q = mixed("kgst,tke->skge", ds_bf16, k_act).astype(jnp.bfloat16)
     d_k = mixed("kgst,skge->tke", ds_bf16, q_act).astype(jnp.bfloat16)
-    d_qk = jnp.concatenate([d_q.reshape(seq, q_width), d_k.reshape(seq, kv_width)], axis=1)
-    d_v = d_v.reshape(seq, kv_width)
-    d_norm = mixed("sw,dw->sd", d_qk, w_qk) + mixed("sw,dw->sd", d_v, w_v)
+    d_qkv = [jnp.concatenate([d_q[:, kv].reshape(seq, group), d_k[:, kv], d_v[:, kv]], axis=1) for kv in range(2)]
+    d_norm = sum(mixed("sw,dw->sd", d_qkv[kv], halves[kv][:, :inner]) for kv in range(2))
     grad_x = (grad_y.astype(jnp.float32) + norm_back(x_loc, d_norm)).astype(jnp.bfloat16)
-    return grad_x, [normed, d_qk, d_v, grad_y, o_act]
+    return grad_x, [normed] + d_qkv + [grad_y, o_act]
 
 
 def solution(mesh):
@@ -303,7 +562,6 @@
     def body(x_in, w_q, w_k, w_v, w_o, w_up, w_down, grad_out):
         pairs, rows, heads, head_dim = w_q.shape
         kv_heads = w_k.shape[2]
-        dims = (kv_heads, heads, head_dim)
         q_width, kv_width = heads * head_dim, kv_heads * head_dim
         half_w = q_width + kv_width
         ff_rows = w_down.shape[1]
@@ -314,14 +572,14 @@
         core = lax.axis_index("c")
         x_loc, g_loc = x_in[0], grad_out[0]
 
-        attn_sh = jnp.concatenate([w_q.reshape(pairs, rows, q_width), w_k.reshape(pairs, rows, kv_width),
-                                   w_v.reshape(pairs, rows, kv_width), w_o.reshape(pairs, rows, q_width)], axis=2)
+        group = q_width // 2
+        attn_sh = jnp.concatenate([w_q.reshape(pairs, rows, 2, group), w_k.reshape(pairs, rows, 2, head_dim),
+                                   w_v.reshape(pairs, rows, 2, head_dim), w_o.reshape(pairs, rows, 2, group)], axis=3)
         up_sh = jnp.pad(w_up.reshape(pairs, rows, chips, 2, ff_rows),
                         ((0, 0), (0, 0), (0, 0), (0, 0), (0, ff_pad - ff_rows)))
         up_sh = up_sh.reshape(pairs, rows, chips, 2, 3, ROWS).transpose(0, 1, 3, 4, 2, 5)
-        up_sh = up_sh.reshape(pairs, rows, 2 * half_f)
-        both = jnp.concatenate([attn_sh[:, :, :half_w], up_sh[:, :, :half_f],
-                                attn_sh[:, :, half_w:], up_sh[:, :, half_f:]], axis=2)
+        up_sh = up_sh.reshape(pairs, rows, 2, half_f)
+        both = jnp.concatenate([attn_sh, up_sh], axis=3).reshape(pairs, rows, 2 * (half_w + half_f))
         both = lax.all_gather(both, "c", axis=1, tiled=True)
         mine = lax.dynamic_slice_in_dim(both, core * (half_w + half_f), half_w + half_f, axis=2)
         down_sh = jnp.pad(w_down, ((0, 0), (0, ff_pad - ff_rows), (0, 0)))
@@ -334,56 +592,42 @@
         def after(value, *deps):
             return lax.optimization_barrier((value,) + deps)[0]
 
-        def attn_weights(front):
-            return front[0, :, :half_w], front[1, :, :kv_width], front[1, :, kv_width:half_w]
-
-        def hidden(normed, front):
-            return [mixed("sd,df->sf", normed, front[half, :, half_w:]) for half in range(2)]
-
-        carry = x_loc
-        inputs = []
-        kept = []
-        front_gate, down_gate = None, None
-        for layer in range(pairs):
-            front = gather(mine[layer] if front_gate is None else after(mine[layer], front_gate))
-            down = gather(after(down_sh[layer], front) if down_gate is None
-                          else after(down_sh[layer], front, down_gate))
-            inputs.append(carry)
-            carry = attn_forward(carry, *attn_weights(front), dims)
-            inputs.append(carry)
-            acts = [jax.nn.gelu(h).astype(jnp.bfloat16) for h in hidden(norm_bf16(carry), front)]
-            front_gate = acts[1]
-            proj = sum(mixed("sf,fd->sd", acts[half][:, width * part:width * part + width],
-                             down[half, :, width * part:width * part + width])
-                       for half in range(2) for part in range(3))
-            carry = (carry.astype(jnp.float32) + proj).astype(jnp.bfloat16)
-            down_gate = carry
-            kept.append((front, down))
-        y_loc = carry
+        def hidden(normed, ups):
+            return [mixed("sd,df->sf", normed, ups[half]) for half in range(2)]
+
+        acts_out, kept = forward_stack(x_loc, jnp.concatenate([mine, down_sh], axis=2))
+        y_loc = acts_out[-1]
+        inputs = [x_loc] + [acts_out[index] for index in range(2 * pairs - 1)]
+        kept = kept.reshape(2, chips * ROWS, PER_HALF * COLS)
 
         grad_x = g_loc
         outputs = []
         front_gate, down_gate = None, None
         for layer in reversed(range(pairs)):
             if layer == pairs - 1:
-                front, down = kept[layer]
+                attns = [kept[half, :, :half_w] for half in range(2)]
+                ups = [kept[half, :, half_w:half_w + half_f] for half in range(2)]
+                downs = [kept[half, :, half_w + half_f:] for half in range(2)]
             else:
                 down = gather(after(down_sh[layer], down_gate))
                 front = gather(after(mine[layer], front_gate))
+                attns = [front[half, :, :half_w] for half in range(2)]
+                ups = [front[half, :, half_w:] for half in range(2)]
+                downs = [down[half] for half in range(2)]
             mlp_x = inputs[2 * layer + 1]
             normed = norm_bf16(mlp_x)
             grad_y = grad_x
             acts, d_hids = [], []
-            for half, h in enumerate(hidden(normed, front)):
+            for half, h in enumerate(hidden(normed, ups)):
                 gelu_f32, gelu_pull = jax.vjp(jax.nn.gelu, h)
                 acts.append(gelu_f32.astype(jnp.bfloat16))
-                d_act = jnp.concatenate([mixed("sd,fd->sf", grad_y, down[half, :, width * part:width * part + width])
+                d_act = jnp.concatenate([mixed("sd,fd->sf", grad_y, downs[half][:, width * part:width * part + width])
                                          for part in range(3)], axis=1)
                 d_hids.append(gelu_pull(d_act)[0].astype(jnp.bfloat16))
             down_gate = d_hids[1]
-            d_norm = sum(mixed("sf,df->sd", d_hids[half], front[half, :, half_w:]) for half in range(2))
+            d_norm = sum(mixed("sf,df->sd", d_hids[half], ups[half]) for half in range(2))
             grad_x = (grad_y.astype(jnp.float32) + norm_back(mlp_x, d_norm)).astype(jnp.bfloat16)
-            grad_x, attn_parts = attn_backward(inputs[2 * layer], *attn_weights(front), dims, grad_x)
+            grad_x, attn_parts = attn_backward(inputs[2 * layer], attns, heads, head_dim, grad_x)
             front_gate = grad_x
             outputs.append(attn_parts + [normed] + d_hids + acts + [grad_y])
 
@@ -391,11 +635,11 @@
         for parts in outputs[::-1]:
             base = len(arrays)
             arrays += parts
-            n_at, dqk, dv, g_at, o_at, n_mlp, dh0, dh1, a0, a1, g_mlp = range(base, base + 11)
-            segments[0] += [(half_w // COLS, n_at, 0, dqk, 0), (half_f // COLS, n_mlp, 0, dh0, 0)]
-            segments[1] += [(kv_width // COLS, n_at, 0, dv, 0), (q_width // COLS, g_at, 0, o_at, 0),
-                            (half_f // COLS, n_mlp, 0, dh1, 0)]
-            for half, act in enumerate((a0, a1)):
+            n_at, dqkv0, dqkv1, g_at, o_at, n_mlp, dh0, dh1, a0, a1, g_mlp = range(base, base + 11)
+            for half, (dqkv, d_hid, act) in enumerate(((dqkv0, dh0, a0), (dqkv1, dh1, a1))):
+                segments[half] += [((group + 2 * head_dim) // COLS, n_at, 0, dqkv, 0),
+                                   (group // COLS, g_at, 0, o_at, group * half),
+                                   (half_f // COLS, n_mlp, 0, d_hid, 0)]
                 segments[half] += [(width // COLS, act, width * part, g_mlp, 0) for part in range(3)]
         summed = grad_scatter(arrays, segments)
 
@@ -406,11 +650,10 @@
         down_grad = down_grad.reshape(pairs, ff_pad, width)[:, :ff_rows]
         merged = lax.all_gather(wide[:, :, None, :split], "c", axis=2, tiled=True)
         merged = lax.dynamic_slice_in_dim(merged, core * rows, rows, axis=1)
-        attn_grad = jnp.concatenate([merged[:, :, 0, :half_w], merged[:, :, 1, :half_w]], axis=2)
         up_grad = merged[:, :, :, half_w:].reshape(pairs, rows, 2, 3, chips, ROWS).transpose(0, 1, 4, 2, 3, 5)
         up_grad = up_grad.reshape(pairs, rows, chips * 2, ff_pad)[:, :, :, :ff_rows].reshape(pairs, rows, ff)
-        splits = [q_width, q_width + kv_width, q_width + 2 * kv_width]
-        d_q, d_k, d_v, d_o = jnp.split(attn_grad, splits, axis=2)
+        cuts = [group, group + head_dim, group + 2 * head_dim]
+        d_q, d_k, d_v, d_o = jnp.split(merged[:, :, :, :half_w], cuts, axis=3)
         return (y_loc[None], grad_x[None],
                 d_q.reshape(w_q.shape), d_k.reshape(w_k.shape), d_v.reshape(w_v.shape), d_o.reshape(w_o.shape),
                 up_grad, down_grad)

time: 1150 us -> 993 us (0.86)
  waiting for transfers between devices: 481 us -> 87.6 us
  Pallas kernels: 264 us -> 529 us
  matrix products: 288 us -> 206 us
  local copies, waits for them, and re-layouts: 84.5 us -> 133 us
    all_gather x6 -> x2, waiting for transfers between devices: 466 us -> 72 us  [gather(): full = lax.all_gather(part, CORE_MAJOR, axis=0, tiled=True)]
    pallas_call x0 -> x1, Pallas kernels: none -> 264 us  [forward_stack(): pl.pallas_call(functools.partial(forward_kernel, n_layers), name='forward...]
    dot_general x59 -> x42, matrix products: 280 us -> 198 us  [mixed(): return jnp.einsum(form, left, right, preferred_element_type=jnp.float32)]
    squeeze x1 -> x8, local copies, waits for them, and re-layouts: 0.81 us -> 35.8 us  [the longest x1 16.1 us: body(): downs = [kept[half, :, half_w + half_f:] for half in range(2)]]
    another operation x0 -> x15, local copies, waits for them, and re-layouts: none -> 17.9 us  [the longest x6 9.09 us: attn_backward(): jnp.stack([mixed('sd,dw->sw', grad_y, half[:, inner:inner + group]).astyp...]
  transfers between devices with their start and end apart: 8 -> 4, of which waited for: 7 -> 3; matrix products, arithmetic and copies ran while one was open for 18% -> 16% of each run, Pallas kernels for 0% -> 0%
where the time goes in v3:
time: 993 us; the launch traced here: 986 us
  Pallas kernels  529 us (53%)
  matrix products  206 us (21%)
  local copies, waits for them, and re-layouts  133 us (13%)
  waiting for transfers between devices  87.6 us (9%)
  between operations  15 us (2%)
  other arithmetic  14.7 us (1%)
    pallas_call x1, Pallas kernels, grad_scatter(): pl.pallas_call(functools.partial(grad_kernel, segments, n_chunks, len(arr...  265 us
    pallas_call x1, Pallas kernels, forward_stack(): pl.pallas_call(functools.partial(forward_kernel, n_layers), name='forward...  264 us
    dot_general x42, matrix products, mixed(): return jnp.einsum(form, left, right, preferred_element_type=jnp.float32)  198 us
    all_gather x2, waiting for transfers between devices, gather(): full = lax.all_gather(part, CORE_MAJOR, axis=0, tiled=True)  72 us
  transfers between devices with their start and end apart: 4, of which 3 were waited for; matrix products, arithmetic and copies ran while one was open for 16% of the time, Pallas kernels for 0%

profile of v3, /device:TPU:1, one launch (start us, length us, event | category | flops | bytes accessed | tf_op | source)
XLA Modules:
  0.0 985.8 jit_solution(4307658636089166220)
XLA Ops:
  7.2 4.3 reshape.208
  13.7 3.1 reshape.210
  20.3 14.6 %all-gather.6.cloned.1.call-done = bf16[2,24,12800]{2,0,1:T(2,128)(2,1)} async-done(((bf16[2,12,12800]{2,0,1:T(2,128)(2,1)}), bf16[2,24,12800]{2,0,1:T(2,128)(2,1)}) %all-gather.6.cloned.1.call-update) | async-done | bytes 1228816 | tf_op jit(solution)/shard_map/all_gather | solution.py:583
  37.6 264.3 %forward_stack.1 = (bf16[4,192,1536]{2,1,0:T(8,128)(2,1)}, bf16[2,4,4,4,24,11008]{5,4,3,2,1,0:T(8,128)(2,1)}) custom-call(bf16[192,1536]{1,0:T(8,128)(2,1)} %bitcast.408, bf16[2,24,11008]{2,1,0:T(8,128)(2,1)} %pad_maximum_fusion.4.shard), custom_call_target="tpu_custom_call" | custom-call | tf_op jit(solution)/shard_map/forward_stack/pallas_call | solution.py:484
  301.9 16.1 %slice_bitcast_fusion.3 = (bf16[1536,4608]{1,0:T(8,128)(2,1)S(1)}, bf16[1536,4608]{1,0:T(8,128)(2,1)}) fusion(bf16[2,1536,11008]{2,1,0:T(8,128)(2,1)} %bitcast.4), kind=kLoop, calls=%fused_computation.7 | loop fusion | bytes 56623104 | tf_op jit(solution)/shard_map/squeeze | solution.py:610
  323.5 9.8 multiply_convert_fusion
  334.5 4.0 fusion.88
  338.6 4.0 fusion.91
  342.6 4.0 fusion.94
  346.6 9.6 multiply_convert_fusion.1
  356.2 11.5 %fusion.4 = f32[192,1536]{1,0:T(8,128)} fusion(bf16[192,4608]{1,0:T(8,128)(2,1)S(1)} %get-tuple-element.52.refs_17_, bf16[2,1536,11008]{2,1,0:T(8,128)(2,1)} %bitcast.4), kind=kOutput, calls=%fused_computation.10 | convolution fusion | flops 2717908992 | bytes 17104896 | tf_op jit(solution)/shard_map/sf,df->sd/dot_general | solution.py:517
  367.6 10.2 %fusion.159 = (f32[192]{0:T(256)S(1)}, f32[192,1536]{1,0:T(8,128)S(1)}) fusion(bf16[4,192,1536]{2,1,0:T(8,128)(2,1)S(1)} %copy-done.1, f32[192,1536]{1,0:T(8,128)} %fusion.4, bf16[192,4608]{1,0:T(8,128)(2,1)S(1)} %copy-done.12, bf16[2,1536,11008]{2,1,0:T(8,128)(2,1)} %bitcast.4), kind=kOutput, calls=%fused_computation.182 | convolution fusion | flops 2719088384 | bytes 18875136 | tf_op jit(solution)/shard_map/sf,df->sd/dot_general | solution.py:517
  379.3 9.2 slice_bitcast_fusion.17
  402.7 3.1 fusion.146
  414.6 4.0 fusion.257
  418.7 5.0 fusion.130
  425.7 5.5 fusion.197
  434.3 3.1 fusion.72
  437.5 3.2 fusion.179
  453.7 5.0 fusion.16
  458.7 5.1 fusion.14
  463.8 5.1 fusion.12
  468.9 5.0 fusion.22
  473.9 5.0 fusion.20
  478.9 5.0 fusion.18
  483.9 72.0 %all-gather.10.cloned.1.call-done = bf16[3072,6400]{1,0:T(8,128)(2,1)} async-done(((bf16[24,6400]{1,0:T(8,128)(2,1)}), bf16[3072,6400]{1,0:T(8,128)(2,1)}) %all-gather.10.cloned.1.call-update) | async-done | bytes 39321616 | tf_op jit(solution)/shard_map/all_gather | solution.py:589
  555.9 9.0 slice_bitcast_fusion.15
  564.9 3.0 fusion.140
  571.5 9.9 %multiply_convert_fusion.3 = (bf16[192,4608]{1,0:T(8,128)(2,1)}, bf16[192,4608]{1,0:T(8,128)(2,1)S(1)}) fusion(f32[192,1536]{1,0:T(8,128)S(1)} %copy-done.63, f32[192,1536]{1,0:T(8,128)S(1)} %copy-done.62, f32[192,1536]{1,0:T(8,128)S(1)} %copy-done.61, bf16[2,1536,6400]{2,1,0:T(8,128)(2,1)} %bitcast.416, f32[192]{0:T(256)S(1)} %fusion.222, ...), kind=kOutput, calls=%fused_computation.89 | convolution fusion | flops 2740027392 | bytes 21824512 | tf_op jit(solution)/shard_map/sd,df->sf/dot_general | solution.py:517
  581.5 11.4 %fusion.8 = f32[192,1536]{1,0:T(8,128)} fusion(bf16[192,4608]{1,0:T(8,128)(2,1)S(1)} %get-tuple-element.56.refs_6_, bf16[2,1536,6400]{2,1,0:T(8,128)(2,1)} %bitcast.417), kind=kOutput, calls=%fused_computation.14 | convolution fusion | flops 2717908992 | bytes 17104896 | tf_op jit(solution)/shard_map/sf,df->sd/dot_general | solution.py:517
  592.9 9.5 multiply_convert_fusion.2
  602.4 10.7 %fusion.163 = (f32[192]{0:T(256)S(1)}, f32[192,1536]{1,0:T(8,128)S(1)}) fusion(bf16[4,192,1536]{2,1,0:T(8,128)(2,1)S(1)} %copy-done.1, f32[192,1536]{1,0:T(8,128)} %fusion.8, bf16[192,4608]{1,0:T(8,128)(2,1)S(1)} %get-tuple-element.54.refs_7_, bf16[2,1536,6400]{2,1,0:T(8,128)(2,1)} %bitcast.419), kind=kOutput, calls=%fused_computation.186 | convolution fusion | flops 2719088384 | bytes 18875136 | tf_op jit(solution)/shard_map/sf,df->sd/dot_general | solution.py:517
  614.5 3.2 fusion.155
  617.7 3.0 fusion.152
  632.5 3.4 fusion.258
  635.9 3.2 fusion.216
  640.6 4.8 fusion.131
  645.4 5.5 fusion.196
  650.9 2.9 fusion.198
  660.4 264.6 %grad_scatter.1 = f32[86,24,256]{2,1,0:T(8,128)} custom-call(bf16[192,1536]{1,0:T(8,128)(2,1)} %fusion.175.refs_0_, bf16[192,1024]{1,0:T(8,128)(2,1)} %pad_maximum_fusion.7.refs_1_, bf16[192,1024]{1,0:T(8,128)(2,1)} %pad_maximum_fusion.8.refs_2_, bf16[192,1536]{1,0:T(8,128)(2,1)} %copy-done.5, bf16[192,1536]{1,0:T(8,128)(2,1)} %reshape.214.refs_4_, ...), custom_call_target="tpu_custom_call" | custom-call | tf_op jit(solution)/shard_map/grad_scatter/pallas_call | solution.py:225
  925.0 3.7 copy.170
  928.6 2.8 reshape.217
  938.5 3.1 fusion.64
  941.6 3.3 fusion.176
  947.0 4.0 reshape.228
  952.2 5.2 reshape.220
  957.5 8.5 copy.132
  966.0 6.1 reshape.221
  (251 shorter events, 99.3 us)
Async XLA Ops:
  7.2 27.7 %all-gather.6.cloned.1.call-start = ((), (), s32[]{:S(2)}) async-start(), calls=%async_computation | async-start | bytes 1843200 | tf_op jit(solution)/shard_map/all_gather | solution.py:583
  12.5 4.4 copy-start.47
  13.7 3.3 copy-start.48
  13.7 3.4 copy-start.55
  13.7 3.4 copy-start.56
  16.9 2.6 copy-start.23
  19.2 434.4 %all-gather.8.cloned.1.call-start = ((), (), s32[]{:S(2)}) async-start(), calls=%async_computation.1 | async-start | bytes 28532736 | tf_op jit(solution)/shard_map/all_gather | solution.py:589
  36.5 281.5 %copy-start.7 = (bf16[2,24,6400]{2,1,0:T(8,128)(2,1)}, bf16[2,24,6400]{2,1,0:T(8,128)(2,1)S(1)}, u32[]{:S(2)}) copy-start(bf16[2,24,6400]{2,1,0:T(8,128)(2,1)S(1)} %copy.151) | copy-start | bytes 1843204
  301.9 16.1 %copy-start.9 = (bf16[1,192,1536]{2,1,0:T(8,128)(2,1)S(1)}, bf16[1,192,1536]{2,1,0:T(8,128)(2,1)}, u32[]{:S(2)}) copy-start(bf16[1,192,1536]{2,1,0:T(8,128)(2,1)} %param.15) | copy-start | bytes 1769476
  333.4 222.6 %all-gather.10.cloned.1.call-start = ((), (), s32[]{:S(2)}) async-start(), calls=%async_computation.2 | async-start | bytes 39628800 | tf_op jit(solution)/shard_map/all_gather | solution.py:589
  356.2 11.5 %copy-start.13 = (bf16[192,4608]{1,0:T(8,128)(2,1)}, bf16[192,4608]{1,0:T(8,128)(2,1)S(1)}, u32[]{:S(2)}) copy-start(bf16[192,4608]{1,0:T(8,128)(2,1)S(1)} %get-tuple-element.52.refs_17_) | copy-start | bytes 5308420
  356.2 11.5 %copy-start.12 = (bf16[192,4608]{1,0:T(8,128)(2,1)S(1)}, bf16[192,4608]{1,0:T(8,128)(2,1)}, u32[]{:S(2)}) copy-start(bf16[192,4608]{1,0:T(8,128)(2,1)} %get-tuple-element.50.refs_18_) | copy-start | bytes 5308420
  379.3 61.4 %copy-start.3 = (bf16[192,1536]{1,0:T(8,128)(2,1)}, bf16[192,1536]{1,0:T(8,128)(2,1)S(1)}, u32[]{:S(2)}) copy-start(bf16[192,1536]{1,0:T(8,128)(2,1)S(1)} %get-tuple-element.62.refs_14_) | copy-start | bytes 1769476
  379.3 9.2 copy-start.10
  402.7 8.2 copy-start.16
  407.8 3.2 copy-start.17
  408.8 5.8 copy-start.38
  408.8 5.8 copy-start.40
  408.8 5.8 copy-start.49
  408.8 5.8 copy-start.50
  411.1 3.6 copy-start.51
  425.7 6.3 copy-start.19
  432.0 2.2 copy-start.35
  432.0 5.4 copy-start.34
  434.2 3.2 copy-start.37
  434.2 3.2 copy-start.36
  434.3 3.2 copy-start.21
  442.7 504.3 %all-gather.12.cloned.1.call-start = ((), (), s32[]{:S(2)}) async-start(), calls=%async_computation.3 | async-start | bytes 3686400 | tf_op jit(solution)/shard_map/all_gather | solution.py:651
  446.3 7.4 copy-start.4
  564.9 4.4 copy-start.2
  564.9 4.4 copy-start.11
  581.4 11.5 %copy-start.14 = (bf16[192,4608]{1,0:T(8,128)(2,1)}, bf16[192,4608]{1,0:T(8,128)(2,1)S(1)}, u32[]{:S(2)}) copy-start(bf16[192,4608]{1,0:T(8,128)(2,1)S(1)} %get-tuple-element.56.refs_6_) | copy-start | bytes 5308420
  581.5 11.4 %copy-start.58 = (f32[192,1536]{1,0:T(8,128)S(1)}, f32[192,1536]{1,0:T(8,128)}, u32[]{:S(2)}) copy-start(f32[192,1536]{1,0:T(8,128)} %fusion.16) | copy-start | bytes 3538948
  581.5 11.4 %copy-start.59 = (f32[192,1536]{1,0:T(8,128)S(1)}, f32[192,1536]{1,0:T(8,128)}, u32[]{:S(2)}) copy-start(f32[192,1536]{1,0:T(8,128)} %fusion.14) | copy-start | bytes 3538948
  581.5 11.4 %copy-start.60 = (f32[192,1536]{1,0:T(8,128)S(1)}, f32[192,1536]{1,0:T(8,128)}, u32[]{:S(2)}) copy-start(f32[192,1536]{1,0:T(8,128)} %fusion.12) | copy-start | bytes 3538948
  602.4 10.7 %copy-start.15 = (bf16[192,4608]{1,0:T(8,128)(2,1)}, bf16[192,4608]{1,0:T(8,128)(2,1)S(1)}, u32[]{:S(2)}) copy-start(bf16[192,4608]{1,0:T(8,128)(2,1)S(1)} %get-tuple-element.54.refs_7_) | copy-start | bytes 5308420
  614.5 3.2 copy-start.5
  622.0 10.5 %copy-start.52 = (pred[192,192]{0,1:T(8,128)(4,1)S(1)}, pred[192,192]{0,1:T(8,128)(4,1)}, u32[]{:S(2)}) copy-start(pred[192,192]{0,1:T(8,128)(4,1)} %iota_compare_fusion) | copy-start | bytes 110596
  622.1 10.4 %copy-start.53 = (bf16[192,1,128]{2,0,1:T(8,128)(2,1)S(1)}, bf16[192,1,128]{2,0,1:T(8,128)(2,1)}, u32[]{:S(2)}) copy-start(bf16[192,1,128]{2,0,1:T(8,128)(2,1)} %get-tuple-element.74) | copy-start | bytes 147460
  622.1 10.4 %copy-start.54 = (bf16[192,1,128]{2,0,1:T(8,128)(2,1)S(1)}, bf16[192,1,128]{2,0,1:T(8,128)(2,1)}, u32[]{:S(2)}) copy-start(bf16[192,1,128]{2,0,1:T(8,128)(2,1)} %get-tuple-element.76) | copy-start | bytes 147460
  632.5 3.4 copy-start.42
  632.5 3.4 copy-start.43
  635.9 3.2 copy-start.65
  635.9 3.2 copy-start.57
  650.9 2.9 copy-start.22
  938.5 3.1 copy-start.27
  938.5 3.1 copy-start.29
  941.6 3.3 copy-start.6
  (23 other events, 36.6 us)
Sparse Core Ops, SparseCore 0:
  19.4 15.5 all-gather.5
  333.5 95.8 all-gather.7
  442.8 113.0 all-gather.9
  934.0 12.9 all-gather.11

commit v4 on v0

v4 whole, which is shorter than its diff:
```python
import functools

import jax
import jax.numpy as jnp
from jax import lax
from jax.experimental import pallas as pl
from jax.experimental.pallas import tpu as pltpu
from jax.sharding import Mesh, PartitionSpec as P

MESH = pl.DeviceIdType.MESH
ALL_AXES = ("z", "y", "x", "c")
EPS = 1e-6
MASK_FILL = -1e30
DIMS = ("z", "y", "x")
ORDERS = (("x", "y", "z"), ("y", "z", "x"), ("z", "x", "y"))
COLS = 256
ROWS = 24
LAG = 2
HEAD = 128
PER_HALF = 43
UP_BLOCKS = 25
UP_END = UP_BLOCKS * COLS
RING = 4
CUBE = (RING, RING, RING)
SLOTS = 3
TILE = 8
COLORS = range(3)
TWO = range(2)
SIX = range(6)
ALL = Ellipsis
EVERY = slice(None)
QKV, ATTN, FF = 4, 7, 18
DOWN_DONE, UP_DONE, O_DONE = 18, 36, 39
G_AT, DH_AT, O_AT, QKV_AT = 0, 6, 42, 48
NORM_MLP, GRAD, NORM_ATTN = 6, 7, 8
VMEM_LIMIT = 67043328


FIFTH = UP_END // 5


def _rows(color):
    return slice(TILE * color, TILE * color + TILE)


def _rem(value, by):
    return lax.rem(value, by)


def _block(color, stage, position):
    dims = tuple(dim for dim in DIMS if dim not in ORDERS[color][:stage])
    return tuple(position if dim == ORDERS[color][stage] else EVERY for dim in dims)


def _dot(left, right):
    return jnp.dot(left, right, preferred_element_type=jnp.float32)


def _dot_rhs_t(left, right):
    return lax.dot_general(left, right, (((1,), (1,)), ((), ())), preferred_element_type=jnp.float32)


def _dot_lhs_t(left, right):
    return lax.dot_general(left, right, (((0,), (0,)), ((), ())), preferred_element_type=jnp.float32)


def _at(start, size):
    return pl.ds(pl.multiple_of(start, size), size)


def _causal(seq):
    return (lax.broadcasted_iota(jnp.int32, (seq, seq), 0) >= lax.broadcasted_iota(jnp.int32, (seq, seq), 1))


def _probs(query, key, causal):
    scores = jnp.where(causal, _dot_rhs_t(query, key) * (HEAD ** -0.5), MASK_FILL)
    weight = jnp.exp(scores - jnp.max(scores, axis=-1, keepdims=True))
    return weight / jnp.sum(weight, axis=-1, keepdims=True)


def _rms(values):
    wide = values.astype(jnp.float32)
    return (wide * lax.rsqrt(jnp.mean(wide * wide, axis=-1, keepdims=True) + EPS)).astype(jnp.bfloat16)


def _rms_back(values, grad):
    wide = values.astype(jnp.float32)
    scale = lax.rsqrt(jnp.mean(wide * wide, axis=-1, keepdims=True) + EPS)
    return scale * grad - wide * (scale * scale * scale) * jnp.mean(wide * grad, axis=-1, keepdims=True)


class Torus:
    def __init__(self, credit):
        self.core = lax.axis_index("c")
        self.place = {dim: lax.axis_index(dim) for dim in DIMS}
        self.near = tuple({dim: _rem(self.place[dim] + step, 4) for dim in DIMS} for step in (1, 3))
        self.far = {dim: _rem(self.place[dim] + 2, 4) for dim in DIMS}
        self.sibling = {"c": 1 - self.core}
        self.sides = ((0, self.core), (1, 1 - self.core))
        self.credit = credit
        self.partners = [({dim: self.near[way][dim]}, 2 * d + 1 - way, 2 * d + way)
                         for d, dim in enumerate(DIMS) for way in TWO]
        self.partners.append((self.sibling, 6, 6))

    def meet(self):
        barrier = pltpu.get_barrier_semaphore()
        for device, _, _ in self.partners:
            pl.semaphore_signal(barrier, inc=1, device_id=device, device_id_type=MESH)
        pl.semaphore_wait(barrier, len(self.partners))

    def remote(self, source, target, send_sem, recv_sem, device):
        return pltpu.make_async_remote_copy(src_ref=source, dst_ref=target, send_sem=send_sem, recv_sem=recv_sem,
                                            device_id=device, device_id_type=MESH)

    def run(self, steps, n_chunks, n_ticks):
        def tick(now, carry):
            @pl.when(now >= 2)
            def _():
                for _, _, mine in self.partners:
                    pl.semaphore_wait(self.credit.at[mine], 1)

            for lag, step in steps:
                @pl.when((now >= lag) & (now < lag + n_chunks))
                def _(lag=lag, step=step):
                    step(now - lag)

            @pl.when(now < n_ticks - 2)
            def _():
                for device, theirs, _ in self.partners:
                    pl.semaphore_signal(self.credit.at[theirs], inc=1, device_id=device, device_id_type=MESH)
            return carry

        lax.fori_loop(0, n_ticks, tick, 0)


def forward_kernel(n_layers, x_ref, rows_ref, down_ref, acts, w_out, hid_out, gelu_out, norm_out, q_out, k_out, v_out,
                   o_out, wbuf, peer, shard, twin, state, normed, q_buf, k_buf, v_buf, o_buf, gelu_buf, hid_buf, acc,
                   ring_send, ring_recv, pair_send, pair_recv, keep_sem, save_sem, hid_sem, twin_sem, credit):
    torus = Torus(credit)
    core, place, near = torus.core, torus.place, torus.near
    slots = wbuf.shape[0]
    n_chunks = n_layers * PER_HALF
    ready = 6 * LAG
    last_lag = ready + 2
    seq = x_ref.shape[0]
    third = 64 * ROWS
    torus.meet()
    swap = torus.remote(rows_ref.at[1 - core], twin, twin_sem.at[0], twin_sem.at[1], torus.sibling)
    swap.start()
    state[ALL] = x_ref[ALL]
    swap.wait_send()
    swap.wait_recv()
    for layer in range(n_layers):
        shard[layer, :, UP_END:] = down_ref[layer]
        for part in range(5):
            cols = slice(FIFTH * part, FIFTH * part + FIFTH)
            mine = rows_ref[core, layer, :, cols].astype(jnp.float32)
            other = twin[layer, :, cols].astype(jnp.float32)
            first = core == 0
            shard[layer, :, cols] = jnp.concatenate(
                [jnp.where(first, mine, other), jnp.where(first, other, mine)], axis=0).astype(jnp.bfloat16)

    def columns(chunk):
        return _at(_rem(chunk, PER_HALF) * COLS, COLS)

    def spot(slot, color, stage, position, cols):
        order = ORDERS[color]
        index = tuple(EVERY if dim in order[:stage] else position if dim == order[stage] else place[dim]
                      for dim in DIMS)
        return wbuf.at[(slot,) + index + (_rows(color), cols)]

    halves = (slice(0, COLS // 2), slice(COLS // 2, COLS))

    def send_own(stage, chunk):
        slot, sem = _rem(chunk, slots), _rem(chunk, RING)
        for color in COLORS:
            dim = ORDERS[color][stage]
            here = spot(slot, color, stage, place[dim], slice(0, COLS))
            source = here
            if stage == 0:
                source = shard.at[chunk // PER_HALF, _rows(color), columns(chunk)]
            for way in TWO:
                torus.remote(source, here, ring_send.at[2 * stage, sem], ring_recv.at[2 * stage, sem],
                             {dim: near[way][dim]}).start()

    def send_far(stage, chunk):
        slot, sem = _rem(chunk, slots), _rem(chunk, RING)
        for color in COLORS:
            dim = ORDERS[color][stage]
            for way in TWO:
                block = spot(slot, color, stage, near[1 - way][dim], halves[way])
                torus.remote(block, block, ring_send.at[2 * stage + 1, sem], ring_recv.at[2 * stage + 1, sem],
                             {dim: near[way][dim]}).start()

    def arrived(part, chunk):
        slot, sem = _rem(chunk, slots), _rem(chunk, RING)
        block = (wbuf.at[slot, 0, 0, 0:2], wbuf.at[slot, 0, 0, 0], wbuf.at[slot, 0, 0:2], wbuf.at[slot, 0, 0],
                 wbuf.at[slot, 0:2], wbuf.at[slot, 0])[part]
        whole = torus.remote(block, block, ring_send.at[part, sem], ring_recv.at[part, sem], torus.sibling)
        whole.wait_send()
        whole.wait_recv()

    def enter(chunk):
        wbuf[_rem(chunk, slots), place["z"], place["y"], place["x"]] = shard[chunk // PER_HALF, :, columns(chunk)]
        send_own(0, chunk)

    def pass_on(part, chunk):
        arrived(part, chunk)
        if part % 2 == 0:
            send_far(part // 2, chunk)
        else:
            send_own(part // 2 + 1, chunk)

    def pair_copy(chunk):
        slot = _rem(chunk, RING)
        return torus.remote(wbuf.at[_rem(chunk, slots)], peer.at[slot], pair_send.at[slot], pair_recv.at[slot],
                            torus.sibling)

    def exchange(chunk):
        arrived(5, chunk)
        pair_copy(chunk).start()

    def keep_copy(chunk):
        return pltpu.make_async_copy(wbuf.at[_rem(chunk, slots)],
                                     w_out.at[chunk // PER_HALF, :, :, :, :, columns(chunk)],
                                     keep_sem.at[_rem(chunk, RING)])

    def save_copies(layer, names):
        parts = {"n0": (normed, norm_out.at[layer, 0], 0), "n1": (normed, norm_out.at[layer, 1], 1),
                 "q": (q_buf, q_out.at[layer], 2), "k": (k_buf, k_out.at[layer], 3), "v": (v_buf, v_out.at[layer], 4),
                 "o": (o_buf, o_out.at[layer], 5)}
        for half in TWO:
            for part in COLORS:
                parts[f"a{half}{part}"] = (gelu_buf.at[half, :, slice(third * part, third * (part + 1))],
                                           gelu_out.at[layer, 3 * half + part], 6 + 3 * half + part)
        return [pltpu.make_async_copy(parts[name][0], parts[name][1], save_sem.at[parts[name][2]]) for name in names]

    gelu_names = [f"a{half}{part}" for half in TWO for part in COLORS]

    def hidden_copies(layer, order):
        slot, part, at = _rem(order, 2), order // 6, _at(_rem(order, 6) * COLS, COLS)
        return [pltpu.make_async_copy(hid_buf.at[slot, half], hid_out.at[layer, part, half, :, at],
                                      hid_sem.at[slot, half]) for half in TWO]

    def compute(chunk):
        layer, index = chunk // PER_HALF, _rem(chunk, PER_HALF)
        pair = pair_copy(chunk)
        pair.wait_send()
        pair.wait_recv()
        keep_copy(chunk).start()

        def weights(role):
            block = wbuf[_rem(chunk, slots)] if role == 0 else peer[_rem(chunk, RING)]
            return block.reshape(third, COLS)

        @pl.when(index == 0)
        def _():
            normed[ALL] = _rms(state[ALL])
            for copy in save_copies(layer, ["n0"]):
                copy.start()

        @pl.when(index < 3)
        def _():
            for role, half in torus.sides:
                q_buf[:, _at(3 * COLS * half + COLS * index, COLS)] = _dot(
                    normed[ALL], weights(role)).astype(jnp.bfloat16)

        @pl.when(index == 3)
        def _():
            for role, half in torus.sides:
                both = _dot(normed[ALL], weights(role)).astype(jnp.bfloat16)
                k_buf[:, _at(HEAD * half, HEAD)] = both[:, :HEAD]
                v_buf[:, _at(HEAD * half, HEAD)] = both[:, HEAD:]

        @pl.when(index == QKV)
        def _():
            acc[ALL] = jnp.zeros_like(acc)
            for copy in save_copies(layer, ["q", "k", "v"]):
                copy.start()

        @pl.when((index >= QKV) & (index < ATTN))
        def _():
            causal = _causal(seq)
            for role, half in torus.sides:
                key, value = k_buf[:, _at(HEAD * half, HEAD)], v_buf[:, _at(HEAD * half, HEAD)]
                outs = []
                for head in TWO:
                    at = _at(3 * COLS * half + COLS * (index - QKV) + HEAD * head, HEAD)
                    prob = _probs(q_buf[:, at], key, causal)
                    outs.append(_dot(prob.astype(jnp.bfloat16), value).astype(jnp.bfloat16))
                block = jnp.concatenate(outs, axis=1)
                o_buf[3 * half + index - QKV] = block
                acc[ALL] += _dot_rhs_t(block, weights(role))

        @pl.when(index == 6)
        def _():
            middle = (state[ALL].astype(jnp.float32) + acc[ALL]).astype(jnp.bfloat16)
            state[ALL] = middle
            acts[2 * layer] = middle
            for copy in save_copies(layer, ["n0"]):
                copy.wait()
            normed[ALL] = _rms(middle)
            for copy in save_copies(layer, ["n1", "o"]):
                copy.start()

        @pl.when((index >= 8) & (index < 26))
        def _():
            for copy in hidden_copies(layer, index - 8):
                copy.wait()

        @pl.when((index >= ATTN) & (index < UP_BLOCKS))
        def _():
            for role, half in torus.sides:
                hidden = _dot(normed[ALL], weights(role))
                hid_buf[_rem(index - ATTN, 2), half] = hidden
                gelu_buf[half, :, _at(COLS * (index - ATTN), COLS)] = jax.nn.gelu(hidden).astype(jnp.bfloat16)
            for copy in hidden_copies(layer, index - ATTN):
                copy.start()

        @pl.when(index == UP_BLOCKS)
        def _():
            for copy in save_copies(layer, gelu_names):
                copy.start()

        @pl.when(index >= UP_BLOCKS)
        def _():
            part, at = (index - UP_BLOCKS) // 6, _at(COLS * _rem(index - UP_BLOCKS, 6), COLS)
            total = sum(_dot(gelu_buf[half, :, _at(third * part, third)], weights(role))
                        for role, half in torus.sides)

            @pl.when(part == 0)
            def _():
                acc[:, at] = total

            @pl.when(part > 0)
            def _():
                acc[:, at] += total

        @pl.when(index == PER_HALF - 1)
        def _():
            result = (state[ALL].astype(jnp.float32) + acc[ALL]).astype(jnp.bfloat16)
            state[ALL] = result
            acts[2 * layer + 1] = result
            for copy in save_copies(layer, ["n1", "q", "k", "v", "o"] + gelu_names):
                copy.wait()

        keep_copy(chunk).wait()

    steps = [(0, enter)] + [((part + 1) * LAG, functools.partial(pass_on, part)) for part in range(5)]
    torus.run(steps + [(ready, exchange), (last_lag, compute)], n_chunks, n_chunks + last_lag)


def forward_stack(x_loc, rows, down):
    n_layers = down.shape[0]
    seq, width = x_loc.shape
    bf16, f32 = jnp.bfloat16, jnp.float32
    slots = 6 * LAG + 4
    chunk = CUBE + (ROWS, COLS)
    shape = jax.ShapeDtypeStruct
    hbm = pl.BlockSpec(memory_space=pl.ANY)
    vmem = pl.BlockSpec(memory_space=pltpu.VMEM)
    dma = pltpu.SemaphoreType.DMA
    return pl.pallas_call(
        functools.partial(forward_kernel, n_layers),
        name="forward_stack",
        out_shape=(shape((2 * n_layers, seq, width), bf16),
                   shape((n_layers, 4, 4, 4, ROWS, PER_HALF * COLS), bf16),
                   shape((n_layers, 3, 2, seq, width), f32), shape((n_layers, 6, seq, width), bf16),
                   shape((n_layers, 2, seq, width), bf16), shape((n_layers, seq, width), bf16),
                   shape((n_layers, seq, 2 * HEAD), bf16), shape((n_layers, seq, 2 * HEAD), bf16),
                   shape((n_layers, 6, seq, COLS), bf16)),
        in_specs=[vmem] * 3,
        out_specs=(vmem,) + (hbm,) * 8,
        scratch_shapes=[
            pltpu.VMEM((slots,) + chunk, bf16), pltpu.VMEM((RING,) + chunk, bf16),
            pltpu.VMEM((n_layers, ROWS, PER_HALF * COLS), bf16), pltpu.VMEM(rows.shape[1:], bf16),
            pltpu.VMEM((seq, width), bf16), pltpu.VMEM((seq, width), bf16),
            pltpu.VMEM((seq, 6 * COLS), bf16), pltpu.VMEM((seq, 2 * HEAD), bf16), pltpu.VMEM((seq, 2 * HEAD), bf16),
            pltpu.VMEM((6, seq, COLS), bf16), pltpu.VMEM((2, seq, 18 * COLS), bf16),
            pltpu.VMEM((2, 2, seq, COLS), f32), pltpu.VMEM((seq, width), f32),
            dma((6, RING)), dma((6, RING)), dma((RING,)), dma((RING,)), dma((RING,)), dma((12,)), dma((2, 2)), dma((2,)),
            pltpu.SemaphoreType.REGULAR((7,))],
        compiler_params=pltpu.CompilerParams(collective_id=1, has_side_effects=True,
                                             vmem_limit_bytes=VMEM_LIMIT),
    )(x_loc, rows, down)


def backward_kernel(n_layers, *refs):
    (g_ref, x_ref, acts, w_own, hid_in, gelu_in, norm_in, q_in, k_in, v_in, o_in,
     rows_out, down_out, dx_ref,
     mine, theirs, lefts, rights, hid_buf, dact, dnorm, q_buf, k_buf, v_buf, x_mid, x_in, dk_acc, dv_acc,
     outgo, peer, out, away, sum0, sum1, sum2, sa0, ra0, sb0, rb0, sa1, ra1, sb1, rb1, sa2, ra2, sb2, rb2,
     load_sem, own_sem, push_send, push_recv, pair_send, pair_recv, ring_send, ring_recv, swap_sem, credit) = refs
    torus = Torus(credit)
    core, place, near = torus.core, torus.place, torus.near
    sums = (sum0, sum1, sum2)
    half_bufs = ((sa0, ra0), (sa1, ra1), (sa2, ra2))
    full_bufs = ((sb0, rb0), (sb1, rb1), (sb2, rb2))
    n_chunks = n_layers * PER_HALF
    seq, width = g_ref.shape
    third = 64 * ROWS
    leads = sum0.shape[0]

    def pair_of(chunk):
        return n_layers - 1 - chunk // PER_HALF

    def columns(chunk):
        index = _rem(chunk, PER_HALF)
        block = jnp.where(index < DOWN_DONE, UP_BLOCKS + index,
                          jnp.where(index < UP_DONE, index - 11, jnp.where(index < O_DONE, index - 32, index - 39)))
        return _at(block * COLS, COLS)

    def loads(pair, names):
        def source(name):
            return {"a": (gelu_in.at[pair], lefts.at[0:6], 0), "n_mlp": (norm_in.at[pair, 1], lefts.at[NORM_MLP], 1),
                    "n_attn": (norm_in.at[pair, 0], lefts.at[NORM_ATTN], 2), "o": (o_in.at[pair], rights.at[O_AT:QKV_AT], 3),
                    "q": (q_in.at[pair], q_buf, 4), "k": (k_in.at[pair], k_buf, 5), "v": (v_in.at[pair], v_buf, 6),
                    "x_mid": (acts.at[2 * pair], x_mid, 7), "h0": (hid_in.at[pair, 0], hid_buf, 8),
                    "h1": (hid_in.at[pair, 1], hid_buf, 8), "h2": (hid_in.at[pair, 2], hid_buf, 8)}[name]
        return [pltpu.make_async_copy(source(name)[0], source(name)[1], load_sem.at[source(name)[2]])
                for name in names]

    def start(pair, names):
        for copy in loads(pair, names):
            copy.start()

    def finish(pair, names):
        for copy in loads(pair, names):
            copy.wait()

    def first_input(ref):
        return pltpu.make_async_copy(ref, x_in, load_sem.at[9])

    torus.meet()
    start(n_layers - 1, ["a"])
    for block in SIX:
        rights[block] = g_ref[:, COLS * block:COLS * block + COLS]

    def own_copy(chunk):
        slot = _rem(chunk, SLOTS)
        return pltpu.make_async_copy(w_own.at[pair_of(chunk), :, :, :, :, columns(chunk)], mine.at[slot],
                                     own_sem.at[slot])

    def push_copy(chunk):
        slot = _rem(chunk, SLOTS)
        return torus.remote(w_own.at[pair_of(chunk), :, :, :, :, columns(chunk)], theirs.at[slot],
                            push_send.at[slot], push_recv.at[slot], torus.sibling)

    def fetch(chunk):
        own_copy(chunk).start()
        push_copy(chunk).start()

    def total_grad():
        return jnp.concatenate([rights[block] for block in SIX], axis=1).astype(jnp.float32)

    def consume(chunk):
        pair, index = pair_of(chunk), _rem(chunk, PER_HALF)
        slot = _rem(chunk, SLOTS)
        own_copy(chunk).wait()
        push = push_copy(chunk)
        push.wait_send()
        push.wait_recv()

        def weights(role):
            return (mine, theirs)[role][slot].reshape(third, COLS)

        @pl.when(index == 0)
        def _():
            start(pair, ["n_mlp", "n_attn", "o", "q", "k", "v", "x_mid", "h0"])

            @pl.when(pair == 0)
            def _():
                first_input(x_ref).start()

            @pl.when(pair > 0)
            def _():
                first_input(acts.at[2 * pair - 1]).start()
            finish(pair, ["a"])

        for part in (1, 2):
            @pl.when(index == 6 * part)
            def _(part=part):
                start(pair, [f"h{part}"])

        @pl.when(index < DOWN_DONE)
        def _():
            block = _rem(index, 6)
            for role, half in torus.sides:
                product = _dot_rhs_t(rights[block], weights(role))

                @pl.when(block == 0)
                def _(product=product, half=half):
                    dact[half] = product

                @pl.when(block > 0)
                def _(product=product, half=half):
                    dact[half] += product

        @pl.when((index < DOWN_DONE) & (_rem(index, 6) == 5))
        def _():
            finish(pair, ["h0"])
            for half in TWO:
                for block in SIX:
                    cols = slice(COLS * block, COLS * block + COLS)
                    hidden = hid_buf[half, :, cols]
                    bend = jnp.tanh(0.7978845608028654 * (hidden + 0.044715 * (hidden * hidden * hidden)))
                    slope = 0.5 * (1.0 + bend) + 0.5 * hidden * (1.0 - bend * bend) * (
                        0.7978845608028654 * (1.0 + 0.134145 * (hidden * hidden)))
                    rights[DH_AT + FF * half + index - 5 + block] = (dact[half, :, cols] * slope).astype(jnp.bfloat16)

        @pl.when(index == DOWN_DONE)
        def _():
            finish(pair, ["n_mlp"])
            dnorm[ALL] = jnp.zeros_like(dnorm)

            @pl.when(pair > 0)
            def _():
                start(pair - 1, ["a"])

        @pl.when((index >= DOWN_DONE) & (index < UP_DONE))
        def _():
            dnorm[ALL] += sum(_dot_rhs_t(rights[DH_AT + FF * half + index - DOWN_DONE], weights(role))
                              for role, half in torus.sides)

        @pl.when(index == UP_DONE - 1)
        def _():
            finish(pair, ["x_mid"])
            lefts[GRAD] = (total_grad() + _rms_back(x_mid[ALL], dnorm[ALL])).astype(jnp.bfloat16)

        @pl.when(index == UP_DONE)
        def _():
            finish(pair, ["o", "q", "k", "v"])
            dk_acc[ALL] = jnp.zeros_like(dk_acc)
            dv_acc[ALL] = jnp.zeros_like(dv_acc)

        @pl.when((index >= UP_DONE) & (index < O_DONE))
        def _():
            causal = _causal(seq)
            for role, half in torus.sides:
                d_o = _dot(lefts[GRAD], weights(role)).astype(jnp.bfloat16)
                key, value = k_buf[:, _at(HEAD * half, HEAD)], v_buf[:, _at(HEAD * half, HEAD)]
                d_q = []
                for head in TWO:
                    query = q_buf[:, _at(3 * COLS * half + COLS * (index - UP_DONE) + HEAD * head, HEAD)]
                    d_head = d_o[:, HEAD * head:HEAD * head + HEAD]
                    prob = _probs(query, key, causal)
                    d_prob = _dot_rhs_t(d_head, value)
                    dv_acc[half] += _dot_lhs_t(prob.astype(jnp.bfloat16), d_head)
                    d_score = prob * (d_prob - jnp.sum(prob * d_prob, axis=-1, keepdims=True))
                    d_score = (d_score * (HEAD ** -0.5)).astype(jnp.bfloat16)
                    d_q.append(_dot(d_score, key).astype(jnp.bfloat16))
                    dk_acc[half] += _dot_lhs_t(d_score, query)
                rights[QKV_AT + QKV * half + index - UP_DONE] = jnp.concatenate(d_q, axis=1)

        @pl.when(index == O_DONE - 1)
        def _():
            for half in TWO:
                rights[QKV_AT + QKV * half + QKV - 1] = jnp.concatenate([dk_acc[half], dv_acc[half]], axis=1).astype(jnp.bfloat16)

        @pl.when(index == O_DONE)
        def _():
            finish(pair, ["n_attn"])
            dnorm[ALL] = jnp.zeros_like(dnorm)

        @pl.when(index >= O_DONE)
        def _():
            dnorm[ALL] += sum(_dot_rhs_t(rights[QKV_AT + QKV * half + index - O_DONE], weights(role))
                              for role, half in torus.sides)

        @pl.when(index == PER_HALF - 1)
        def _():
            first_input(x_ref).wait()
            result = (lefts[GRAD].astype(jnp.float32) + _rms_back(x_in[ALL], dnorm[ALL])).astype(jnp.bfloat16)
            dx_ref[ALL] = result
            for block in SIX:
                rights[block] = result[:, COLS * block:COLS * block + COLS]

    def pair_copy(slot):
        return torus.remote(outgo.at[slot], peer.at[slot], pair_send.at[slot], pair_recv.at[slot], torus.sibling)

    def multiply(chunk):
        index = _rem(chunk, PER_HALF)
        slot = _rem(chunk, RING)
        quarter = third // RING
        for role, half in torus.sides[::-1]:
            left = jnp.where(index < DOWN_DONE, 3 * half + index // 6,
                             jnp.where(index < UP_DONE, NORM_MLP, jnp.where(index < O_DONE, GRAD, NORM_ATTN)))
            right = jnp.where(index < DOWN_DONE, _rem(index, 6),
                              jnp.where(index < UP_DONE, DH_AT + FF * half + index - DOWN_DONE,
                                        jnp.where(index < O_DONE, O_AT + 3 * half + index - UP_DONE, QKV_AT + QKV * half + index - O_DONE)))
            for z in range(RING):
                part = _dot_lhs_t(lefts[left, :, quarter * z:quarter * z + quarter], rights[right])
                if role == 0:
                    sum0[_rem(chunk, leads), z] = part.reshape(RING, RING, ROWS, COLS)
                else:
                    outgo[slot, z] = part.astype(jnp.bfloat16).reshape(RING, RING, ROWS, COLS)
        pair_copy(slot).start()

    def merge_pair(chunk):
        slot, lead = _rem(chunk, RING), _rem(chunk, leads)
        pair_copy(slot).wait_send()
        pair_copy(slot).wait_recv()
        for z in range(RING):
            for y in range(RING):
                sum0[lead, z, y] = sum0[lead, z, y] + peer[slot, z, y].astype(jnp.float32)

    def ring_copy(stage, part, slot, color, way):
        send, recv = (half_bufs, full_bufs)[part][stage]
        dim = ORDERS[color][stage]
        return torus.remote(send.at[slot, color, way], recv.at[slot, color, way],
                            ring_send.at[2 * stage + part, slot], ring_recv.at[2 * stage + part, slot],
                            {dim: near[way][dim]})

    def ring_wait(stage, part, slot):
        send, recv = (half_bufs, full_bufs)[part][stage]
        whole = torus.remote(send.at[slot], recv.at[slot], ring_send.at[2 * stage + part, slot],
                             ring_recv.at[2 * stage + part, slot], torus.sibling)
        whole.wait_send()
        whole.wait_recv()

    def source(stage, chunk, color, position, cols):
        lead = _rem(chunk, leads)
        if stage == 0:
            return sum0[(lead,) + _block(color, 0, position) + (_rows(color), cols)]
        return sums[stage][(lead, color) + _block(color, stage, position) + (EVERY, cols)]

    left_cols, right_cols, every = slice(0, COLS // 2), slice(COLS // 2, COLS), slice(0, COLS)

    def store_halves(stage, chunk):
        slot = _rem(chunk, RING)
        send = half_bufs[stage][0]
        for color in COLORS:
            far = torus.far[ORDERS[color][stage]]
            send[slot, color, 0] = source(stage, chunk, color, far, left_cols).astype(jnp.bfloat16)
            send[slot, color, 1] = source(stage, chunk, color, far, right_cols).astype(jnp.bfloat16)

    def store_fulls(stage, chunk):
        slot = _rem(chunk, RING)
        ring_wait(stage, 0, slot)
        recv = half_bufs[stage][1]
        send = full_bufs[stage][0]
        lead = (EVERY,) * (len(send.shape) - 4)
        for color in COLORS:
            dim = ORDERS[color][stage]
            for way, summed, plain in ((0, left_cols, right_cols), (1, right_cols, left_cols)):
                send[(slot, color, way) + lead + (summed,)] = (
                    source(stage, chunk, color, near[way][dim], summed)
                    + recv[slot, color, way].astype(jnp.float32)).astype(jnp.bfloat16)
                send[(slot, color, way) + lead + (plain,)] = source(
                    stage, chunk, color, near[way][dim], plain).astype(jnp.bfloat16)

    def close_stage(stage, chunk):
        slot = _rem(chunk, RING)
        ring_wait(stage, 1, slot)
        recv = full_bufs[stage][1]
        for color in COLORS:
            dim = ORDERS[color][stage]
            total = (source(stage, chunk, color, place[dim], every)
                     + recv[slot, color, 0].astype(jnp.float32)
                     + recv[slot, color, 1].astype(jnp.float32))
            if stage < 2:
                sums[stage + 1][_rem(chunk, leads), color] = total
            else:
                out[pair_of(chunk), _rows(color), columns(chunk)] = total

    def send_all(stage, part, chunk):
        for color in COLORS:
            for way in TWO:
                ring_copy(stage, part, _rem(chunk, RING), color, way).start()

    def open_first(chunk):
        merge_pair(chunk)
        store_halves(0, chunk)
        send_all(0, 0, chunk)

    def middle(stage, chunk):
        store_fulls(stage, chunk)
        send_all(stage, 1, chunk)

    def turn(stage, chunk):
        close_stage(stage, chunk)
        if stage < 2:
            store_halves(stage + 1, chunk)
            send_all(stage + 1, 0, chunk)

    base = 1
    steps = [(0, fetch), (base + 2 * LAG, functools.partial(middle, 0)), (base + LAG, open_first),
             (base + 3 * LAG, functools.partial(turn, 0)), (base + 4 * LAG, functools.partial(middle, 1)),
             (base + 5 * LAG, functools.partial(turn, 1)), (base + 6 * LAG, functools.partial(middle, 2)),
             (base + 7 * LAG, functools.partial(turn, 2)), (base, consume), (base, multiply)]
    torus.run(steps, n_chunks, n_chunks + base + 7 * LAG)

    half_rows = ROWS // 2
    for layer in range(n_layers):
        for part in range(5):
            cols = slice(FIFTH * part, FIFTH * part + FIFTH)
            both = out[layer, :, cols]
            low, high = both[:half_rows], both[half_rows:]
            rows_out[core, layer, :, cols] = jnp.where(core == 0, low, high)
            away[layer, :, cols] = jnp.where(core == 0, high, low)
    swap = torus.remote(away, rows_out.at[core], swap_sem.at[0], swap_sem.at[1], torus.sibling)
    down_out[ALL] = out[:, :, UP_END:]
    swap.start()
    swap.wait_send()
    swap.wait_recv()


def backward_stack(n_layers, g_loc, *saved):
    seq, width = g_loc.shape
    bf16, f32 = jnp.bfloat16, jnp.float32
    half = COLS // 2
    chunk = CUBE + (ROWS, COLS)
    leads = 7
    shape = jax.ShapeDtypeStruct
    hbm = pl.BlockSpec(memory_space=pl.ANY)
    vmem = pl.BlockSpec(memory_space=pltpu.VMEM)
    dma = pltpu.SemaphoreType.DMA
    half_rows = ROWS // 2
    scratch = [pltpu.VMEM((SLOTS,) + chunk, bf16), pltpu.VMEM((SLOTS,) + chunk, bf16),
               pltpu.VMEM((9, seq, width), bf16), pltpu.VMEM((56, seq, COLS), bf16),
               pltpu.VMEM((2, seq, width), f32), pltpu.VMEM((2, seq, width), f32), pltpu.VMEM((seq, width), f32),
               pltpu.VMEM((seq, 6 * COLS), bf16), pltpu.VMEM((seq, 2 * HEAD), bf16), pltpu.VMEM((seq, 2 * HEAD), bf16),
               pltpu.VMEM((seq, width), bf16), pltpu.VMEM((seq, width), bf16),
               pltpu.VMEM((2, seq, HEAD), f32), pltpu.VMEM((2, seq, HEAD), f32),
               pltpu.VMEM((RING,) + chunk, bf16), pltpu.VMEM((RING,) + chunk, bf16),
               pltpu.VMEM((n_layers, ROWS, PER_HALF * COLS), f32), pltpu.VMEM((n_layers, half_rows, UP_END), f32),
               pltpu.VMEM((leads,) + chunk, f32), pltpu.VMEM((leads, 3, RING, RING, TILE, COLS), f32),
               pltpu.VMEM((leads, 3, RING, TILE, COLS), f32)]
    for size in ((RING, RING), (RING,), ()):
        scratch += [pltpu.VMEM((RING, 3, 2) + size + (TILE, half), bf16)] * 2
        scratch += [pltpu.VMEM((RING, 3, 2) + size + (TILE, COLS), bf16)] * 2
    scratch += [dma((10,)), dma((SLOTS,)), dma((SLOTS,)), dma((SLOTS,)), dma((RING,)), dma((RING,)), dma((6, RING)), dma((6, RING)), dma((2,)),
                pltpu.SemaphoreType.REGULAR((7,))]
    return pl.pallas_call(
        functools.partial(backward_kernel, n_layers),
        name="backward_stack",
        out_shape=(shape((2, n_layers, half_rows, UP_END), f32),
                   shape((n_layers, ROWS, (PER_HALF - UP_BLOCKS) * COLS), f32), shape((seq, width), bf16)),
        in_specs=[vmem] + [hbm] * len(saved),
        out_specs=(vmem,) * 3,
        scratch_shapes=scratch,
        compiler_params=pltpu.CompilerParams(collective_id=0, has_side_effects=True,
                                             vmem_limit_bytes=VMEM_LIMIT),
    )(g_loc, *saved)


def solution(mesh):
    mesh4 = Mesh(mesh.devices.reshape(CUBE + (2,)), ALL_AXES)
    row_spec = P(ALL_AXES)
    weight_spec = P(None, ALL_AXES)

    def body(x_in, w_q, w_k, w_v, w_o, w_up, w_down, grad_out):
        pairs, rows, heads, head_dim = w_q.shape
        group = heads // 2 * head_dim
        half_w = 2 * group + 2 * head_dim
        ff_rows = w_down.shape[1]
        ff, width = w_up.shape[2], w_down.shape[2]
        chips = ff // ff_rows // 2
        ff_pad = 3 * ROWS
        half_f = chips * ff_pad
        x_loc, g_loc = x_in[0], grad_out[0]

        attn_sh = jnp.concatenate([w_q.reshape(pairs, rows, 2, group), w_k.reshape(pairs, rows, 2, head_dim),
                                   w_v.reshape(pairs, rows, 2, head_dim), w_o.reshape(pairs, rows, 2, group)], axis=3)
        up_sh = jnp.pad(w_up.reshape(pairs, rows, chips, 2, ff_rows),
                        ((0, 0), (0, 0), (0, 0), (0, 0), (0, ff_pad - ff_rows)))
        up_sh = up_sh.reshape(pairs, rows, chips, 2, 3, ROWS).transpose(0, 1, 3, 4, 2, 5)
        up_sh = up_sh.reshape(pairs, rows, 2, half_f)
        rows_sh = jnp.concatenate([attn_sh, up_sh], axis=3).transpose(2, 0, 1, 3)
        down_sh = jnp.pad(w_down, ((0, 0), (0, ff_pad - ff_rows), (0, 0)))
        down_sh = jnp.concatenate([down_sh[:, ROWS * part:ROWS * part + ROWS] for part in COLORS], axis=2)

        acts, *saved = forward_stack(x_loc, rows_sh, down_sh)
        row_grad, down_grad, grad_x = backward_stack(pairs, g_loc, x_loc, acts, *saved)

        down_grad = down_grad.reshape(pairs, ROWS, 3, width).transpose(0, 2, 1, 3)
        down_grad = down_grad.reshape(pairs, ff_pad, width)[:, :ff_rows]
        row_grad = row_grad.transpose(1, 2, 0, 3)
        up_grad = row_grad[:, :, :, half_w:].reshape(pairs, rows, 2, 3, chips, ROWS).transpose(0, 1, 4, 2, 3, 5)
        up_grad = up_grad.reshape(pairs, rows, chips * 2, ff_pad)[:, :, :, :ff_rows].reshape(pairs, rows, ff)
        cuts = [group, group + head_dim, group + 2 * head_dim]
        d_q, d_k, d_v, d_o = jnp.split(row_grad[:, :, :, :half_w], cuts, axis=3)
        return (acts[2 * pairs - 1][None], grad_x[None],
                d_q.reshape(w_q.shape), d_k.reshape(w_k.shape), d_v.reshape(w_v.shape), d_o.reshape(w_o.shape),
                up_grad, down_grad)

    return jax.shard_map(body, mesh=mesh4, in_specs=(row_spec,) + (weight_spec,) * 6 + (row_spec,),
                         out_specs=(row_spec, row_spec) + (weight_spec,) * 6, check_vma=False)
```

time: 3830 us -> 597 us (0.16)
  waiting for transfers between devices: 2210 us -> 0 us
  blocking collectives: 1100 us -> 0 us
  Pallas kernels: 0 us -> 546 us
  matrix products: 307 us -> 0 us
  local copies, waits for them, and re-layouts: 150 us -> 49 us
    all_gather x20 -> x0, waiting for transfers between devices: 1280 us -> none  [the longest x4 554 us: body(): up_full = lax.all_gather(up_copy, 'sub', axis=0, tiled=True)]
    unnamed x32 -> x0, waiting for transfers between devices: 927 us -> none
    unnamed x2 -> x0, blocking collectives: 821 us -> none
    pallas_call x0 -> x2, Pallas kernels: none -> 546 us  [the longest x1 278 us: backward_stack(): pl.pallas_call(functools.partial(backward_kernel, n_layers), name='backwa...]
    dot_general x54 -> x0, matrix products: 307 us -> none  [mixed(): return jnp.einsum(form, left, right, preferred_element_type=jnp.float32)]
    all_gather x8 -> x0, blocking collectives: 283 us -> none  [gather_all(): return lax.all_gather(shard, AXES, axis=0, tiled=True)]
    all_gather x16 -> x0, local copies, waits for them, and re-layouts: 67 us -> none  [the longest x8 42.9 us: gather_all(): return lax.all_gather(shard, AXES, axis=0, tiled=True)]
  transfers between devices with their start and end apart: 30 -> 0, of which waited for: 17 -> 0; matrix products, arithmetic and copies ran while one was open for 31% -> 0% of each run, Pallas kernels for 0% -> 0%
where the time goes in v4:
time: 597 us; the launch traced here: 596 us
  Pallas kernels  546 us (91%)
  local copies, waits for them, and re-layouts  49 us (8%)
    pallas_call x1, Pallas kernels, backward_stack(): pl.pallas_call(functools.partial(backward_kernel, n_layers), name='backwa...  278 us
    pallas_call x1, Pallas kernels, forward_stack(): pl.pallas_call(functools.partial(forward_kernel, n_layers), name='forward...  267 us

profile of v4, /device:TPU:1, one launch (start us, length us, event | category | flops | bytes accessed | tf_op | source)
XLA Modules:
  0.0 596.4 jit_solution(1165807850212186373)
XLA Ops:
  0.6 0.9 copy.44
  1.6 0.9 copy.45
  2.5 0.0 copy-start.4
  2.5 0.0 copy-start.5
  2.6 0.0 copy-start.3
  2.6 1.1 copy.53
  3.7 0.8 pad_maximum_fusion.down_ref
  4.5 0.7 copy_dynamic-update-slice_fusion.1
  5.2 0.0 copy-done.4
  5.2 0.6 copy_dynamic-update-slice_fusion.3
  5.8 0.0 copy-done.5
  5.8 0.6 copy_dynamic-update-slice_fusion.2
  6.4 0.7 copy_dynamic-update-slice_fusion
  7.0 0.0 copy-done.3
  7.0 2.7 reshape.54
  9.8 0.7 copy.70
  10.5 0.2 pad.8.clone
  10.7 1.2 copy.67
  11.9 4.0 reshape.64
  15.9 0.9 constant_dynamic-update-slice_fusion
  16.8 267.5 %forward_stack.1 = (bf16[4,192,1536]{2,1,0:T(8,128)(2,1)}, bf16[2,4,4,4,24,11008]{5,4,3,2,1,0:T(8,128)(2,1)}, f32[2,3,2,192,1536]{4,3,2,1,0:T(8,128)}, bf16[2,6,...) custom-call(bf16[192,1536]{1,0:T(8,128)(2,1)} %bitcast.26, ...), custom_call_target="tpu_custom_call" | custom-call | tf_op jit(solution)/shard_map/forward_stack/pallas_call | solution.py:363
  284.3 278.3 %backward_stack.1 = (f32[2,2,12,6400]{3,2,1,0:T(8,128)}, f32[2,24,4608]{2,1,0:T(8,128)}, bf16[192,1536]{1,0:T(8,128)(2,1)}) custom-call(bf16[192,1536]{1,0:T(8,128)(2,1)} %bitcast.31, bf16[192,1536]{1,0:T(8,128)(2,1)} %bitcast.27, bf16[4,192,1536]{2,1,0:T(8,128)(2,1)} %get-tuple-element.20.refs_2_, ...), custom_call_target="tpu_custom_call" | custom-call | tf_op jit(solution)/shard_map/backward_stack/pallas_call | solution.py:734
  562.6 0.0 copy-start
  562.6 2.0 slice.31
  564.7 0.8 fusion.1
  565.4 0.6 copy.64
  566.1 0.6 copy.63
  566.7 1.0 fusion
  567.7 0.0 copy-done
  567.8 0.1 slice.37
  567.8 0.0 copy-start.1
  567.8 0.7 copy.58
  568.5 0.1 copy.57
  568.7 0.1 reshape.58
  568.8 0.8 copy.65
  569.6 0.1 copy.56
  569.7 0.1 reshape.57
  569.8 0.8 copy.62
  570.6 0.6 reshape.62
  571.2 0.3 copy.61
  571.5 1.6 copy.66
  573.1 5.1 reshape.59
  578.2 8.5 %copy.59 = f32[2,12,64,2,3,24]{5,4,3,2,1,0:T(4,128)} copy(f32[2,12,64,2,3,24]{5,2,4,3,1,0:T(8,128)} %bitcast.21) | data formatting | bytes 1769472 | tf_op jit(solution)/shard_map/transpose | solution.py:779
  586.7 6.1 %reshape.60 = f32[2,12,128,72]{3,2,1,0:T(8,128)S(1)} reshape(f32[2,12,64,2,3,24]{5,4,3,2,1,0:T(4,128)} %copy.59) | data formatting | bytes 1769472 | tf_op jit(solution)/shard_map/reshape | solution.py:780
  592.8 1.2 reshape.65
  594.0 1.6 copy.68
  595.6 0.0 copy-done.2
  595.6 0.8 copy.80
  (5 shorter events, 0.1 us)
Async XLA Ops:
  2.5 2.7 copy-start.4
  2.5 3.3 copy-start.5
  2.6 4.5 copy-start.3
  562.6 5.1 copy-start
  567.8 2.8 copy-start.1
  594.0 1.6 copy-start.2

commit v5 on v4

--- a/solution.py
+++ b/solution.py
@@ -1,4 +1,5 @@
 import functools
+import math
 
 import jax
 import jax.numpy as jnp
@@ -133,7 +134,7 @@
         lax.fori_loop(0, n_ticks, tick, 0)
 
 
-def forward_kernel(n_layers, x_ref, rows_ref, down_ref, acts, w_out, hid_out, gelu_out, norm_out, q_out, k_out, v_out,
+def forward_kernel(n_layers, x_ref, rows_ref, down_ref, y_ref, acts, w_out, hid_out, gelu_out, norm_out, q_out, k_out, v_out,
                    o_out, wbuf, peer, shard, twin, state, normed, q_buf, k_buf, v_buf, o_buf, gelu_buf, hid_buf, acc,
                    ring_send, ring_recv, pair_send, pair_recv, keep_sem, save_sem, hid_sem, twin_sem, credit):
     torus = Torus(credit)
@@ -141,7 +142,7 @@
     slots = wbuf.shape[0]
     n_chunks = n_layers * PER_HALF
     ready = 6 * LAG
-    last_lag = ready + 2
+    last_lag = ready + 1
     seq = x_ref.shape[0]
     third = 64 * ROWS
     torus.meet()
@@ -340,7 +341,14 @@
         def _():
             result = (state[ALL].astype(jnp.float32) + acc[ALL]).astype(jnp.bfloat16)
             state[ALL] = result
-            acts[2 * layer + 1] = result
+
+            @pl.when(layer < n_layers - 1)
+            def _():
+                acts[2 * layer + 1] = result
+
+            @pl.when(layer == n_layers - 1)
+            def _():
+                y_ref[ALL] = result
             for copy in save_copies(layer, ["n1", "q", "k", "v", "o"] + gelu_names):
                 copy.wait()
 
@@ -363,14 +371,14 @@
     return pl.pallas_call(
         functools.partial(forward_kernel, n_layers),
         name="forward_stack",
-        out_shape=(shape((2 * n_layers, seq, width), bf16),
+        out_shape=(shape((seq, width), bf16), shape((2 * n_layers - 1, seq, width), bf16),
                    shape((n_layers, 4, 4, 4, ROWS, PER_HALF * COLS), bf16),
                    shape((n_layers, 3, 2, seq, width), f32), shape((n_layers, 6, seq, width), bf16),
                    shape((n_layers, 2, seq, width), bf16), shape((n_layers, seq, width), bf16),
                    shape((n_layers, seq, 2 * HEAD), bf16), shape((n_layers, seq, 2 * HEAD), bf16),
                    shape((n_layers, 6, seq, COLS), bf16)),
         in_specs=[vmem] * 3,
-        out_specs=(vmem,) + (hbm,) * 8,
+        out_specs=(vmem,) * 2 + (hbm,) * 8,
         scratch_shapes=[
             pltpu.VMEM((slots,) + chunk, bf16), pltpu.VMEM((RING,) + chunk, bf16),
             pltpu.VMEM((n_layers, ROWS, PER_HALF * COLS), bf16), pltpu.VMEM(rows.shape[1:], bf16),
@@ -435,6 +443,7 @@
     start(n_layers - 1, ["a"])
     for block in SIX:
         rights[block] = g_ref[:, COLS * block:COLS * block + COLS]
+    finish(n_layers - 1, ["a"])
 
     def own_copy(chunk):
         slot = _rem(chunk, SLOTS)
@@ -475,26 +484,20 @@
             @pl.when(pair > 0)
             def _():
                 first_input(acts.at[2 * pair - 1]).start()
-            finish(pair, ["a"])
 
         for part in (1, 2):
             @pl.when(index == 6 * part)
             def _(part=part):
                 start(pair, [f"h{part}"])
 
+        @pl.when((index < DOWN_DONE) & (_rem(index, 6) == 0))
+        def _():
+            dact[ALL] = jnp.zeros_like(dact)
+
         @pl.when(index < DOWN_DONE)
         def _():
-            block = _rem(index, 6)
             for role, half in torus.sides:
-                product = _dot_rhs_t(rights[block], weights(role))
-
-                @pl.when(block == 0)
-                def _(product=product, half=half):
-                    dact[half] = product
-
-                @pl.when(block > 0)
-                def _(product=product, half=half):
-                    dact[half] += product
+                dact[half] += _dot_rhs_t(rights[_rem(index, 6)], weights(role))
 
         @pl.when((index < DOWN_DONE) & (_rem(index, 6) == 5))
         def _():
@@ -508,9 +511,12 @@
                         0.7978845608028654 * (1.0 + 0.134145 * (hidden * hidden)))
                     rights[DH_AT + FF * half + index - 5 + block] = (dact[half, :, cols] * slope).astype(jnp.bfloat16)
 
+        @pl.when(index == DOWN_DONE - 1)
+        def _():
+            finish(pair, ["n_mlp"])
+
         @pl.when(index == DOWN_DONE)
         def _():
-            finish(pair, ["n_mlp"])
             dnorm[ALL] = jnp.zeros_like(dnorm)
 
             @pl.when(pair > 0)
@@ -524,12 +530,12 @@
 
         @pl.when(index == UP_DONE - 1)
         def _():
-            finish(pair, ["x_mid"])
+            finish(pair, ["x_mid", "o"])
             lefts[GRAD] = (total_grad() + _rms_back(x_mid[ALL], dnorm[ALL])).astype(jnp.bfloat16)
 
         @pl.when(index == UP_DONE)
         def _():
-            finish(pair, ["o", "q", "k", "v"])
+            finish(pair, ["q", "k", "v"])
             dk_acc[ALL] = jnp.zeros_like(dk_acc)
             dv_acc[ALL] = jnp.zeros_like(dv_acc)
 
@@ -554,12 +560,12 @@
 
         @pl.when(index == O_DONE - 1)
         def _():
+            finish(pair, ["n_attn"])
             for half in TWO:
                 rights[QKV_AT + QKV * half + QKV - 1] = jnp.concatenate([dk_acc[half], dv_acc[half]], axis=1).astype(jnp.bfloat16)
 
         @pl.when(index == O_DONE)
         def _():
-            finish(pair, ["n_attn"])
             dnorm[ALL] = jnp.zeros_like(dnorm)
 
         @pl.when(index >= O_DONE)
@@ -570,6 +576,10 @@
         @pl.when(index == PER_HALF - 1)
         def _():
             first_input(x_ref).wait()
+
+            @pl.when(pair > 0)
+            def _():
+                finish(pair - 1, ["a"])
             result = (lefts[GRAD].astype(jnp.float32) + _rms_back(x_in[ALL], dnorm[ALL])).astype(jnp.bfloat16)
             dx_ref[ALL] = result
             for block in SIX:
@@ -683,11 +693,11 @@
             store_halves(stage + 1, chunk)
             send_all(stage + 1, 0, chunk)
 
-    base = 1
+    base = 0
     steps = [(0, fetch), (base + 2 * LAG, functools.partial(middle, 0)), (base + LAG, open_first),
              (base + 3 * LAG, functools.partial(turn, 0)), (base + 4 * LAG, functools.partial(middle, 1)),
              (base + 5 * LAG, functools.partial(turn, 1)), (base + 6 * LAG, functools.partial(middle, 2)),
-             (base + 7 * LAG, functools.partial(turn, 2)), (base, consume), (base, multiply)]
+             (base + 7 * LAG, functools.partial(turn, 2)), (1, consume), (0, multiply)]
     torus.run(steps, n_chunks, n_chunks + base + 7 * LAG)
 
     half_rows = ROWS // 2
@@ -744,45 +754,136 @@
     )(g_loc, *saved)
 
 
+LANES = 128
+
+
+def _pieces(moves, size):
+    tiles = [[] for _ in range(size // LANES)]
+    for target, source, length in moves:
+        while length:
+            step = min(length, LANES - target % LANES, LANES - source % LANES)
+            tiles[target // LANES].append((target % LANES, source // LANES, (target - source) % LANES))
+            target, source, length = target + step, source + step, length - step
+    return [sorted(tile) for tile in tiles]
+
+
+def _gather_tile(load, tile, lane):
+    total = None
+    for first, source, shift in tile:
+        value = load(source)
+        if shift:
+            value = pltpu.roll(value, shift, axis=value.ndim - 1)
+        total = value if total is None else jnp.where(lane >= first, value, total)
+    return total
+
+
+def pack_kernel(blocks, q_ref, k_ref, v_ref, o_ref, up_ref, down_ref, rows_out, down_out):
+    layers, rows = up_ref.shape[0], up_ref.shape[1]
+    group = q_ref.shape[-1] // 2
+    for half in TWO:
+        first = 0
+        for ref, size in ((q_ref, group), (k_ref, HEAD), (v_ref, HEAD), (o_ref, group)):
+            rows_out[half, :, :, first:first + size] = ref[:, :, size * half:size * half + size]
+            first += size
+    lane = lax.broadcasted_iota(jnp.int32, (layers, rows, LANES), 2)
+    chips, block = blocks
+    moves = []
+    for half in TWO:
+        for part in COLORS:
+            for chip in range(chips):
+                used = min(ROWS, block - ROWS * part)
+                target = chips * ROWS * (3 * half + part) + ROWS * chip
+                moves.append((target, block * (2 * chip + half) + ROWS * part, used))
+    half_f = 3 * chips * ROWS
+    for index, tile in enumerate(_pieces(moves, 2 * half_f)):
+        value = _gather_tile(lambda source: up_ref[:, :, LANES * source:LANES * source + LANES].astype(jnp.float32),
+                             tile, lane)
+        last = 3 * ROWS - block
+        position = lane + LANES * index % ROWS
+        if LANES * index % half_f >= 2 * chips * ROWS:
+            value = jnp.where(lax.rem(position, ROWS) < ROWS - last, value, 0.0)
+        half, at = divmod(LANES * index, half_f)
+        rows_out[half, :, :, ATTN * COLS + at:ATTN * COLS + at + LANES] = value.astype(jnp.bfloat16)
+    width = down_ref.shape[-1]
+    for part in COLORS:
+        used = min(ROWS, block - ROWS * part)
+        value = down_ref[:, ROWS * part:ROWS * part + used, :].astype(jnp.float32)
+        if used < ROWS:
+            value = jnp.concatenate([value, jnp.zeros((layers, ROWS - used, width), jnp.float32)], axis=1)
+        down_out[:, :, width * part:width * part + width] = value.astype(jnp.bfloat16)
+
+
+def pack_weights(w_q, w_k, w_v, w_o, w_up, w_down, chips):
+    layers, rows = w_up.shape[:2]
+    block, width = w_down.shape[1:]
+    vmem = pl.BlockSpec(memory_space=pltpu.VMEM)
+    shape = jax.ShapeDtypeStruct
+    return pl.pallas_call(
+        functools.partial(pack_kernel, (chips, block)), name="pack_weights",
+        out_shape=(shape((2, layers, rows, UP_END), jnp.bfloat16), shape((layers, ROWS, 3 * width), jnp.bfloat16)),
+        in_specs=[vmem] * 6, out_specs=(vmem,) * 2,
+        compiler_params=pltpu.CompilerParams(vmem_limit_bytes=VMEM_LIMIT),
+    )(*[weight.reshape(layers, rows, -1) for weight in (w_q, w_k, w_v, w_o, w_up)], w_down)
+
+
+def unpack_kernel(blocks, rows_ref, down_ref, q_out, k_out, v_out, o_out, up_out, down_out):
+    layers, rows = up_out.shape[0], up_out.shape[1]
+    group = q_out.shape[-1] // 2
+    for half in TWO:
+        first = 0
+        for ref, size in ((q_out, group), (k_out, HEAD), (v_out, HEAD), (o_out, group)):
+            ref[:, :, size * half:size * half + size] = rows_ref[half, :, :, first:first + size]
+            first += size
+    lane = lax.broadcasted_iota(jnp.int32, (layers, rows, LANES), 2)
+    chips, block = blocks
+    moves = []
+    for half in TWO:
+        for part in COLORS:
+            for chip in range(chips):
+                used = min(ROWS, block - ROWS * part)
+                source = chips * ROWS * (3 * half + part) + ROWS * chip
+                moves.append((block * (2 * chip + half) + ROWS * part, source, used))
+    half_f = 3 * chips * ROWS
+
+    def load(source):
+        half, at = divmod(LANES * source, half_f)
+        return rows_ref[half, :, :, ATTN * COLS + at:ATTN * COLS + at + LANES]
+
+    for index, tile in enumerate(_pieces(moves, 2 * chips * block)):
+        up_out[:, :, LANES * index:LANES * index + LANES] = _gather_tile(load, tile, lane)
+    width = down_out.shape[-1]
+    for part in COLORS:
+        used = min(ROWS, block - ROWS * part)
+        down_out[:, ROWS * part:ROWS * part + used, :] = down_ref[:, :used, width * part:width * part + width]
+
+
+def unpack_grads(row_grad, down_grad, shapes, chips):
+    layers, rows = row_grad.shape[1:3]
+    block, width = shapes[5][1:]
+    vmem = pl.BlockSpec(memory_space=pltpu.VMEM)
+    shape = jax.ShapeDtypeStruct
+    flat = [shape((layers, rows, math.prod(full[2:])), jnp.float32) for full in shapes[:5]]
+    outs = pl.pallas_call(
+        functools.partial(unpack_kernel, (chips, block)), name="unpack_grads",
+        out_shape=tuple(flat) + (shape((layers, block, width), jnp.float32),),
+        in_specs=[vmem] * 2, out_specs=(vmem,) * 6,
+        compiler_params=pltpu.CompilerParams(vmem_limit_bytes=VMEM_LIMIT),
+    )(row_grad, down_grad)
+    return tuple(out.reshape(full) for out, full in zip(outs, shapes))
+
+
 def solution(mesh):
     mesh4 = Mesh(mesh.devices.reshape(CUBE + (2,)), ALL_AXES)
     row_spec = P(ALL_AXES)
     weight_spec = P(None, ALL_AXES)
 
     def body(x_in, w_q, w_k, w_v, w_o, w_up, w_down, grad_out):
-        pairs, rows, heads, head_dim = w_q.shape
-        group = heads // 2 * head_dim
-        half_w = 2 * group + 2 * head_dim
-        ff_rows = w_down.shape[1]
-        ff, width = w_up.shape[2], w_down.shape[2]
-        chips = ff // ff_rows // 2
-        ff_pad = 3 * ROWS
-        half_f = chips * ff_pad
-        x_loc, g_loc = x_in[0], grad_out[0]
-
-        attn_sh = jnp.concatenate([w_q.reshape(pairs, rows, 2, group), w_k.reshape(pairs, rows, 2, head_dim),
-                                   w_v.reshape(pairs, rows, 2, head_dim), w_o.reshape(pairs, rows, 2, group)], axis=3)
-        up_sh = jnp.pad(w_up.reshape(pairs, rows, chips, 2, ff_rows),
-                        ((0, 0), (0, 0), (0, 0), (0, 0), (0, ff_pad - ff_rows)))
-        up_sh = up_sh.reshape(pairs, rows, chips, 2, 3, ROWS).transpose(0, 1, 3, 4, 2, 5)
-        up_sh = up_sh.reshape(pairs, rows, 2, half_f)
-        rows_sh = jnp.concatenate([attn_sh, up_sh], axis=3).transpose(2, 0, 1, 3)
-        down_sh = jnp.pad(w_down, ((0, 0), (0, ff_pad - ff_rows), (0, 0)))
-        down_sh = jnp.concatenate([down_sh[:, ROWS * part:ROWS * part + ROWS] for part in COLORS], axis=2)
-
-        acts, *saved = forward_stack(x_loc, rows_sh, down_sh)
-        row_grad, down_grad, grad_x = backward_stack(pairs, g_loc, x_loc, acts, *saved)
-
-        down_grad = down_grad.reshape(pairs, ROWS, 3, width).transpose(0, 2, 1, 3)
-        down_grad = down_grad.reshape(pairs, ff_pad, width)[:, :ff_rows]
-        row_grad = row_grad.transpose(1, 2, 0, 3)
-        up_grad = row_grad[:, :, :, half_w:].reshape(pairs, rows, 2, 3, chips, ROWS).transpose(0, 1, 4, 2, 3, 5)
-        up_grad = up_grad.reshape(pairs, rows, chips * 2, ff_pad)[:, :, :, :ff_rows].reshape(pairs, rows, ff)
-        cuts = [group, group + head_dim, group + 2 * head_dim]
-        d_q, d_k, d_v, d_o = jnp.split(row_grad[:, :, :, :half_w], cuts, axis=3)
-        return (acts[2 * pairs - 1][None], grad_x[None],
-                d_q.reshape(w_q.shape), d_k.reshape(w_k.shape), d_v.reshape(w_v.shape), d_o.reshape(w_o.shape),
-                up_grad, down_grad)
+        weights = (w_q, w_k, w_v, w_o, w_up, w_down)
+        chips = w_up.shape[2] // w_down.shape[1] // 2
+        rows, down = pack_weights(*weights, chips)
+        y_loc, acts, *saved = forward_stack(x_in[0], rows, down)
+        row_grad, down_grad, grad_x = backward_stack(w_q.shape[0], grad_out[0], x_in[0], acts, *saved)
+        return (y_loc[None], grad_x[None]) + unpack_grads(row_grad, down_grad, [w.shape for w in weights], chips)
 
     return jax.shard_map(body, mesh=mesh4, in_specs=(row_spec,) + (weight_spec,) * 6 + (row_spec,),
                          out_specs=(row_spec, row_spec) + (weight_spec,) * 6, check_vma=False)

time: 597 us -> 573 us (0.960)
  local copies, waits for them, and re-layouts: 49 us -> 20.6 us
    reshape x12 -> x8, local copies, waits for them, and re-layouts: 22.9 us -> 10.5 us  [the longest x4 5.72 us: pack_weights(): weight.reshape(layers, rows, -1)]
    transpose x2 -> x0, local copies, waits for them, and re-layouts: 8.76 us -> none  [the longest x1 8.49 us: body(): row_grad[:, :, :, half_w:].reshape(pairs, rows, 2, 3, chips, ROWS)]
    pallas_call x0 -> x2, Pallas kernels: none -> 8.61 us  [the longest x1 5.17 us: unpack_grads(): pl.pallas_call(functools.partial(unpack_kernel, (chips, block)), name='un...]
where the time goes in v5:
time: 573 us; the launch traced here: 572 us
  Pallas kernels  551 us (96%)
  local copies, waits for them, and re-layouts  20.6 us (4%)
    pallas_call x1, Pallas kernels, backward_stack(): pl.pallas_call(functools.partial(backward_kernel, n_layers), name='backwa...  275 us
    pallas_call x1, Pallas kernels, forward_stack(): pl.pallas_call(functools.partial(forward_kernel, n_layers), name='forward...  267 us

profile of v5, /device:TPU:1, one launch (start us, length us, event | category | flops | bytes accessed | tf_op | source)
XLA Modules:
  0.0 572.0 jit_solution(13426318595465678330)
XLA Ops:
  0.6 1.3 reshape.48.k_ref
  2.0 1.3 reshape.49.v_ref
  3.3 1.5 copy.28.q_ref
  4.8 1.5 copy.31.o_ref
  6.4 1.8 copy.33.down_ref
  8.2 1.9 copy.32.up_ref
  10.0 3.4 pack_weights.1
  13.5 266.9 %forward_stack.1 = (bf16[192,1536]{1,0:T(8,128)(2,1)}, bf16[3,192,1536]{2,1,0:T(8,128)(2,1)}, bf16[2,4,4,4,24,11008]{5,4,3,2,1,0:T(8,128)(2,1)}, f32[2,3,2,192,1...) custom-call(bf16[192,1536]{1,0:T(8,128)(2,1)} %bitcast.6, ...), custom_call_target="tpu_custom_call" | custom-call | tf_op jit(solution)/shard_map/forward_stack/pallas_call | solution.py:371
  280.4 275.2 %backward_stack.1 = (f32[2,2,12,6400]{3,2,1,0:T(8,128)}, f32[2,24,4608]{2,1,0:T(8,128)}, bf16[192,1536]{1,0:T(8,128)(2,1)}) custom-call(bf16[192,1536]{1,0:T(8,128)(2,1)} %bitcast.10, bf16[192,1536]{1,0:T(8,128)(2,1)} %bitcast.7, bf16[3,192,1536]{2,1,0:T(8,128)(2,1)} %get-tuple-element.32.refs_2_, ...), custom_call_target="tpu_custom_call" | custom-call | tf_op jit(solution)/shard_map/backward_stack/pallas_call | solution.py:744
  555.6 5.2 unpack_grads.1
  560.8 0.0 copy-start
  560.8 0.0 copy-start.1
  560.8 1.1 reshape.50
  561.9 0.8 copy.38
  562.7 1.4 reshape.51
  564.0 1.4 reshape.52
  565.4 1.0 reshape.53
  566.4 0.8 copy.41
  567.2 0.0 copy-done
  567.2 0.0 copy-start.2
  567.2 1.6 copy.42
  568.7 0.0 copy-done.1
  568.7 0.0 copy-start.3
  568.7 1.6 copy.43
  570.3 0.0 copy-done.2
  570.3 0.8 copy.54
  571.1 0.0 copy-done.3
  571.1 0.8 copy.55
Async XLA Ops:
  560.8 6.4 %copy-start = (f32[2,12,8960]{2,1,0:T(8,128)S(1)}, f32[2,12,8960]{2,1,0:T(8,128)}, u32[]{:S(2)}) copy-start(f32[2,12,8960]{2,1,0:T(8,128)} %get-tuple-element.64) | copy-start | bytes 2580484
  560.8 8.0 %copy-start.1 = (f32[2,70,1536]{2,1,0:T(8,128)S(1)}, f32[2,70,1536]{2,1,0:T(8,128)}, u32[]{:S(2)}) copy-start(f32[2,70,1536]{2,1,0:T(8,128)} %get-tuple-element.65) | copy-start | bytes 2580484
  567.2 3.1 copy-start.2
  568.7 2.4 copy-start.3

commit v6 on v5

--- a/solution.py
+++ b/solution.py
@@ -1,5 +1,4 @@
 import functools
-import math
 
 import jax
 import jax.numpy as jnp
@@ -145,21 +144,25 @@
     last_lag = ready + 1
     seq = x_ref.shape[0]
     third = 64 * ROWS
+    state[ALL] = x_ref[ALL]
     torus.meet()
     swap = torus.remote(rows_ref.at[1 - core], twin, twin_sem.at[0], twin_sem.at[1], torus.sibling)
     swap.start()
-    state[ALL] = x_ref[ALL]
     swap.wait_send()
     swap.wait_recv()
-    for layer in range(n_layers):
-        shard[layer, :, UP_END:] = down_ref[layer]
-        for part in range(5):
-            cols = slice(FIFTH * part, FIFTH * part + FIFTH)
-            mine = rows_ref[core, layer, :, cols].astype(jnp.float32)
-            other = twin[layer, :, cols].astype(jnp.float32)
-            first = core == 0
+
+    def assemble(chunk):
+        @pl.when(chunk < 5 * n_layers)
+        def _():
+            layer, part = chunk // 5, _rem(chunk, 5)
+            cols = _at(part * FIFTH, FIFTH)
+            mine, other = [ref[layer, :, cols].astype(jnp.float32) for ref in (rows_ref.at[core], twin)]
             shard[layer, :, cols] = jnp.concatenate(
-                [jnp.where(first, mine, other), jnp.where(first, other, mine)], axis=0).astype(jnp.bfloat16)
+                [jnp.where(core == 0, mine, other), jnp.where(core == 0, other, mine)], axis=0).astype(jnp.bfloat16)
+
+            @pl.when(part == 4)
+            def _():
+                shard[layer, :, UP_END:] = down_ref[layer]
 
     def columns(chunk):
         return _at(_rem(chunk, PER_HALF) * COLS, COLS)
@@ -354,7 +357,7 @@
 
         keep_copy(chunk).wait()
 
-    steps = [(0, enter)] + [((part + 1) * LAG, functools.partial(pass_on, part)) for part in range(5)]
+    steps = [(0, assemble), (0, enter)] + [((part + 1) * LAG, functools.partial(pass_on, part)) for part in range(5)]
     torus.run(steps + [(ready, exchange), (last_lag, compute)], n_chunks, n_chunks + last_lag)
 
 
@@ -439,10 +442,10 @@
     def first_input(ref):
         return pltpu.make_async_copy(ref, x_in, load_sem.at[9])
 
-    torus.meet()
     start(n_layers - 1, ["a"])
     for block in SIX:
         rights[block] = g_ref[:, COLS * block:COLS * block + COLS]
+    torus.meet()
     finish(n_layers - 1, ["a"])
 
     def own_copy(chunk):
@@ -757,6 +760,18 @@
 LANES = 128
 
 
+def _moves(chips, block, packed_first):
+    moves = []
+    for half in TWO:
+        for part in COLORS:
+            for chip in range(chips):
+                packed = chips * ROWS * (3 * half + part) + ROWS * chip
+                plain = block * (2 * chip + half) + ROWS * part
+                pair = (packed, plain) if packed_first else (plain, packed)
+                moves.append(pair + (min(ROWS, block - ROWS * part),))
+    return moves
+
+
 def _pieces(moves, size):
     tiles = [[] for _ in range(size // LANES)]
     for target, source, length in moves:
@@ -777,99 +792,110 @@
     return total
 
 
-def pack_kernel(blocks, q_ref, k_ref, v_ref, o_ref, up_ref, down_ref, rows_out, down_out):
-    layers, rows = up_ref.shape[0], up_ref.shape[1]
-    group = q_ref.shape[-1] // 2
+def _span(index, size):
+    return slice(size * index, size * index + size)
+
+
+def pack_kernel(chips, q_ref, k_ref, v_ref, o_ref, up_ref, down_ref, rows_out, down_out, wide):
+    rows, layers, cols = up_ref.shape
+    block, _, width = down_ref.shape
+    heads = q_ref.shape[1] // 2
     for half in TWO:
-        first = 0
-        for ref, size in ((q_ref, group), (k_ref, HEAD), (v_ref, HEAD), (o_ref, group)):
-            rows_out[half, :, :, first:first + size] = ref[:, :, size * half:size * half + size]
-            first += size
+        for layer in range(layers):
+            for at, ref in ((0, q_ref), (heads + 2, o_ref)):
+                for head in range(heads):
+                    rows_out[half, layer, :, _span(at + head, LANES)] = ref[
+                        :, heads * half + head].astype(jnp.float32)[:, layer].astype(jnp.bfloat16)
+            for at, ref in ((heads, k_ref), (heads + 1, v_ref)):
+                rows_out[half, layer, :, _span(at, LANES)] = ref[layer].astype(
+                    jnp.float32)[:, half].astype(jnp.bfloat16)
+    for tile in range(cols // LANES):
+        both = up_ref[:, :, _span(tile, LANES)].astype(jnp.float32)
+        for layer in range(layers):
+            wide[layer, :, _span(tile, LANES)] = both[:, layer]
     lane = lax.broadcasted_iota(jnp.int32, (layers, rows, LANES), 2)
-    chips, block = blocks
-    moves = []
-    for half in TWO:
-        for part in COLORS:
-            for chip in range(chips):
-                used = min(ROWS, block - ROWS * part)
-                target = chips * ROWS * (3 * half + part) + ROWS * chip
-                moves.append((target, block * (2 * chip + half) + ROWS * part, used))
     half_f = 3 * chips * ROWS
-    for index, tile in enumerate(_pieces(moves, 2 * half_f)):
-        value = _gather_tile(lambda source: up_ref[:, :, LANES * source:LANES * source + LANES].astype(jnp.float32),
-                             tile, lane)
-        last = 3 * ROWS - block
-        position = lane + LANES * index % ROWS
-        if LANES * index % half_f >= 2 * chips * ROWS:
-            value = jnp.where(lax.rem(position, ROWS) < ROWS - last, value, 0.0)
+    for index, tile in enumerate(_pieces(_moves(chips, block, True), 2 * half_f)):
+        value = _gather_tile(lambda source: wide[:, :, _span(source, LANES)], tile, lane)
         half, at = divmod(LANES * index, half_f)
-        rows_out[half, :, :, ATTN * COLS + at:ATTN * COLS + at + LANES] = value.astype(jnp.bfloat16)
-    width = down_ref.shape[-1]
+        if at >= 2 * chips * ROWS:
+            position = lax.rem(lane + LANES * index % ROWS, ROWS)
+            value = jnp.where(position < block - 2 * ROWS, value, 0.0)
+        start = ATTN * COLS + at
+        rows_out[half, :, :, start:start + LANES] = value.astype(jnp.bfloat16)
     for part in COLORS:
         used = min(ROWS, block - ROWS * part)
-        value = down_ref[:, ROWS * part:ROWS * part + used, :].astype(jnp.float32)
-        if used < ROWS:
-            value = jnp.concatenate([value, jnp.zeros((layers, ROWS - used, width), jnp.float32)], axis=1)
-        down_out[:, :, width * part:width * part + width] = value.astype(jnp.bfloat16)
+        value = down_ref[ROWS * part:ROWS * part + used].astype(jnp.float32)
+        for layer in range(layers):
+            one = value[:, layer]
+            if used < ROWS:
+                one = jnp.concatenate([one, jnp.zeros((ROWS - used, width), jnp.float32)], axis=0)
+            down_out[layer, :, _span(part, width)] = one.astype(jnp.bfloat16)
 
 
 def pack_weights(w_q, w_k, w_v, w_o, w_up, w_down, chips):
     layers, rows = w_up.shape[:2]
-    block, width = w_down.shape[1:]
+    width = w_down.shape[2]
     vmem = pl.BlockSpec(memory_space=pltpu.VMEM)
     shape = jax.ShapeDtypeStruct
     return pl.pallas_call(
-        functools.partial(pack_kernel, (chips, block)), name="pack_weights",
+        functools.partial(pack_kernel, chips), name="pack_weights",
         out_shape=(shape((2, layers, rows, UP_END), jnp.bfloat16), shape((layers, ROWS, 3 * width), jnp.bfloat16)),
         in_specs=[vmem] * 6, out_specs=(vmem,) * 2,
+        scratch_shapes=[pltpu.VMEM(w_up.shape, jnp.float32)],
         compiler_params=pltpu.CompilerParams(vmem_limit_bytes=VMEM_LIMIT),
-    )(*[weight.reshape(layers, rows, -1) for weight in (w_q, w_k, w_v, w_o, w_up)], w_down)
-
-
-def unpack_kernel(blocks, rows_ref, down_ref, q_out, k_out, v_out, o_out, up_out, down_out):
-    layers, rows = up_out.shape[0], up_out.shape[1]
-    group = q_out.shape[-1] // 2
+    )(w_q.transpose(1, 2, 0, 3), w_k, w_v, w_o.transpose(1, 2, 0, 3), w_up.transpose(1, 0, 2),
+      w_down.transpose(1, 0, 2))
+
+
+def unpack_kernel(chips, rows_ref, down_ref, y_ref, dx_ref, q_out, k_out, v_out, o_out, up_out, down_out, y_out,
+                  dx_out):
+    rows, layers, cols = up_out.shape
+    block, _, width = down_out.shape
+    heads = q_out.shape[1] // 2
     for half in TWO:
-        first = 0
-        for ref, size in ((q_out, group), (k_out, HEAD), (v_out, HEAD), (o_out, group)):
-            ref[:, :, size * half:size * half + size] = rows_ref[half, :, :, first:first + size]
-            first += size
+        for layer in range(layers):
+            for at, ref in ((0, q_out), (heads + 2, o_out)):
+                for head in range(heads):
+                    ref[:, heads * half + head, layer, :] = rows_ref[half, layer, :, _span(at + head, LANES)]
+            for at, ref in ((heads, k_out), (heads + 1, v_out)):
+                ref[layer, :, half, :] = rows_ref[half, layer, :, _span(at, LANES)]
     lane = lax.broadcasted_iota(jnp.int32, (layers, rows, LANES), 2)
-    chips, block = blocks
-    moves = []
-    for half in TWO:
-        for part in COLORS:
-            for chip in range(chips):
-                used = min(ROWS, block - ROWS * part)
-                source = chips * ROWS * (3 * half + part) + ROWS * chip
-                moves.append((block * (2 * chip + half) + ROWS * part, source, used))
     half_f = 3 * chips * ROWS
 
     def load(source):
         half, at = divmod(LANES * source, half_f)
         return rows_ref[half, :, :, ATTN * COLS + at:ATTN * COLS + at + LANES]
 
-    for index, tile in enumerate(_pieces(moves, 2 * chips * block)):
-        up_out[:, :, LANES * index:LANES * index + LANES] = _gather_tile(load, tile, lane)
-    width = down_out.shape[-1]
+    for index, tile in enumerate(_pieces(_moves(chips, block, False), cols)):
+        value = _gather_tile(load, tile, lane)
+        for layer in range(layers):
+            up_out[:, layer, _span(index, LANES)] = value[layer]
     for part in COLORS:
         used = min(ROWS, block - ROWS * part)
-        down_out[:, ROWS * part:ROWS * part + used, :] = down_ref[:, :used, width * part:width * part + width]
-
-
-def unpack_grads(row_grad, down_grad, shapes, chips):
-    layers, rows = row_grad.shape[1:3]
-    block, width = shapes[5][1:]
+        for layer in range(layers):
+            down_out[ROWS * part:ROWS * part + used, layer, :] = down_ref[layer, :used, _span(part, width)]
+    y_out[ALL] = y_ref[ALL]
+    dx_out[ALL] = dx_ref[ALL]
+
+
+def unpack_grads(row_grad, down_grad, y_loc, grad_x, shapes, chips):
     vmem = pl.BlockSpec(memory_space=pltpu.VMEM)
+    q_shape, k_shape, _, _, up_shape, down_shape = shapes
+    layers, rows, heads, head_dim = q_shape
+    turned = [(rows, heads, layers, head_dim), k_shape, k_shape, (rows, heads, layers, head_dim),
+              (rows, layers, up_shape[2]), (down_shape[1], layers, down_shape[2])]
     shape = jax.ShapeDtypeStruct
-    flat = [shape((layers, rows, math.prod(full[2:])), jnp.float32) for full in shapes[:5]]
     outs = pl.pallas_call(
-        functools.partial(unpack_kernel, (chips, block)), name="unpack_grads",
-        out_shape=tuple(flat) + (shape((layers, block, width), jnp.float32),),
-        in_specs=[vmem] * 2, out_specs=(vmem,) * 6,
+        functools.partial(unpack_kernel, chips), name="unpack_grads",
+        out_shape=tuple(shape(full, jnp.float32) for full in turned) + tuple(
+            shape(value.shape, value.dtype) for value in (y_loc, grad_x)),
+        in_specs=[vmem] * 4, out_specs=(vmem,) * 8,
         compiler_params=pltpu.CompilerParams(vmem_limit_bytes=VMEM_LIMIT),
-    )(row_grad, down_grad)
-    return tuple(out.reshape(full) for out, full in zip(outs, shapes))
+    )(row_grad, down_grad, y_loc, grad_x)
+    d_q, d_k, d_v, d_o, d_up, d_down, y_out, dx_out = outs
+    return (y_out[None], dx_out[None], d_q.transpose(2, 0, 1, 3), d_k, d_v, d_o.transpose(2, 0, 1, 3),
+            d_up.transpose(1, 0, 2), d_down.transpose(1, 0, 2))
 
 
 def solution(mesh):
@@ -883,7 +909,7 @@
         rows, down = pack_weights(*weights, chips)
         y_loc, acts, *saved = forward_stack(x_in[0], rows, down)
         row_grad, down_grad, grad_x = backward_stack(w_q.shape[0], grad_out[0], x_in[0], acts, *saved)
-        return (y_loc[None], grad_x[None]) + unpack_grads(row_grad, down_grad, [w.shape for w in weights], chips)
+        return unpack_grads(row_grad, down_grad, y_loc, grad_x, [weight.shape for weight in weights], chips)
 
     return jax.shard_map(body, mesh=mesh4, in_specs=(row_spec,) + (weight_spec,) * 6 + (row_spec,),
                          out_specs=(row_spec, row_spec) + (weight_spec,) * 6, check_vma=False)

time: 573 us -> 553 us (0.965)
  local copies, waits for them, and re-layouts: 20.6 us -> 0 us
    reshape x8 -> x0, local copies, waits for them, and re-layouts: 10.5 us -> none  [the longest x4 5.72 us: pack_weights(): weight.reshape(layers, rows, -1)]
    unnamed x16 -> x0, local copies, waits for them, and re-layouts: 10 us -> none
where the time goes in v6:
time: 553 us; the launch traced here: 552 us
  Pallas kernels  552 us (100%)
    pallas_call x1, Pallas kernels, backward_stack(): pl.pallas_call(functools.partial(backward_kernel, n_layers), name='backwa...  274 us
    pallas_call x1, Pallas kernels, forward_stack(): pl.pallas_call(functools.partial(forward_kernel, n_layers), name='forward...  267 us

profile of v6, /device:TPU:1, one launch (start us, length us, event | category | flops | bytes accessed | tf_op | source)
XLA Modules:
  0.0 552.5 jit_solution(7184137748860074019)
XLA Ops:
  0.6 5.4 pack_weights.1
  6.0 266.8 %forward_stack.1 = (bf16[192,1536]{1,0:T(8,128)(2,1)}, bf16[3,192,1536]{2,1,0:T(8,128)(2,1)}, bf16[2,4,4,4,24,11008]{5,4,3,2,1,0:T(8,128)(2,1)}, f32[2,3,2,192,1...) custom-call(bf16[192,1536]{1,0:T(8,128)(2,1)} %bitcast.12, ...), custom_call_target="tpu_custom_call" | custom-call | tf_op jit(solution)/shard_map/forward_stack/pallas_call | solution.py:374
  272.8 273.8 %backward_stack.1 = (f32[2,2,12,6400]{3,2,1,0:T(8,128)}, f32[2,24,4608]{2,1,0:T(8,128)}, bf16[192,1536]{1,0:T(8,128)(2,1)}) custom-call(bf16[192,1536]{1,0:T(8,128)(2,1)} %bitcast.14, bf16[192,1536]{1,0:T(8,128)(2,1)} %bitcast.13, bf16[3,192,1536]{2,1,0:T(8,128)(2,1)} %get-tuple-element.33.refs_2_, ...), custom_call_target="tpu_custom_call" | custom-call | tf_op jit(solution)/shard_map/backward_stack/pallas_call | solution.py:747
  546.6 5.9 %unpack_grads.1 = (f32[12,12,2,128]{3,2,1,0:T(2,128)}, f32[2,12,2,128]{3,2,1,0:T(2,128)}, f32[2,12,2,128]{3,2,1,0:T(2,128)}, f32[12,12,2,128]{3,2,1,0:T(2,128)},...) custom-call(f32[2,2,12,6400]{3,2,1,0:T(8,128)} %get-tuple-element.42.ro, ...), custom_call_target="tpu_custom_call" | custom-call | tf_op jit(solution)/shard_map/unpack_grads/pallas_call | solution.py:889

commit v7 on v6

--- a/solution.py
+++ b/solution.py
@@ -23,6 +23,9 @@
 RING = 4
 CUBE = (RING, RING, RING)
 SLOTS = 3
+EVEN, EARLY, LATE = range(3)
+AHEAD = 8
+MANY = 2 * AHEAD
 TILE = 8
 COLORS = range(3)
 TWO = range(2)
@@ -112,17 +115,38 @@
         return pltpu.make_async_remote_copy(src_ref=source, dst_ref=target, send_sem=send_sem, recv_sem=recv_sem,
                                             device_id=device, device_id_type=MESH)
 
-    def run(self, steps, n_chunks, n_ticks):
+    def run(self, steps, n_chunks, n_ticks, after=None):
         def tick(now, carry):
             @pl.when(now >= 2)
             def _():
                 for _, _, mine in self.partners:
                     pl.semaphore_wait(self.credit.at[mine], 1)
 
-            for lag, step in steps:
-                @pl.when((now >= lag) & (now < lag + n_chunks))
-                def _(lag=lag, step=step):
-                    step(now - lag)
+            for lag, pace, action in steps:
+                beat = now - lag
+                if pace == EVEN:
+                    @pl.when((beat >= 0) & (beat < n_chunks))
+                    def _(beat=beat, action=action):
+                        action(beat)
+                    continue
+                if pace == EARLY:
+                    double = beat < AHEAD
+                    first = jnp.where(double, 2 * beat, beat + AHEAD)
+                    active = (beat >= 0) & (beat < n_chunks - AHEAD)
+                else:
+                    double = beat >= n_chunks - AHEAD
+                    first = jnp.where(double, 2 * beat - n_chunks, beat - AHEAD)
+                    active = (beat >= AHEAD) & (beat < n_chunks)
+
+                @pl.when(active)
+                def _(first=first, double=double, action=action):
+                    def one(order, inner):
+                        action(first + order)
+                        return inner
+                    lax.fori_loop(0, jnp.where(double, 2, 1), one, 0)
+
+            if after is not None:
+                after(now)
 
             @pl.when(now < n_ticks - 2)
             def _():
@@ -176,7 +200,7 @@
     halves = (slice(0, COLS // 2), slice(COLS // 2, COLS))
 
     def send_own(stage, chunk):
-        slot, sem = _rem(chunk, slots), _rem(chunk, RING)
+        slot, sem = _rem(chunk, slots), _rem(chunk, MANY)
         for color in COLORS:
             dim = ORDERS[color][stage]
             here = spot(slot, color, stage, place[dim], slice(0, COLS))
@@ -188,7 +212,7 @@
                              {dim: near[way][dim]}).start()
 
     def send_far(stage, chunk):
-        slot, sem = _rem(chunk, slots), _rem(chunk, RING)
+        slot, sem = _rem(chunk, slots), _rem(chunk, MANY)
         for color in COLORS:
             dim = ORDERS[color][stage]
             for way in TWO:
@@ -197,7 +221,7 @@
                              {dim: near[way][dim]}).start()
 
     def arrived(part, chunk):
-        slot, sem = _rem(chunk, slots), _rem(chunk, RING)
+        slot, sem = _rem(chunk, slots), _rem(chunk, MANY)
         block = (wbuf.at[slot, 0, 0, 0:2], wbuf.at[slot, 0, 0, 0], wbuf.at[slot, 0, 0:2], wbuf.at[slot, 0, 0],
                  wbuf.at[slot, 0:2], wbuf.at[slot, 0])[part]
         whole = torus.remote(block, block, ring_send.at[part, sem], ring_recv.at[part, sem], torus.sibling)
@@ -357,15 +381,17 @@
 
         keep_copy(chunk).wait()
 
-    steps = [(0, assemble), (0, enter)] + [((part + 1) * LAG, functools.partial(pass_on, part)) for part in range(5)]
-    torus.run(steps + [(ready, exchange), (last_lag, compute)], n_chunks, n_chunks + last_lag)
+    paces = (EARLY, EARLY, EARLY, EVEN, EVEN)
+    steps = [(0, EVEN, assemble), (0, EARLY, enter)]
+    steps += [((part + 1) * LAG, paces[part], functools.partial(pass_on, part)) for part in range(len(paces))]
+    torus.run(steps + [(ready, EVEN, exchange), (last_lag, EVEN, compute)], n_chunks, n_chunks + last_lag)
 
 
 def forward_stack(x_loc, rows, down):
     n_layers = down.shape[0]
     seq, width = x_loc.shape
     bf16, f32 = jnp.bfloat16, jnp.float32
-    slots = 6 * LAG + 4
+    slots = 6 * LAG + 4 + AHEAD
     chunk = CUBE + (ROWS, COLS)
     shape = jax.ShapeDtypeStruct
     hbm = pl.BlockSpec(memory_space=pl.ANY)
@@ -389,7 +415,7 @@
             pltpu.VMEM((seq, 6 * COLS), bf16), pltpu.VMEM((seq, 2 * HEAD), bf16), pltpu.VMEM((seq, 2 * HEAD), bf16),
             pltpu.VMEM((6, seq, COLS), bf16), pltpu.VMEM((2, seq, 18 * COLS), bf16),
             pltpu.VMEM((2, 2, seq, COLS), f32), pltpu.VMEM((seq, width), f32),
-            dma((6, RING)), dma((6, RING)), dma((RING,)), dma((RING,)), dma((RING,)), dma((12,)), dma((2, 2)), dma((2,)),
+            dma((6, MANY)), dma((6, MANY)), dma((RING,)), dma((RING,)), dma((RING,)), dma((12,)), dma((2, 2)), dma((2,)),
             pltpu.SemaphoreType.REGULAR((7,))],
         compiler_params=pltpu.CompilerParams(collective_id=1, has_side_effects=True,
                                              vmem_limit_bytes=VMEM_LIMIT),
@@ -617,6 +643,9 @@
             for y in range(RING):
                 sum0[lead, z, y] = sum0[lead, z, y] + peer[slot, z, y].astype(jnp.float32)
 
+    def ring_slot(stage, chunk):
+        return _rem(chunk, RING if stage == 0 else AHEAD)
+
     def ring_copy(stage, part, slot, color, way):
         send, recv = (half_bufs, full_bufs)[part][stage]
         dim = ORDERS[color][stage]
@@ -632,7 +661,7 @@
         whole.wait_recv()
 
     def source(stage, chunk, color, position, cols):
-        lead = _rem(chunk, leads)
+        lead = _rem(chunk, sums[stage].shape[0])
         if stage == 0:
             return sum0[(lead,) + _block(color, 0, position) + (_rows(color), cols)]
         return sums[stage][(lead, color) + _block(color, stage, position) + (EVERY, cols)]
@@ -640,7 +669,7 @@
     left_cols, right_cols, every = slice(0, COLS // 2), slice(COLS // 2, COLS), slice(0, COLS)
 
     def store_halves(stage, chunk):
-        slot = _rem(chunk, RING)
+        slot = ring_slot(stage, chunk)
         send = half_bufs[stage][0]
         for color in COLORS:
             far = torus.far[ORDERS[color][stage]]
@@ -648,7 +677,7 @@
             send[slot, color, 1] = source(stage, chunk, color, far, right_cols).astype(jnp.bfloat16)
 
     def store_fulls(stage, chunk):
-        slot = _rem(chunk, RING)
+        slot = ring_slot(stage, chunk)
         ring_wait(stage, 0, slot)
         recv = half_bufs[stage][1]
         send = full_bufs[stage][0]
@@ -663,7 +692,7 @@
                     stage, chunk, color, near[way][dim], plain).astype(jnp.bfloat16)
 
     def close_stage(stage, chunk):
-        slot = _rem(chunk, RING)
+        slot = ring_slot(stage, chunk)
         ring_wait(stage, 1, slot)
         recv = full_bufs[stage][1]
         for color in COLORS:
@@ -672,14 +701,14 @@
                      + recv[slot, color, 0].astype(jnp.float32)
                      + recv[slot, color, 1].astype(jnp.float32))
             if stage < 2:
-                sums[stage + 1][_rem(chunk, leads), color] = total
+                sums[stage + 1][_rem(chunk, sums[stage + 1].shape[0]), color] = total
             else:
                 out[pair_of(chunk), _rows(color), columns(chunk)] = total
 
     def send_all(stage, part, chunk):
         for color in COLORS:
             for way in TWO:
-                ring_copy(stage, part, _rem(chunk, RING), color, way).start()
+                ring_copy(stage, part, ring_slot(stage, chunk), color, way).start()
 
     def open_first(chunk):
         merge_pair(chunk)
@@ -690,30 +719,51 @@
         store_fulls(stage, chunk)
         send_all(stage, 1, chunk)
 
+    def open_stage(stage, chunk):
+        store_halves(stage, chunk)
+        send_all(stage, 0, chunk)
+
     def turn(stage, chunk):
         close_stage(stage, chunk)
         if stage < 2:
-            store_halves(stage + 1, chunk)
-            send_all(stage + 1, 0, chunk)
-
-    base = 0
-    steps = [(0, fetch), (base + 2 * LAG, functools.partial(middle, 0)), (base + LAG, open_first),
-             (base + 3 * LAG, functools.partial(turn, 0)), (base + 4 * LAG, functools.partial(middle, 1)),
-             (base + 5 * LAG, functools.partial(turn, 1)), (base + 6 * LAG, functools.partial(middle, 2)),
-             (base + 7 * LAG, functools.partial(turn, 2)), (1, consume), (0, multiply)]
-    torus.run(steps, n_chunks, n_chunks + base + 7 * LAG)
+            open_stage(stage + 1, chunk)
 
     half_rows = ROWS // 2
-    for layer in range(n_layers):
-        for part in range(5):
-            cols = slice(FIFTH * part, FIFTH * part + FIFTH)
-            both = out[layer, :, cols]
-            low, high = both[:half_rows], both[half_rows:]
-            rows_out[core, layer, :, cols] = jnp.where(core == 0, low, high)
-            away[layer, :, cols] = jnp.where(core == 0, high, low)
+
+    def hand_over(layer, part):
+        cols = _at(part * FIFTH, FIFTH)
+        both = out[layer, :, cols]
+        low, high = both[:half_rows], both[half_rows:]
+        rows_out[core, layer, :, cols] = jnp.where(core == 0, low, high)
+        away[layer, :, cols] = jnp.where(core == 0, high, low)
+        torus.remote(away.at[layer, :, cols], rows_out.at[core, layer, :, cols], swap_sem.at[0], swap_sem.at[1],
+                     torus.sibling).start()
+
+    n_ticks = n_chunks + 7 * LAG
+    tail = 2
+
+    def hand_on(now):
+        for layer in range(1, n_layers):
+            begin = (n_layers - layer) * PER_HALF + AHEAD + 8 * LAG
+
+            @pl.when((now >= begin) & (now < begin + 5))
+            def _(layer=layer, begin=begin):
+                hand_over(layer, now - begin)
+
+        @pl.when(now >= n_ticks - 5 + tail)
+        def _():
+            hand_over(0, now - n_ticks + 5)
+
+    steps = [(0, EVEN, fetch), (2 * LAG, EVEN, functools.partial(middle, 0)), (LAG, EVEN, open_first),
+             (3 * LAG, EVEN, functools.partial(close_stage, 0)), (3 * LAG, LATE, functools.partial(open_stage, 1)),
+             (4 * LAG, LATE, functools.partial(middle, 1)), (5 * LAG, LATE, functools.partial(turn, 1)),
+             (6 * LAG, LATE, functools.partial(middle, 2)), (7 * LAG, LATE, functools.partial(turn, 2)),
+             (1, EVEN, consume), (0, EVEN, multiply)]
+    torus.run(steps, n_chunks, n_ticks, hand_on)
+    for part in range(tail):
+        hand_over(0, part)
+    down_out[ALL] = out[:, :, UP_END:]
     swap = torus.remote(away, rows_out.at[core], swap_sem.at[0], swap_sem.at[1], torus.sibling)
-    down_out[ALL] = out[:, :, UP_END:]
-    swap.start()
     swap.wait_send()
     swap.wait_recv()
 
@@ -737,12 +787,12 @@
                pltpu.VMEM((2, seq, HEAD), f32), pltpu.VMEM((2, seq, HEAD), f32),
                pltpu.VMEM((RING,) + chunk, bf16), pltpu.VMEM((RING,) + chunk, bf16),
                pltpu.VMEM((n_layers, ROWS, PER_HALF * COLS), f32), pltpu.VMEM((n_layers, half_rows, UP_END), f32),
-               pltpu.VMEM((leads,) + chunk, f32), pltpu.VMEM((leads, 3, RING, RING, TILE, COLS), f32),
-               pltpu.VMEM((leads, 3, RING, TILE, COLS), f32)]
-    for size in ((RING, RING), (RING,), ()):
-        scratch += [pltpu.VMEM((RING, 3, 2) + size + (TILE, half), bf16)] * 2
-        scratch += [pltpu.VMEM((RING, 3, 2) + size + (TILE, COLS), bf16)] * 2
-    scratch += [dma((10,)), dma((SLOTS,)), dma((SLOTS,)), dma((SLOTS,)), dma((RING,)), dma((RING,)), dma((6, RING)), dma((6, RING)), dma((2,)),
+               pltpu.VMEM((leads,) + chunk, f32), pltpu.VMEM((leads + 6, 3, RING, RING, TILE, COLS), f32),
+               pltpu.VMEM((leads + 3, 3, RING, TILE, COLS), f32)]
+    for slots, size in ((RING, (RING, RING)), (AHEAD, (RING,)), (AHEAD, ())):
+        scratch += [pltpu.VMEM((slots, 3, 2) + size + (TILE, half), bf16)] * 2
+        scratch += [pltpu.VMEM((slots, 3, 2) + size + (TILE, COLS), bf16)] * 2
+    scratch += [dma((10,)), dma((SLOTS,)), dma((SLOTS,)), dma((SLOTS,)), dma((RING,)), dma((RING,)), dma((6, AHEAD)), dma((6, AHEAD)), dma((2,)),
                 pltpu.SemaphoreType.REGULAR((7,))]
     return pl.pallas_call(
         functools.partial(backward_kernel, n_layers),

time: 553 us -> 551 us (level)
  no operation moved by 1% of the time
where the time goes in v7:
time: 551 us; the launch traced here: 550 us
  Pallas kernels  550 us (100%)
    pallas_call x1, Pallas kernels, backward_stack(): pl.pallas_call(functools.partial(backward_kernel, n_layers), name='backwa...  273 us
    pallas_call x1, Pallas kernels, forward_stack(): pl.pallas_call(functools.partial(forward_kernel, n_layers), name='forward...  266 us

profile of v7, /device:TPU:1, one launch (start us, length us, event | category | flops | bytes accessed | tf_op | source)
XLA Modules:
  0.0 550.4 jit_solution(7102435658090483465)
XLA Ops:
  0.6 5.4 pack_weights.1
  6.0 265.6 %forward_stack.1 = (bf16[192,1536]{1,0:T(8,128)(2,1)}, bf16[3,192,1536]{2,1,0:T(8,128)(2,1)}, bf16[2,4,4,4,24,11008]{5,4,3,2,1,0:T(8,128)(2,1)}, f32[2,3,2,192,1...) custom-call(bf16[192,1536]{1,0:T(8,128)(2,1)} %bitcast.12, ...), custom_call_target="tpu_custom_call" | custom-call | tf_op jit(solution)/shard_map/forward_stack/pallas_call | solution.py:400
  271.6 272.9 %backward_stack.1 = (f32[2,2,12,6400]{3,2,1,0:T(8,128)}, f32[2,24,4608]{2,1,0:T(8,128)}, bf16[192,1536]{1,0:T(8,128)(2,1)}) custom-call(bf16[192,1536]{1,0:T(8,128)(2,1)} %bitcast.14, bf16[192,1536]{1,0:T(8,128)(2,1)} %bitcast.13, bf16[3,192,1536]{2,1,0:T(8,128)(2,1)} %get-tuple-element.33.refs_2_, ...), custom_call_target="tpu_custom_call" | custom-call | tf_op jit(solution)/shard_map/backward_stack/pallas_call | solution.py:797
  544.5 5.9 %unpack_grads.1 = (f32[12,12,2,128]{3,2,1,0:T(2,128)}, f32[2,12,2,128]{3,2,1,0:T(2,128)}, f32[2,12,2,128]{3,2,1,0:T(2,128)}, f32[12,12,2,128]{3,2,1,0:T(2,128)},...) custom-call(f32[2,2,12,6400]{3,2,1,0:T(8,128)} %get-tuple-element.42.ro, ...), custom_call_target="tpu_custom_call" | custom-call | tf_op jit(solution)/shard_map/unpack_grads/pallas_call | solution.py:939

commit v8 on v6

--- a/solution.py
+++ b/solution.py
@@ -112,17 +112,18 @@
         return pltpu.make_async_remote_copy(src_ref=source, dst_ref=target, send_sem=send_sem, recv_sem=recv_sem,
                                             device_id=device, device_id_type=MESH)
 
-    def run(self, steps, n_chunks, n_ticks):
+    def run(self, steps, n_chunks, n_ticks, after):
         def tick(now, carry):
             @pl.when(now >= 2)
             def _():
                 for _, _, mine in self.partners:
                     pl.semaphore_wait(self.credit.at[mine], 1)
 
-            for lag, step in steps:
+            for lag, action in steps:
                 @pl.when((now >= lag) & (now < lag + n_chunks))
-                def _(lag=lag, step=step):
-                    step(now - lag)
+                def _(lag=lag, action=action):
+                    action(now - lag)
+            after(now)
 
             @pl.when(now < n_ticks - 2)
             def _():
@@ -133,19 +134,17 @@
         lax.fori_loop(0, n_ticks, tick, 0)
 
 
-def forward_kernel(n_layers, x_ref, rows_ref, down_ref, y_ref, acts, w_out, hid_out, gelu_out, norm_out, q_out, k_out, v_out,
-                   o_out, wbuf, peer, shard, twin, state, normed, q_buf, k_buf, v_buf, o_buf, gelu_buf, hid_buf, acc,
-                   ring_send, ring_recv, pair_send, pair_recv, keep_sem, save_sem, hid_sem, twin_sem, credit):
-    torus = Torus(credit)
+def forward_steps(torus, n_layers, x_ref, rows_ref, down_ref, y_ref, saved, wbuf, peer, shard, twin, state, lefts, rights,
+                  q_buf, k_buf, v_buf, hid_buf, acc, ring_send, ring_recv, pair_send, pair_recv, keep_sem, save_sem,
+                  hid_sem, twin_sem):
+    acts, w_out, hid_out, gelu_out, norm_out, q_out, k_out, v_out, o_out = saved
     core, place, near = torus.core, torus.place, torus.near
     slots = wbuf.shape[0]
     n_chunks = n_layers * PER_HALF
     ready = 6 * LAG
-    last_lag = ready + 1
     seq = x_ref.shape[0]
     third = 64 * ROWS
-    state[ALL] = x_ref[ALL]
-    torus.meet()
+    last = n_layers - 1
     swap = torus.remote(rows_ref.at[1 - core], twin, twin_sem.at[0], twin_sem.at[1], torus.sibling)
     swap.start()
     swap.wait_send()
@@ -230,16 +229,23 @@
                                      keep_sem.at[_rem(chunk, RING)])
 
     def save_copies(layer, names):
-        parts = {"n0": (normed, norm_out.at[layer, 0], 0), "n1": (normed, norm_out.at[layer, 1], 1),
+        parts = {"n0": (lefts.at[NORM_ATTN], norm_out.at[layer, 0], 0), "n1": (lefts.at[NORM_MLP], norm_out.at[layer, 1], 1),
                  "q": (q_buf, q_out.at[layer], 2), "k": (k_buf, k_out.at[layer], 3), "v": (v_buf, v_out.at[layer], 4),
-                 "o": (o_buf, o_out.at[layer], 5)}
-        for half in TWO:
-            for part in COLORS:
-                parts[f"a{half}{part}"] = (gelu_buf.at[half, :, slice(third * part, third * (part + 1))],
-                                           gelu_out.at[layer, 3 * half + part], 6 + 3 * half + part)
+                 "o": (rights.at[O_AT:QKV_AT], o_out.at[layer], 5), "a": (lefts.at[0:6], gelu_out.at[layer], 6),
+                 "mid": (state, acts.at[2 * layer], 7), "end": (state, acts.at[2 * layer + 1], 8)}
         return [pltpu.make_async_copy(parts[name][0], parts[name][1], save_sem.at[parts[name][2]]) for name in names]
 
-    gelu_names = [f"a{half}{part}" for half in TWO for part in COLORS]
+    def save(layer, names):
+        @pl.when(layer < last)
+        def _():
+            for copy in save_copies(layer, names):
+                copy.start()
+
+    def saved_all(layer, names):
+        @pl.when(layer < last)
+        def _():
+            for copy in save_copies(layer, names):
+                copy.wait()
 
     def hidden_copies(layer, order):
         slot, part, at = _rem(order, 2), order // 6, _at(_rem(order, 6) * COLS, COLS)
@@ -259,28 +265,26 @@
 
         @pl.when(index == 0)
         def _():
-            normed[ALL] = _rms(state[ALL])
-            for copy in save_copies(layer, ["n0"]):
-                copy.start()
+            lefts[NORM_ATTN] = _rms(state[ALL])
+            save(layer, ["n0"])
 
         @pl.when(index < 3)
         def _():
             for role, half in torus.sides:
                 q_buf[:, _at(3 * COLS * half + COLS * index, COLS)] = _dot(
-                    normed[ALL], weights(role)).astype(jnp.bfloat16)
+                    lefts[NORM_ATTN], weights(role)).astype(jnp.bfloat16)
 
         @pl.when(index == 3)
         def _():
             for role, half in torus.sides:
-                both = _dot(normed[ALL], weights(role)).astype(jnp.bfloat16)
+                both = _dot(lefts[NORM_ATTN], weights(role)).astype(jnp.bfloat16)
                 k_buf[:, _at(HEAD * half, HEAD)] = both[:, :HEAD]
                 v_buf[:, _at(HEAD * half, HEAD)] = both[:, HEAD:]
 
         @pl.when(index == QKV)
         def _():
             acc[ALL] = jnp.zeros_like(acc)
-            for copy in save_copies(layer, ["q", "k", "v"]):
-                copy.start()
+            save(layer, ["q", "k", "v"])
 
         @pl.when((index >= QKV) & (index < ATTN))
         def _():
@@ -293,44 +297,46 @@
                     prob = _probs(q_buf[:, at], key, causal)
                     outs.append(_dot(prob.astype(jnp.bfloat16), value).astype(jnp.bfloat16))
                 block = jnp.concatenate(outs, axis=1)
-                o_buf[3 * half + index - QKV] = block
+                rights[O_AT + 3 * half + index - QKV] = block
                 acc[ALL] += _dot_rhs_t(block, weights(role))
 
-        @pl.when(index == 6)
-        def _():
+        @pl.when(index == ATTN - 1)
+        def _():
+            @pl.when(layer > 0)
+            def _():
+                saved_all(layer - 1, ["end"])
             middle = (state[ALL].astype(jnp.float32) + acc[ALL]).astype(jnp.bfloat16)
             state[ALL] = middle
-            acts[2 * layer] = middle
-            for copy in save_copies(layer, ["n0"]):
+            lefts[NORM_MLP] = _rms(middle)
+            save(layer, ["n1", "o"])
+            mid = save_copies(layer, ["mid"])[0]
+            mid.start()
+
+        @pl.when((index > ATTN) & (index <= UP_BLOCKS))
+        def _():
+            for copy in hidden_copies(layer, index - ATTN - 1):
                 copy.wait()
-            normed[ALL] = _rms(middle)
-            for copy in save_copies(layer, ["n1", "o"]):
+
+        @pl.when((index >= ATTN) & (index < UP_BLOCKS))
+        def _():
+            order = index - ATTN
+            for role, half in torus.sides:
+                hidden = _dot(lefts[NORM_MLP], weights(role))
+                hid_buf[_rem(order, 2), half] = hidden
+                lefts[3 * half + order // 6, :, _at(COLS * _rem(order, 6), COLS)] = jax.nn.gelu(
+                    hidden).astype(jnp.bfloat16)
+            for copy in hidden_copies(layer, order):
                 copy.start()
 
-        @pl.when((index >= 8) & (index < 26))
-        def _():
-            for copy in hidden_copies(layer, index - 8):
-                copy.wait()
-
-        @pl.when((index >= ATTN) & (index < UP_BLOCKS))
-        def _():
-            for role, half in torus.sides:
-                hidden = _dot(normed[ALL], weights(role))
-                hid_buf[_rem(index - ATTN, 2), half] = hidden
-                gelu_buf[half, :, _at(COLS * (index - ATTN), COLS)] = jax.nn.gelu(hidden).astype(jnp.bfloat16)
-            for copy in hidden_copies(layer, index - ATTN):
-                copy.start()
-
         @pl.when(index == UP_BLOCKS)
         def _():
-            for copy in save_copies(layer, gelu_names):
-                copy.start()
+            save(layer, ["a"])
+            save_copies(layer, ["mid"])[0].wait()
 
         @pl.when(index >= UP_BLOCKS)
         def _():
             part, at = (index - UP_BLOCKS) // 6, _at(COLS * _rem(index - UP_BLOCKS, 6), COLS)
-            total = sum(_dot(gelu_buf[half, :, _at(third * part, third)], weights(role))
-                        for role, half in torus.sides)
+            total = sum(_dot(lefts[3 * half + part], weights(role)) for role, half in torus.sides)
 
             @pl.when(part == 0)
             def _():
@@ -342,78 +348,45 @@
 
         @pl.when(index == PER_HALF - 1)
         def _():
+            saved_all(layer, ["n0", "n1", "q", "k", "v", "o", "a"])
             result = (state[ALL].astype(jnp.float32) + acc[ALL]).astype(jnp.bfloat16)
             state[ALL] = result
-
-            @pl.when(layer < n_layers - 1)
-            def _():
-                acts[2 * layer + 1] = result
-
-            @pl.when(layer == n_layers - 1)
+            save(layer, ["end"])
+
+            @pl.when(layer == last)
             def _():
                 y_ref[ALL] = result
-            for copy in save_copies(layer, ["n1", "q", "k", "v", "o"] + gelu_names):
-                copy.wait()
 
         keep_copy(chunk).wait()
 
-    steps = [(0, assemble), (0, enter)] + [((part + 1) * LAG, functools.partial(pass_on, part)) for part in range(5)]
-    torus.run(steps + [(ready, exchange), (last_lag, compute)], n_chunks, n_chunks + last_lag)
-
-
-def forward_stack(x_loc, rows, down):
-    n_layers = down.shape[0]
-    seq, width = x_loc.shape
-    bf16, f32 = jnp.bfloat16, jnp.float32
-    slots = 6 * LAG + 4
-    chunk = CUBE + (ROWS, COLS)
-    shape = jax.ShapeDtypeStruct
-    hbm = pl.BlockSpec(memory_space=pl.ANY)
-    vmem = pl.BlockSpec(memory_space=pltpu.VMEM)
-    dma = pltpu.SemaphoreType.DMA
-    return pl.pallas_call(
-        functools.partial(forward_kernel, n_layers),
-        name="forward_stack",
-        out_shape=(shape((seq, width), bf16), shape((2 * n_layers - 1, seq, width), bf16),
-                   shape((n_layers, 4, 4, 4, ROWS, PER_HALF * COLS), bf16),
-                   shape((n_layers, 3, 2, seq, width), f32), shape((n_layers, 6, seq, width), bf16),
-                   shape((n_layers, 2, seq, width), bf16), shape((n_layers, seq, width), bf16),
-                   shape((n_layers, seq, 2 * HEAD), bf16), shape((n_layers, seq, 2 * HEAD), bf16),
-                   shape((n_layers, 6, seq, COLS), bf16)),
-        in_specs=[vmem] * 3,
-        out_specs=(vmem,) * 2 + (hbm,) * 8,
-        scratch_shapes=[
-            pltpu.VMEM((slots,) + chunk, bf16), pltpu.VMEM((RING,) + chunk, bf16),
-            pltpu.VMEM((n_layers, ROWS, PER_HALF * COLS), bf16), pltpu.VMEM(rows.shape[1:], bf16),
-            pltpu.VMEM((seq, width), bf16), pltpu.VMEM((seq, width), bf16),
-            pltpu.VMEM((seq, 6 * COLS), bf16), pltpu.VMEM((seq, 2 * HEAD), bf16), pltpu.VMEM((seq, 2 * HEAD), bf16),
-            pltpu.VMEM((6, seq, COLS), bf16), pltpu.VMEM((2, seq, 18 * COLS), bf16),
-            pltpu.VMEM((2, 2, seq, COLS), f32), pltpu.VMEM((seq, width), f32),
-            dma((6, RING)), dma((6, RING)), dma((RING,)), dma((RING,)), dma((RING,)), dma((12,)), dma((2, 2)), dma((2,)),
-            pltpu.SemaphoreType.REGULAR((7,))],
-        compiler_params=pltpu.CompilerParams(collective_id=1, has_side_effects=True,
-                                             vmem_limit_bytes=VMEM_LIMIT),
-    )(x_loc, rows, down)
-
-
-def backward_kernel(n_layers, *refs):
-    (g_ref, x_ref, acts, w_own, hid_in, gelu_in, norm_in, q_in, k_in, v_in, o_in,
-     rows_out, down_out, dx_ref,
-     mine, theirs, lefts, rights, hid_buf, dact, dnorm, q_buf, k_buf, v_buf, x_mid, x_in, dk_acc, dv_acc,
-     outgo, peer, out, away, sum0, sum1, sum2, sa0, ra0, sb0, rb0, sa1, ra1, sb1, rb1, sa2, ra2, sb2, rb2,
-     load_sem, own_sem, push_send, push_recv, pair_send, pair_recv, ring_send, ring_recv, swap_sem, credit) = refs
-    torus = Torus(credit)
-    core, place, near = torus.core, torus.place, torus.near
-    sums = (sum0, sum1, sum2)
-    half_bufs = ((sa0, ra0), (sa1, ra1), (sa2, ra2))
-    full_bufs = ((sb0, rb0), (sb1, rb1), (sb2, rb2))
-    n_chunks = n_layers * PER_HALF
-    seq, width = g_ref.shape
+    steps = [(0, assemble), (0, enter)]
+    steps += [((part + 1) * LAG, functools.partial(pass_on, part)) for part in range(5)]
+    return steps + [(ready, exchange), (ready + 1, compute)]
+
+
+def backward_steps(torus, n_layers, g_ref, x_ref, dx_ref, saved, out, wbuf, lefts, rights, hid_buf, dact, dnorm, q_buf,
+                   k_buf, v_buf, x_mid, x_in, dk_acc, dv_acc, sums, half_bufs, full_bufs, load_sem, own_sem, push_send,
+                   push_recv, pair_send, pair_recv, ring_send, ring_recv):
+    acts, w_own, hid_in, gelu_in, norm_in, q_in, k_in, v_in, o_in = saved
+    place, near = torus.place, torus.near
+    seq = g_ref.shape[0]
     third = 64 * ROWS
-    leads = sum0.shape[0]
+    last = n_layers - 1
+
+    def mine_slot(chunk):
+        return 6 * _rem(chunk, 2)
+
+    def out_slot(chunk):
+        return 7 + _rem(chunk, 2)
+
+    def their_slot(chunk):
+        return 9 + _rem(chunk, SLOTS)
+
+    def peer_slot(chunk):
+        return 12 + _rem(chunk, RING)
 
     def pair_of(chunk):
-        return n_layers - 1 - chunk // PER_HALF
+        return last - chunk // PER_HALF
 
     def columns(chunk):
         index = _rem(chunk, PER_HALF)
@@ -442,20 +415,16 @@
     def first_input(ref):
         return pltpu.make_async_copy(ref, x_in, load_sem.at[9])
 
-    start(n_layers - 1, ["a"])
     for block in SIX:
         rights[block] = g_ref[:, COLS * block:COLS * block + COLS]
-    torus.meet()
-    finish(n_layers - 1, ["a"])
 
     def own_copy(chunk):
-        slot = _rem(chunk, SLOTS)
-        return pltpu.make_async_copy(w_own.at[pair_of(chunk), :, :, :, :, columns(chunk)], mine.at[slot],
-                                     own_sem.at[slot])
+        return pltpu.make_async_copy(w_own.at[pair_of(chunk), :, :, :, :, columns(chunk)], wbuf.at[mine_slot(chunk)],
+                                     own_sem.at[_rem(chunk, 2)])
 
     def push_copy(chunk):
         slot = _rem(chunk, SLOTS)
-        return torus.remote(w_own.at[pair_of(chunk), :, :, :, :, columns(chunk)], theirs.at[slot],
+        return torus.remote(w_own.at[pair_of(chunk), :, :, :, :, columns(chunk)], wbuf.at[their_slot(chunk)],
                             push_send.at[slot], push_recv.at[slot], torus.sibling)
 
     def fetch(chunk):
@@ -467,22 +436,25 @@
 
     def consume(chunk):
         pair, index = pair_of(chunk), _rem(chunk, PER_HALF)
-        slot = _rem(chunk, SLOTS)
         own_copy(chunk).wait()
         push = push_copy(chunk)
         push.wait_send()
         push.wait_recv()
 
         def weights(role):
-            return (mine, theirs)[role][slot].reshape(third, COLS)
+            return wbuf[(mine_slot, their_slot)[role](chunk)].reshape(third, COLS)
 
         @pl.when(index == 0)
         def _():
-            start(pair, ["n_mlp", "n_attn", "o", "q", "k", "v", "x_mid", "h0"])
+            start(pair, ["x_mid", "h0"])
+
+            @pl.when(pair < last)
+            def _():
+                start(pair, ["n_mlp", "n_attn", "o", "q", "k", "v"])
 
             @pl.when(pair == 0)
             def _():
-                first_input(x_ref).start()
+                x_in[ALL] = x_ref[ALL]
 
             @pl.when(pair > 0)
             def _():
@@ -516,7 +488,9 @@
 
         @pl.when(index == DOWN_DONE - 1)
         def _():
-            finish(pair, ["n_mlp"])
+            @pl.when(pair < last)
+            def _():
+                finish(pair, ["n_mlp", "n_attn", "o", "q", "k", "v"])
 
         @pl.when(index == DOWN_DONE)
         def _():
@@ -533,12 +507,11 @@
 
         @pl.when(index == UP_DONE - 1)
         def _():
-            finish(pair, ["x_mid", "o"])
+            finish(pair, ["x_mid"])
             lefts[GRAD] = (total_grad() + _rms_back(x_mid[ALL], dnorm[ALL])).astype(jnp.bfloat16)
 
         @pl.when(index == UP_DONE)
         def _():
-            finish(pair, ["q", "k", "v"])
             dk_acc[ALL] = jnp.zeros_like(dk_acc)
             dv_acc[ALL] = jnp.zeros_like(dv_acc)
 
@@ -563,7 +536,6 @@
 
         @pl.when(index == O_DONE - 1)
         def _():
-            finish(pair, ["n_attn"])
             for half in TWO:
                 rights[QKV_AT + QKV * half + QKV - 1] = jnp.concatenate([dk_acc[half], dv_acc[half]], axis=1).astype(jnp.bfloat16)
 
@@ -578,44 +550,46 @@
 
         @pl.when(index == PER_HALF - 1)
         def _():
-            first_input(x_ref).wait()
-
             @pl.when(pair > 0)
             def _():
+                first_input(acts.at[2 * pair - 1]).wait()
                 finish(pair - 1, ["a"])
             result = (lefts[GRAD].astype(jnp.float32) + _rms_back(x_in[ALL], dnorm[ALL])).astype(jnp.bfloat16)
             dx_ref[ALL] = result
             for block in SIX:
                 rights[block] = result[:, COLS * block:COLS * block + COLS]
 
-    def pair_copy(slot):
-        return torus.remote(outgo.at[slot], peer.at[slot], pair_send.at[slot], pair_recv.at[slot], torus.sibling)
+    def pair_copy(chunk):
+        slot = _rem(chunk, RING)
+        return torus.remote(wbuf.at[out_slot(chunk)], wbuf.at[peer_slot(chunk)], pair_send.at[slot], pair_recv.at[slot],
+                            torus.sibling)
 
     def multiply(chunk):
         index = _rem(chunk, PER_HALF)
-        slot = _rem(chunk, RING)
+        lead = _rem(chunk, sums[0].shape[0])
         quarter = third // RING
         for role, half in torus.sides[::-1]:
             left = jnp.where(index < DOWN_DONE, 3 * half + index // 6,
                              jnp.where(index < UP_DONE, NORM_MLP, jnp.where(index < O_DONE, GRAD, NORM_ATTN)))
             right = jnp.where(index < DOWN_DONE, _rem(index, 6),
                               jnp.where(index < UP_DONE, DH_AT + FF * half + index - DOWN_DONE,
-                                        jnp.where(index < O_DONE, O_AT + 3 * half + index - UP_DONE, QKV_AT + QKV * half + index - O_DONE)))
+                                        jnp.where(index < O_DONE, O_AT + 3 * half + index - UP_DONE,
+                                                  QKV_AT + QKV * half + index - O_DONE)))
             for z in range(RING):
                 part = _dot_lhs_t(lefts[left, :, quarter * z:quarter * z + quarter], rights[right])
                 if role == 0:
-                    sum0[_rem(chunk, leads), z] = part.reshape(RING, RING, ROWS, COLS)
+                    sums[0][lead, z] = part.reshape(RING, RING, ROWS, COLS)
                 else:
-                    outgo[slot, z] = part.astype(jnp.bfloat16).reshape(RING, RING, ROWS, COLS)
-        pair_copy(slot).start()
+                    wbuf[out_slot(chunk), z] = part.astype(jnp.bfloat16).reshape(RING, RING, ROWS, COLS)
+        pair_copy(chunk).start()
 
     def merge_pair(chunk):
-        slot, lead = _rem(chunk, RING), _rem(chunk, leads)
-        pair_copy(slot).wait_send()
-        pair_copy(slot).wait_recv()
+        lead = _rem(chunk, sums[0].shape[0])
+        pair_copy(chunk).wait_send()
+        pair_copy(chunk).wait_recv()
         for z in range(RING):
             for y in range(RING):
-                sum0[lead, z, y] = sum0[lead, z, y] + peer[slot, z, y].astype(jnp.float32)
+                sums[0][lead, z, y] = sums[0][lead, z, y] + wbuf[peer_slot(chunk), z, y].astype(jnp.float32)
 
     def ring_copy(stage, part, slot, color, way):
         send, recv = (half_bufs, full_bufs)[part][stage]
@@ -632,9 +606,9 @@
         whole.wait_recv()
 
     def source(stage, chunk, color, position, cols):
-        lead = _rem(chunk, leads)
+        lead = _rem(chunk, sums[stage].shape[0])
         if stage == 0:
-            return sum0[(lead,) + _block(color, 0, position) + (_rows(color), cols)]
+            return sums[0][(lead,) + _block(color, 0, position) + (_rows(color), cols)]
         return sums[stage][(lead, color) + _block(color, stage, position) + (EVERY, cols)]
 
     left_cols, right_cols, every = slice(0, COLS // 2), slice(COLS // 2, COLS), slice(0, COLS)
@@ -672,7 +646,7 @@
                      + recv[slot, color, 0].astype(jnp.float32)
                      + recv[slot, color, 1].astype(jnp.float32))
             if stage < 2:
-                sums[stage + 1][_rem(chunk, leads), color] = total
+                sums[stage + 1][_rem(chunk, sums[stage + 1].shape[0]), color] = total
             else:
                 out[pair_of(chunk), _rows(color), columns(chunk)] = total
 
@@ -690,71 +664,109 @@
         store_fulls(stage, chunk)
         send_all(stage, 1, chunk)
 
+    def open_stage(stage, chunk):
+        store_halves(stage, chunk)
+        send_all(stage, 0, chunk)
+
     def turn(stage, chunk):
         close_stage(stage, chunk)
         if stage < 2:
-            store_halves(stage + 1, chunk)
-            send_all(stage + 1, 0, chunk)
-
-    base = 0
-    steps = [(0, fetch), (base + 2 * LAG, functools.partial(middle, 0)), (base + LAG, open_first),
-             (base + 3 * LAG, functools.partial(turn, 0)), (base + 4 * LAG, functools.partial(middle, 1)),
-             (base + 5 * LAG, functools.partial(turn, 1)), (base + 6 * LAG, functools.partial(middle, 2)),
-             (base + 7 * LAG, functools.partial(turn, 2)), (1, consume), (0, multiply)]
-    torus.run(steps, n_chunks, n_chunks + base + 7 * LAG)
-
+            open_stage(stage + 1, chunk)
+
+    return [(0, fetch), (2 * LAG, functools.partial(middle, 0)), (LAG, open_first),
+            (3 * LAG, functools.partial(turn, 0)), (4 * LAG, functools.partial(middle, 1)),
+            (5 * LAG, functools.partial(turn, 1)), (6 * LAG, functools.partial(middle, 2)),
+            (7 * LAG, functools.partial(turn, 2)), (1, consume), (0, multiply)]
+
+
+def train_kernel(n_layers, x_ref, g_ref, rows_ref, down_ref, y_ref, dx_ref, rows_out, out, *refs):
+    saved, refs = refs[:9], refs[9:]
+    (wbuf, peer, shard, twin, state, lefts, rights, q_buf, k_buf, v_buf, hid_out_buf, acc, hid_in_buf, dact, x_mid, x_in,
+     dk_acc, dv_acc, away), refs = refs[:19], refs[19:]
+    sums, half_bufs, full_bufs, refs = refs[:3], refs[3:9], refs[9:15], refs[15:]
+    half_bufs = [half_bufs[2 * stage:2 * stage + 2] for stage in COLORS]
+    full_bufs = [full_bufs[2 * stage:2 * stage + 2] for stage in COLORS]
+    forward_sems, backward_sems, (swap_sem, credit) = refs[:8], refs[8:16], refs[16:]
+    torus = Torus(credit)
+    core = torus.core
+    n_chunks = n_layers * PER_HALF
+    state[ALL] = x_ref[ALL]
+    torus.meet()
+    forward = forward_steps(torus, n_layers, x_ref, rows_ref, down_ref, y_ref, saved, wbuf, peer, shard, twin, state, lefts,
+                            rights, q_buf, k_buf, v_buf, hid_out_buf, acc, *forward_sems)
+    backward = backward_steps(torus, n_layers, g_ref, x_ref, dx_ref, saved, out, wbuf, lefts, rights, hid_in_buf, dact, acc,
+                              q_buf, k_buf, v_buf, x_mid, x_in, dk_acc, dv_acc, sums, half_bufs, full_bufs,
+                              *backward_sems)
+    turn_at = n_chunks + 8
+    backward = [(lag + turn_at, step) for lag, step in backward]
+    n_ticks = turn_at + n_chunks + 7 * LAG
     half_rows = ROWS // 2
-    for layer in range(n_layers):
-        for part in range(5):
-            cols = slice(FIFTH * part, FIFTH * part + FIFTH)
-            both = out[layer, :, cols]
-            low, high = both[:half_rows], both[half_rows:]
-            rows_out[core, layer, :, cols] = jnp.where(core == 0, low, high)
-            away[layer, :, cols] = jnp.where(core == 0, high, low)
+    tail = 2
+
+    def hand_over(layer, part):
+        cols = _at(part * FIFTH, FIFTH)
+        both = out[layer, :, cols]
+        low, high = both[:half_rows], both[half_rows:]
+        rows_out[core, layer, :, cols] = jnp.where(core == 0, low, high)
+        away[layer, :, cols] = jnp.where(core == 0, high, low)
+        torus.remote(away.at[layer, :, cols], rows_out.at[core, layer, :, cols], swap_sem.at[0], swap_sem.at[1],
+                     torus.sibling).start()
+
+    def hand_on(now):
+        for layer in range(1, n_layers):
+            begin = turn_at + (n_layers - layer) * PER_HALF + 8 * LAG
+
+            @pl.when((now >= begin) & (now < begin + 5))
+            def _(layer=layer, begin=begin):
+                hand_over(layer, now - begin)
+
+        @pl.when(now >= n_ticks - 5 + tail)
+        def _():
+            hand_over(0, now - n_ticks + 5)
+
+    torus.run(backward[:1] + forward + backward[1:], n_chunks, n_ticks, hand_on)
+    for part in range(tail):
+        hand_over(0, part)
     swap = torus.remote(away, rows_out.at[core], swap_sem.at[0], swap_sem.at[1], torus.sibling)
-    down_out[ALL] = out[:, :, UP_END:]
-    swap.start()
     swap.wait_send()
     swap.wait_recv()
 
 
-def backward_stack(n_layers, g_loc, *saved):
-    seq, width = g_loc.shape
+def train_stack(x_loc, g_loc, rows, down):
+    n_layers = down.shape[0]
+    seq, width = x_loc.shape
     bf16, f32 = jnp.bfloat16, jnp.float32
     half = COLS // 2
     chunk = CUBE + (ROWS, COLS)
-    leads = 7
     shape = jax.ShapeDtypeStruct
     hbm = pl.BlockSpec(memory_space=pl.ANY)
     vmem = pl.BlockSpec(memory_space=pltpu.VMEM)
     dma = pltpu.SemaphoreType.DMA
-    half_rows = ROWS // 2
-    scratch = [pltpu.VMEM((SLOTS,) + chunk, bf16), pltpu.VMEM((SLOTS,) + chunk, bf16),
-               pltpu.VMEM((9, seq, width), bf16), pltpu.VMEM((56, seq, COLS), bf16),
-               pltpu.VMEM((2, seq, width), f32), pltpu.VMEM((2, seq, width), f32), pltpu.VMEM((seq, width), f32),
-               pltpu.VMEM((seq, 6 * COLS), bf16), pltpu.VMEM((seq, 2 * HEAD), bf16), pltpu.VMEM((seq, 2 * HEAD), bf16),
-               pltpu.VMEM((seq, width), bf16), pltpu.VMEM((seq, width), bf16),
-               pltpu.VMEM((2, seq, HEAD), f32), pltpu.VMEM((2, seq, HEAD), f32),
-               pltpu.VMEM((RING,) + chunk, bf16), pltpu.VMEM((RING,) + chunk, bf16),
-               pltpu.VMEM((n_layers, ROWS, PER_HALF * COLS), f32), pltpu.VMEM((n_layers, half_rows, UP_END), f32),
-               pltpu.VMEM((leads,) + chunk, f32), pltpu.VMEM((leads, 3, RING, RING, TILE, COLS), f32),
-               pltpu.VMEM((leads, 3, RING, TILE, COLS), f32)]
-    for size in ((RING, RING), (RING,), ()):
-        scratch += [pltpu.VMEM((RING, 3, 2) + size + (TILE, half), bf16)] * 2
-        scratch += [pltpu.VMEM((RING, 3, 2) + size + (TILE, COLS), bf16)] * 2
-    scratch += [dma((10,)), dma((SLOTS,)), dma((SLOTS,)), dma((SLOTS,)), dma((RING,)), dma((RING,)), dma((6, RING)), dma((6, RING)), dma((2,)),
-                pltpu.SemaphoreType.REGULAR((7,))]
+    saved = (shape((2 * n_layers - 1, seq, width), bf16), shape((n_layers,) + CUBE + (ROWS, PER_HALF * COLS), bf16),
+             shape((n_layers, 3, 2, seq, width), f32), shape((n_layers, 6, seq, width), bf16),
+             shape((n_layers, 2, seq, width), bf16), shape((n_layers, seq, width), bf16),
+             shape((n_layers, seq, 2 * HEAD), bf16), shape((n_layers, seq, 2 * HEAD), bf16),
+             shape((n_layers, 6, seq, COLS), bf16))
+    scratch = [pltpu.VMEM(full, kind) for full, kind in (
+        ((6 * LAG + 4,) + chunk, bf16), ((RING,) + chunk, bf16), ((n_layers, ROWS, PER_HALF * COLS), bf16),
+        (rows.shape[1:], bf16), ((seq, width), bf16), ((9, seq, width), bf16), ((56, seq, COLS), bf16),
+        ((seq, 6 * COLS), bf16), ((seq, 2 * HEAD), bf16), ((seq, 2 * HEAD), bf16), ((2, 2, seq, COLS), f32),
+        ((seq, width), f32), ((2, seq, width), f32), ((2, seq, width), f32), ((seq, width), bf16), ((seq, width), bf16),
+        ((2, seq, HEAD), f32), ((2, seq, HEAD), f32), ((n_layers, ROWS // 2, UP_END), f32), ((6,) + chunk, f32),
+        ((5, 3, RING, RING, TILE, COLS), f32), ((5, 3, RING, TILE, COLS), f32))]
+    for cols in (half, COLS):
+        for size in ((RING, RING), (RING,), ()):
+            scratch += [pltpu.VMEM((RING, 3, 2) + size + (TILE, cols), bf16)] * 2
+    scratch += [dma((6, RING)), dma((6, RING)), dma((RING,)), dma((RING,)), dma((RING,)), dma((9,)), dma((2, 2)), dma((2,))]
+    scratch += [dma((10,)), dma((2,)), dma((SLOTS,)), dma((SLOTS,)), dma((RING,)), dma((RING,)), dma((6, RING)),
+                dma((6, RING)), dma((2,)), pltpu.SemaphoreType.REGULAR((7,))]
     return pl.pallas_call(
-        functools.partial(backward_kernel, n_layers),
-        name="backward_stack",
-        out_shape=(shape((2, n_layers, half_rows, UP_END), f32),
-                   shape((n_layers, ROWS, (PER_HALF - UP_BLOCKS) * COLS), f32), shape((seq, width), bf16)),
-        in_specs=[vmem] + [hbm] * len(saved),
-        out_specs=(vmem,) * 3,
-        scratch_shapes=scratch,
-        compiler_params=pltpu.CompilerParams(collective_id=0, has_side_effects=True,
-                                             vmem_limit_bytes=VMEM_LIMIT),
-    )(g_loc, *saved)
+        functools.partial(train_kernel, n_layers), name="train_stack",
+        out_shape=(shape((seq, width), bf16), shape((seq, width), bf16), shape((2, n_layers, ROWS // 2, UP_END), f32),
+                   shape((n_layers, ROWS, PER_HALF * COLS), f32)) + saved,
+        in_specs=[vmem] * 4, out_specs=(vmem,) * 4 + (hbm,) * len(saved), scratch_shapes=scratch,
+        compiler_params=pltpu.CompilerParams(collective_id=0, has_side_effects=True, vmem_limit_bytes=VMEM_LIMIT),
+    )(x_loc, g_loc, rows, down)[:4]
 
 
 LANES = 128
@@ -874,7 +886,7 @@
     for part in COLORS:
         used = min(ROWS, block - ROWS * part)
         for layer in range(layers):
-            down_out[ROWS * part:ROWS * part + used, layer, :] = down_ref[layer, :used, _span(part, width)]
+            down_out[ROWS * part:ROWS * part + used, layer, :] = down_ref[layer, :used, UP_END + width * part:UP_END + width * part + width]
     y_out[ALL] = y_ref[ALL]
     dx_out[ALL] = dx_ref[ALL]
 
@@ -907,8 +919,7 @@
         weights = (w_q, w_k, w_v, w_o, w_up, w_down)
         chips = w_up.shape[2] // w_down.shape[1] // 2
         rows, down = pack_weights(*weights, chips)
-        y_loc, acts, *saved = forward_stack(x_in[0], rows, down)
-        row_grad, down_grad, grad_x = backward_stack(w_q.shape[0], grad_out[0], x_in[0], acts, *saved)
+        y_loc, grad_x, row_grad, down_grad = train_stack(x_in[0], grad_out[0], rows, down)
         return unpack_grads(row_grad, down_grad, y_loc, grad_x, [weight.shape for weight in weights], chips)
 
     return jax.shard_map(body, mesh=mesh4, in_specs=(row_spec,) + (weight_spec,) * 6 + (row_spec,),

time: 553 us -> 546 us (0.987)
  Pallas kernels: 552 us -> 546 us
    pallas_call x2 -> x1, Pallas kernels: 541 us -> 534 us  [train_stack(): pl.pallas_call(functools.partial(train_kernel, n_layers), name='train_sta...]
where the time goes in v8:
time: 546 us
  Pallas kernels  546 us (100%)
    pallas_call x1, Pallas kernels, train_stack(): pl.pallas_call(functools.partial(train_kernel, n_layers), name='train_sta...  534 us

profile of v8, /device:TPU:1, one launch (start us, length us, event | category | flops | bytes accessed | tf_op | source)
XLA Modules:
  0.0 546.3 jit_solution(9163186644998827826)
XLA Ops:
  0.6 5.4 pack_weights.1
  6.0 534.0 %train_stack.1 = (bf16[192,1536]{1,0:T(8,128)(2,1)}, bf16[192,1536]{1,0:T(8,128)(2,1)}, f32[2,2,12,6400]{3,2,1,0:T(8,128)}, f32[2,24,11008]{2,1,0:T(8,128)}, bf1...) custom-call(bf16[192,1536]{1,0:T(8,128)(2,1)} %bitcast.12, ...), custom_call_target="tpu_custom_call" | custom-call | tf_op jit(solution)/shard_map/train_stack/pallas_call | solution.py:763
  540.0 6.3 %unpack_grads.1 = (f32[12,12,2,128]{3,2,1,0:T(2,128)}, f32[2,12,2,128]{3,2,1,0:T(2,128)}, f32[2,12,2,128]{3,2,1,0:T(2,128)}, f32[12,12,2,128]{3,2,1,0:T(2,128)},...) custom-call(f32[2,2,12,6400]{3,2,1,0:T(8,128)} %get-tuple-element.24.ro, ...), custom_call_target="tpu_custom_call" | custom-call | tf_op jit(solution)/shard_map/unpack_grads/pallas_call | solution.py:901

commit v9 on v8

--- a/solution.py
+++ b/solution.py
@@ -37,6 +37,7 @@
 
 
 FIFTH = UP_END // 5
+GATHER_SLOTS = 6 * LAG + 4
 
 
 def _rows(color):
@@ -139,10 +140,10 @@
                   hid_sem, twin_sem):
     acts, w_out, hid_out, gelu_out, norm_out, q_out, k_out, v_out, o_out = saved
     core, place, near = torus.core, torus.place, torus.near
-    slots = wbuf.shape[0]
+    slots = GATHER_SLOTS
     n_chunks = n_layers * PER_HALF
     ready = 6 * LAG
-    seq = x_ref.shape[0]
+    seq = state.shape[0]
     third = 64 * ROWS
     last = n_layers - 1
     swap = torus.remote(rows_ref.at[1 - core], twin, twin_sem.at[0], twin_sem.at[1], torus.sibling)
@@ -355,7 +356,7 @@
 
             @pl.when(layer == last)
             def _():
-                y_ref[ALL] = result
+                pltpu.make_async_copy(state, y_ref, save_sem.at[9]).start()
 
         keep_copy(chunk).wait()
 
@@ -365,7 +366,7 @@
 
 
 def backward_steps(torus, n_layers, g_ref, x_ref, dx_ref, saved, out, wbuf, lefts, rights, hid_buf, dact, dnorm, q_buf,
-                   k_buf, v_buf, x_mid, x_in, dk_acc, dv_acc, sums, half_bufs, full_bufs, load_sem, own_sem, push_send,
+                   k_buf, v_buf, x_buf, dk_acc, dv_acc, sums, half_bufs, full_bufs, load_sem, own_sem, push_send,
                    push_recv, pair_send, pair_recv, ring_send, ring_recv):
     acts, w_own, hid_in, gelu_in, norm_in, q_in, k_in, v_in, o_in = saved
     place, near = torus.place, torus.near
@@ -374,16 +375,17 @@
     last = n_layers - 1
 
     def mine_slot(chunk):
-        return 6 * _rem(chunk, 2)
+        return GATHER_SLOTS + _rem(chunk, 2)
 
     def out_slot(chunk):
-        return 7 + _rem(chunk, 2)
+        return GATHER_SLOTS + 2 + _rem(chunk, 2)
 
     def their_slot(chunk):
-        return 9 + _rem(chunk, SLOTS)
+        return 7 + _rem(chunk, SLOTS)
 
     def peer_slot(chunk):
-        return 12 + _rem(chunk, RING)
+        order = _rem(chunk, RING)
+        return jnp.where(order == 0, 6, jnp.where(order == 3, 10, GATHER_SLOTS + 3 + order))
 
     def pair_of(chunk):
         return last - chunk // PER_HALF
@@ -399,8 +401,7 @@
             return {"a": (gelu_in.at[pair], lefts.at[0:6], 0), "n_mlp": (norm_in.at[pair, 1], lefts.at[NORM_MLP], 1),
                     "n_attn": (norm_in.at[pair, 0], lefts.at[NORM_ATTN], 2), "o": (o_in.at[pair], rights.at[O_AT:QKV_AT], 3),
                     "q": (q_in.at[pair], q_buf, 4), "k": (k_in.at[pair], k_buf, 5), "v": (v_in.at[pair], v_buf, 6),
-                    "x_mid": (acts.at[2 * pair], x_mid, 7), "h0": (hid_in.at[pair, 0], hid_buf, 8),
-                    "h1": (hid_in.at[pair, 1], hid_buf, 8), "h2": (hid_in.at[pair, 2], hid_buf, 8)}[name]
+                    "x_mid": (acts.at[2 * pair], x_buf, 7)}[name]
         return [pltpu.make_async_copy(source(name)[0], source(name)[1], load_sem.at[source(name)[2]])
                 for name in names]
 
@@ -413,10 +414,10 @@
             copy.wait()
 
     def first_input(ref):
-        return pltpu.make_async_copy(ref, x_in, load_sem.at[9])
-
-    for block in SIX:
-        rights[block] = g_ref[:, COLS * block:COLS * block + COLS]
+        return pltpu.make_async_copy(ref, x_buf, load_sem.at[9])
+
+    def hidden_load(pair, part, half):
+        return pltpu.make_async_copy(hid_in.at[pair, part, half], hid_buf, load_sem.at[8])
 
     def own_copy(chunk):
         return pltpu.make_async_copy(w_own.at[pair_of(chunk), :, :, :, :, columns(chunk)], wbuf.at[mine_slot(chunk)],
@@ -446,28 +447,30 @@
 
         @pl.when(index == 0)
         def _():
-            start(pair, ["x_mid", "h0"])
+            start(pair, ["x_mid"])
 
             @pl.when(pair < last)
             def _():
                 start(pair, ["n_mlp", "n_attn", "o", "q", "k", "v"])
 
-            @pl.when(pair == 0)
-            def _():
-                x_in[ALL] = x_ref[ALL]
-
-            @pl.when(pair > 0)
-            def _():
-                first_input(acts.at[2 * pair - 1]).start()
-
-        for part in (1, 2):
-            @pl.when(index == 6 * part)
-            def _(part=part):
-                start(pair, [f"h{part}"])
+        def bend_back(part, half):
+            hidden_load(pair, part, half).wait()
+            for block in SIX:
+                cols = slice(COLS * block, COLS * block + COLS)
+                hidden = hid_buf[:, cols]
+                bend = jnp.tanh(0.7978845608028654 * (hidden + 0.044715 * (hidden * hidden * hidden)))
+                slope = 0.5 * (1.0 + bend) + 0.5 * hidden * (1.0 - bend * bend) * (
+                    0.7978845608028654 * (1.0 + 0.134145 * (hidden * hidden)))
+                rights[DH_AT + FF * half + 6 * part + block] = (dact[half, :, cols] * slope).astype(jnp.bfloat16)
+
+        @pl.when((index > 0) & (index <= DOWN_DONE) & (_rem(index, 6) == 0))
+        def _():
+            bend_back(index // 6 - 1, 1)
 
         @pl.when((index < DOWN_DONE) & (_rem(index, 6) == 0))
         def _():
             dact[ALL] = jnp.zeros_like(dact)
+            hidden_load(pair, index // 6, 0).start()
 
         @pl.when(index < DOWN_DONE)
         def _():
@@ -476,15 +479,8 @@
 
         @pl.when((index < DOWN_DONE) & (_rem(index, 6) == 5))
         def _():
-            finish(pair, ["h0"])
-            for half in TWO:
-                for block in SIX:
-                    cols = slice(COLS * block, COLS * block + COLS)
-                    hidden = hid_buf[half, :, cols]
-                    bend = jnp.tanh(0.7978845608028654 * (hidden + 0.044715 * (hidden * hidden * hidden)))
-                    slope = 0.5 * (1.0 + bend) + 0.5 * hidden * (1.0 - bend * bend) * (
-                        0.7978845608028654 * (1.0 + 0.134145 * (hidden * hidden)))
-                    rights[DH_AT + FF * half + index - 5 + block] = (dact[half, :, cols] * slope).astype(jnp.bfloat16)
+            bend_back(index // 6, 0)
+            hidden_load(pair, index // 6, 1).start()
 
         @pl.when(index == DOWN_DONE - 1)
         def _():
@@ -508,10 +504,17 @@
         @pl.when(index == UP_DONE - 1)
         def _():
             finish(pair, ["x_mid"])
-            lefts[GRAD] = (total_grad() + _rms_back(x_mid[ALL], dnorm[ALL])).astype(jnp.bfloat16)
+            lefts[GRAD] = (total_grad() + _rms_back(x_buf[ALL], dnorm[ALL])).astype(jnp.bfloat16)
 
         @pl.when(index == UP_DONE)
         def _():
+            @pl.when(pair == 0)
+            def _():
+                first_input(x_ref).start()
+
+            @pl.when(pair > 0)
+            def _():
+                first_input(acts.at[2 * pair - 1]).start()
             dk_acc[ALL] = jnp.zeros_like(dk_acc)
             dv_acc[ALL] = jnp.zeros_like(dv_acc)
 
@@ -550,11 +553,12 @@
 
         @pl.when(index == PER_HALF - 1)
         def _():
+            first_input(x_ref).wait()
+
             @pl.when(pair > 0)
             def _():
-                first_input(acts.at[2 * pair - 1]).wait()
                 finish(pair - 1, ["a"])
-            result = (lefts[GRAD].astype(jnp.float32) + _rms_back(x_in[ALL], dnorm[ALL])).astype(jnp.bfloat16)
+            result = (lefts[GRAD].astype(jnp.float32) + _rms_back(x_buf[ALL], dnorm[ALL])).astype(jnp.bfloat16)
             dx_ref[ALL] = result
             for block in SIX:
                 rights[block] = result[:, COLS * block:COLS * block + COLS]
@@ -681,8 +685,8 @@
 
 def train_kernel(n_layers, x_ref, g_ref, rows_ref, down_ref, y_ref, dx_ref, rows_out, out, *refs):
     saved, refs = refs[:9], refs[9:]
-    (wbuf, peer, shard, twin, state, lefts, rights, q_buf, k_buf, v_buf, hid_out_buf, acc, hid_in_buf, dact, x_mid, x_in,
-     dk_acc, dv_acc, away), refs = refs[:19], refs[19:]
+    (wbuf, peer, shard, twin, state, lefts, rights, q_buf, k_buf, v_buf, hid_out_buf, acc, hid_in_buf, dact, x_buf,
+     dk_acc, dv_acc, away), refs = refs[:18], refs[18:]
     sums, half_bufs, full_bufs, refs = refs[:3], refs[3:9], refs[9:15], refs[15:]
     half_bufs = [half_bufs[2 * stage:2 * stage + 2] for stage in COLORS]
     full_bufs = [full_bufs[2 * stage:2 * stage + 2] for stage in COLORS]
@@ -690,14 +694,20 @@
     torus = Torus(credit)
     core = torus.core
     n_chunks = n_layers * PER_HALF
-    state[ALL] = x_ref[ALL]
+    fill = pltpu.make_async_copy(x_ref, state, forward_sems[5].at[9])
+    fill.start()
+    for block in SIX:
+        pltpu.make_async_copy(g_ref.at[:, COLS * block:COLS * block + COLS], rights.at[block],
+                              backward_sems[0].at[3]).start()
     torus.meet()
+    fill.wait()
+    pltpu.make_async_copy(rights.at[0:6], rights.at[0:6], backward_sems[0].at[3]).wait()
     forward = forward_steps(torus, n_layers, x_ref, rows_ref, down_ref, y_ref, saved, wbuf, peer, shard, twin, state, lefts,
                             rights, q_buf, k_buf, v_buf, hid_out_buf, acc, *forward_sems)
     backward = backward_steps(torus, n_layers, g_ref, x_ref, dx_ref, saved, out, wbuf, lefts, rights, hid_in_buf, dact, acc,
-                              q_buf, k_buf, v_buf, x_mid, x_in, dk_acc, dv_acc, sums, half_bufs, full_bufs,
+                              q_buf, k_buf, v_buf, x_buf, dk_acc, dv_acc, sums, half_bufs, full_bufs,
                               *backward_sems)
-    turn_at = n_chunks + 8
+    turn_at = n_chunks
     backward = [(lag + turn_at, step) for lag, step in backward]
     n_ticks = turn_at + n_chunks + 7 * LAG
     half_rows = ROWS // 2
@@ -730,6 +740,7 @@
     swap = torus.remote(away, rows_out.at[core], swap_sem.at[0], swap_sem.at[1], torus.sibling)
     swap.wait_send()
     swap.wait_recv()
+    pltpu.make_async_copy(state, y_ref, forward_sems[5].at[9]).wait()
 
 
 def train_stack(x_loc, g_loc, rows, down):
@@ -748,23 +759,23 @@
              shape((n_layers, seq, 2 * HEAD), bf16), shape((n_layers, seq, 2 * HEAD), bf16),
              shape((n_layers, 6, seq, COLS), bf16))
     scratch = [pltpu.VMEM(full, kind) for full, kind in (
-        ((6 * LAG + 4,) + chunk, bf16), ((RING,) + chunk, bf16), ((n_layers, ROWS, PER_HALF * COLS), bf16),
+        ((GATHER_SLOTS + 6,) + chunk, bf16), ((RING,) + chunk, bf16), ((n_layers, ROWS, PER_HALF * COLS), bf16),
         (rows.shape[1:], bf16), ((seq, width), bf16), ((9, seq, width), bf16), ((56, seq, COLS), bf16),
         ((seq, 6 * COLS), bf16), ((seq, 2 * HEAD), bf16), ((seq, 2 * HEAD), bf16), ((2, 2, seq, COLS), f32),
-        ((seq, width), f32), ((2, seq, width), f32), ((2, seq, width), f32), ((seq, width), bf16), ((seq, width), bf16),
+        ((seq, width), f32), ((seq, width), f32), ((2, seq, width), f32), ((seq, width), bf16),
         ((2, seq, HEAD), f32), ((2, seq, HEAD), f32), ((n_layers, ROWS // 2, UP_END), f32), ((6,) + chunk, f32),
         ((5, 3, RING, RING, TILE, COLS), f32), ((5, 3, RING, TILE, COLS), f32))]
     for cols in (half, COLS):
         for size in ((RING, RING), (RING,), ()):
             scratch += [pltpu.VMEM((RING, 3, 2) + size + (TILE, cols), bf16)] * 2
-    scratch += [dma((6, RING)), dma((6, RING)), dma((RING,)), dma((RING,)), dma((RING,)), dma((9,)), dma((2, 2)), dma((2,))]
+    scratch += [dma((6, RING)), dma((6, RING)), dma((RING,)), dma((RING,)), dma((RING,)), dma((10,)), dma((2, 2)), dma((2,))]
     scratch += [dma((10,)), dma((2,)), dma((SLOTS,)), dma((SLOTS,)), dma((RING,)), dma((RING,)), dma((6, RING)),
                 dma((6, RING)), dma((2,)), pltpu.SemaphoreType.REGULAR((7,))]
     return pl.pallas_call(
         functools.partial(train_kernel, n_layers), name="train_stack",
         out_shape=(shape((seq, width), bf16), shape((seq, width), bf16), shape((2, n_layers, ROWS // 2, UP_END), f32),
                    shape((n_layers, ROWS, PER_HALF * COLS), f32)) + saved,
-        in_specs=[vmem] * 4, out_specs=(vmem,) * 4 + (hbm,) * len(saved), scratch_shapes=scratch,
+        in_specs=[hbm, hbm, vmem, vmem], out_specs=(hbm,) + (vmem,) * 3 + (hbm,) * len(saved), scratch_shapes=scratch,
         compiler_params=pltpu.CompilerParams(collective_id=0, has_side_effects=True, vmem_limit_bytes=VMEM_LIMIT),
     )(x_loc, g_loc, rows, down)[:4]
 

time: 546 us -> 534 us (0.978)
  Pallas kernels: 546 us -> 533 us
    pallas_call x1, Pallas kernels: 534 us -> 522 us  [train_stack(): pl.pallas_call(functools.partial(train_kernel, n_layers), name='train_sta...]
where the time goes in v9:
time: 534 us
  Pallas kernels  533 us (100%)
    pallas_call x1, Pallas kernels, train_stack(): pl.pallas_call(functools.partial(train_kernel, n_layers), name='train_sta...  522 us

profile of v9, /device:TPU:1, one launch (start us, length us, event | category | flops | bytes accessed | tf_op | source)
XLA Modules:
  0.0 533.9 jit_solution(5278678480668463316)
XLA Ops:
  0.6 5.4 %pack_weights.1 = (bf16[2,2,12,6400]{3,2,1,0:T(8,128)(2,1)}, bf16[2,24,4608]{2,1,0:T(8,128)(2,1)}) custom-call(bf16[12,12,2,128]{3,2,1,0:T(2,128)(2,1)} %bitcast.16, bf16[2,12,2,128]{3,2,1,0:T(2,128)(2,1)} %k_ref.1, bf16[2,12,2,128]{3,2,1,0:T(2,128)(2,1)} %v_ref.1, bf16[12,12,2,128]{3,2,1,0:T(2,128)(2,1)} %bitcast.17, bf16[12,2,8960]{2,1,0:T(2,128)(2,1)} %bitcast.14, ...), custom_call_target="tpu_custom_call" | custom-call | tf_op jit(solution)/shard_map/pack_weights/pallas_call | solution.py:864
  6.0 521.7 %train_stack.1 = (bf16[192,1536]{1,0:T(8,128)(2,1)}, bf16[192,1536]{1,0:T(8,128)(2,1)}, f32[2,2,12,6400]{3,2,1,0:T(8,128)}, f32[2,24,11008]{2,1,0:T(8,128)}, bf1...) custom-call(bf16[192,1536]{1,0:T(8,128)(2,1)} %bitcast.12, ...), custom_call_target="tpu_custom_call" | custom-call | tf_op jit(solution)/shard_map/train_stack/pallas_call | solution.py:774
  527.7 6.3 %unpack_grads.1 = (f32[12,12,2,128]{3,2,1,0:T(2,128)}, f32[2,12,2,128]{3,2,1,0:T(2,128)}, f32[2,12,2,128]{3,2,1,0:T(2,128)}, f32[12,12,2,128]{3,2,1,0:T(2,128)},...) custom-call(f32[2,2,12,6400]{3,2,1,0:T(8,128)} %get-tuple-element.24.ro, ...), custom_call_target="tpu_custom_call" | custom-call | tf_op jit(solution)/shard_map/unpack_grads/pallas_call | solution.py:912

commit v10 on v9

--- a/solution.py
+++ b/solution.py
@@ -16,12 +16,17 @@
 COLS = 256
 ROWS = 24
 LAG = 2
+WIDE = COLS // 2
+HALF_ROWS = ROWS // 2
 HEAD = 128
 PER_HALF = 43
 UP_BLOCKS = 25
 UP_END = UP_BLOCKS * COLS
 RING = 4
+STAGES = 3
+FINAL = STAGES - 1
 CUBE = (RING, RING, RING)
+CHIPS = RING ** STAGES
 SLOTS = 3
 TILE = 8
 COLORS = range(3)
@@ -30,14 +35,19 @@
 ALL = Ellipsis
 EVERY = slice(None)
 QKV, ATTN, FF = 4, 7, 18
-DOWN_DONE, UP_DONE, O_DONE = 18, 36, 39
-G_AT, DH_AT, O_AT, QKV_AT = 0, 6, 42, 48
+DOWN_DONE = FF
+UP_DONE = DOWN_DONE + FF
+O_DONE = UP_DONE + ATTN - QKV
+SIXTH = 6
+DH_AT = SIXTH
+O_AT = DH_AT + UP_DONE
+QKV_AT = O_AT + SIXTH
 NORM_MLP, GRAD, NORM_ATTN = 6, 7, 8
 VMEM_LIMIT = 67043328
 
 
 FIFTH = UP_END // 5
-GATHER_SLOTS = 6 * LAG + 4
+GATHER_SLOTS = SIXTH * LAG + RING
 
 
 def _rows(color):
@@ -94,8 +104,8 @@
     def __init__(self, credit):
         self.core = lax.axis_index("c")
         self.place = {dim: lax.axis_index(dim) for dim in DIMS}
-        self.near = tuple({dim: _rem(self.place[dim] + step, 4) for dim in DIMS} for step in (1, 3))
-        self.far = {dim: _rem(self.place[dim] + 2, 4) for dim in DIMS}
+        self.near = tuple({dim: _rem(self.place[dim] + step, RING) for dim in DIMS} for step in (1, 3))
+        self.far = {dim: _rem(self.place[dim] + 2, RING) for dim in DIMS}
         self.sibling = {"c": 1 - self.core}
         self.sides = ((0, self.core), (1, 1 - self.core))
         self.credit = credit
@@ -142,9 +152,9 @@
     core, place, near = torus.core, torus.place, torus.near
     slots = GATHER_SLOTS
     n_chunks = n_layers * PER_HALF
-    ready = 6 * LAG
+    ready = SIXTH * LAG
     seq = state.shape[0]
-    third = 64 * ROWS
+    third = CHIPS * ROWS
     last = n_layers - 1
     swap = torus.remote(rows_ref.at[1 - core], twin, twin_sem.at[0], twin_sem.at[1], torus.sibling)
     swap.start()
@@ -173,7 +183,7 @@
                       for dim in DIMS)
         return wbuf.at[(slot,) + index + (_rows(color), cols)]
 
-    halves = (slice(0, COLS // 2), slice(COLS // 2, COLS))
+    halves = (slice(0, WIDE), slice(WIDE, COLS))
 
     def send_own(stage, chunk):
         slot, sem = _rem(chunk, slots), _rem(chunk, RING)
@@ -198,8 +208,8 @@
 
     def arrived(part, chunk):
         slot, sem = _rem(chunk, slots), _rem(chunk, RING)
-        block = (wbuf.at[slot, 0, 0, 0:2], wbuf.at[slot, 0, 0, 0], wbuf.at[slot, 0, 0:2], wbuf.at[slot, 0, 0],
-                 wbuf.at[slot, 0:2], wbuf.at[slot, 0])[part]
+        count = slice(0, 2) if part % 2 == 0 else 0
+        block = wbuf.at[(slot,) + (0,) * (2 - part // 2) + (count,)]
         whole = torus.remote(block, block, ring_send.at[part, sem], ring_recv.at[part, sem], torus.sibling)
         whole.wait_send()
         whole.wait_recv()
@@ -230,11 +240,12 @@
                                      keep_sem.at[_rem(chunk, RING)])
 
     def save_copies(layer, names):
-        parts = {"n0": (lefts.at[NORM_ATTN], norm_out.at[layer, 0], 0), "n1": (lefts.at[NORM_MLP], norm_out.at[layer, 1], 1),
-                 "q": (q_buf, q_out.at[layer], 2), "k": (k_buf, k_out.at[layer], 3), "v": (v_buf, v_out.at[layer], 4),
-                 "o": (rights.at[O_AT:QKV_AT], o_out.at[layer], 5), "a": (lefts.at[0:6], gelu_out.at[layer], 6),
-                 "mid": (state, acts.at[2 * layer], 7), "end": (state, acts.at[2 * layer + 1], 8)}
-        return [pltpu.make_async_copy(parts[name][0], parts[name][1], save_sem.at[parts[name][2]]) for name in names]
+        parts = {"n0": (lefts.at[NORM_ATTN], norm_out.at[layer, 0]), "n1": (lefts.at[NORM_MLP], norm_out.at[layer, 1]),
+                 "q": (q_buf, q_out.at[layer]), "k": (k_buf, k_out.at[layer]), "v": (v_buf, v_out.at[layer]),
+                 "o": (rights.at[O_AT:QKV_AT], o_out.at[layer]), "a": (lefts.at[:NORM_MLP], gelu_out.at[layer]),
+                 "mid": (state, acts.at[2 * layer]), "end": (state, acts.at[2 * layer + 1])}
+        places = list(parts)
+        return [pltpu.make_async_copy(*parts[name], save_sem.at[places.index(name)]) for name in names]
 
     def save(layer, names):
         @pl.when(layer < last)
@@ -249,7 +260,7 @@
                 copy.wait()
 
     def hidden_copies(layer, order):
-        slot, part, at = _rem(order, 2), order // 6, _at(_rem(order, 6) * COLS, COLS)
+        slot, part, at = _rem(order, 2), order // SIXTH, _at(_rem(order, SIXTH) * COLS, COLS)
         return [pltpu.make_async_copy(hid_buf.at[slot, half], hid_out.at[layer, part, half, :, at],
                                       hid_sem.at[slot, half]) for half in TWO]
 
@@ -272,7 +283,7 @@
         @pl.when(index < 3)
         def _():
             for role, half in torus.sides:
-                q_buf[:, _at(3 * COLS * half + COLS * index, COLS)] = _dot(
+                q_buf[:, _at(STAGES * COLS * half + COLS * index, COLS)] = _dot(
                     lefts[NORM_ATTN], weights(role)).astype(jnp.bfloat16)
 
         @pl.when(index == 3)
@@ -294,11 +305,11 @@
                 key, value = k_buf[:, _at(HEAD * half, HEAD)], v_buf[:, _at(HEAD * half, HEAD)]
                 outs = []
                 for head in TWO:
-                    at = _at(3 * COLS * half + COLS * (index - QKV) + HEAD * head, HEAD)
+                    at = _at(STAGES * COLS * half + COLS * (index - QKV) + HEAD * head, HEAD)
                     prob = _probs(q_buf[:, at], key, causal)
                     outs.append(_dot(prob.astype(jnp.bfloat16), value).astype(jnp.bfloat16))
                 block = jnp.concatenate(outs, axis=1)
-                rights[O_AT + 3 * half + index - QKV] = block
+                rights[O_AT + STAGES * half + index - QKV] = block
                 acc[ALL] += _dot_rhs_t(block, weights(role))
 
         @pl.when(index == ATTN - 1)
@@ -324,7 +335,7 @@
             for role, half in torus.sides:
                 hidden = _dot(lefts[NORM_MLP], weights(role))
                 hid_buf[_rem(order, 2), half] = hidden
-                lefts[3 * half + order // 6, :, _at(COLS * _rem(order, 6), COLS)] = jax.nn.gelu(
+                lefts[STAGES * half + order // SIXTH, :, _at(COLS * _rem(order, SIXTH), COLS)] = jax.nn.gelu(
                     hidden).astype(jnp.bfloat16)
             for copy in hidden_copies(layer, order):
                 copy.start()
@@ -336,8 +347,8 @@
 
         @pl.when(index >= UP_BLOCKS)
         def _():
-            part, at = (index - UP_BLOCKS) // 6, _at(COLS * _rem(index - UP_BLOCKS, 6), COLS)
-            total = sum(_dot(lefts[3 * half + part], weights(role)) for role, half in torus.sides)
+            part, at = (index - UP_BLOCKS) // SIXTH, _at(COLS * _rem(index - UP_BLOCKS, SIXTH), COLS)
+            total = sum(_dot(lefts[STAGES * half + part], weights(role)) for role, half in torus.sides)
 
             @pl.when(part == 0)
             def _():
@@ -365,13 +376,13 @@
     return steps + [(ready, exchange), (ready + 1, compute)]
 
 
-def backward_steps(torus, n_layers, g_ref, x_ref, dx_ref, saved, out, wbuf, lefts, rights, hid_buf, dact, dnorm, q_buf,
+def backward_steps(torus, n_layers, x_ref, x_out, saved, out, wbuf, lefts, rights, hid_buf, dact, dnorm, q_buf,
                    k_buf, v_buf, x_buf, dk_acc, dv_acc, sums, half_bufs, full_bufs, load_sem, own_sem, push_send,
                    push_recv, pair_send, pair_recv, ring_send, ring_recv):
     acts, w_own, hid_in, gelu_in, norm_in, q_in, k_in, v_in, o_in = saved
     place, near = torus.place, torus.near
-    seq = g_ref.shape[0]
-    third = 64 * ROWS
+    seq = k_buf.shape[0]
+    third = CHIPS * ROWS
     last = n_layers - 1
 
     def mine_slot(chunk):
@@ -397,13 +408,12 @@
         return _at(block * COLS, COLS)
 
     def loads(pair, names):
-        def source(name):
-            return {"a": (gelu_in.at[pair], lefts.at[0:6], 0), "n_mlp": (norm_in.at[pair, 1], lefts.at[NORM_MLP], 1),
-                    "n_attn": (norm_in.at[pair, 0], lefts.at[NORM_ATTN], 2), "o": (o_in.at[pair], rights.at[O_AT:QKV_AT], 3),
-                    "q": (q_in.at[pair], q_buf, 4), "k": (k_in.at[pair], k_buf, 5), "v": (v_in.at[pair], v_buf, 6),
-                    "x_mid": (acts.at[2 * pair], x_buf, 7)}[name]
-        return [pltpu.make_async_copy(source(name)[0], source(name)[1], load_sem.at[source(name)[2]])
-                for name in names]
+        parts = {"a": (gelu_in.at[pair], lefts.at[:NORM_MLP]), "n_mlp": (norm_in.at[pair, 1], lefts.at[NORM_MLP]),
+                 "n_attn": (norm_in.at[pair, 0], lefts.at[NORM_ATTN]), "o": (o_in.at[pair], rights.at[O_AT:QKV_AT]),
+                 "q": (q_in.at[pair], q_buf), "k": (k_in.at[pair], k_buf), "v": (v_in.at[pair], v_buf),
+                 "x_mid": (acts.at[2 * pair], x_buf)}
+        places = list(parts)
+        return [pltpu.make_async_copy(*parts[name], load_sem.at[places.index(name)]) for name in names]
 
     def start(pair, names):
         for copy in loads(pair, names):
@@ -461,26 +471,26 @@
                 bend = jnp.tanh(0.7978845608028654 * (hidden + 0.044715 * (hidden * hidden * hidden)))
                 slope = 0.5 * (1.0 + bend) + 0.5 * hidden * (1.0 - bend * bend) * (
                     0.7978845608028654 * (1.0 + 0.134145 * (hidden * hidden)))
-                rights[DH_AT + FF * half + 6 * part + block] = (dact[half, :, cols] * slope).astype(jnp.bfloat16)
-
-        @pl.when((index > 0) & (index <= DOWN_DONE) & (_rem(index, 6) == 0))
-        def _():
-            bend_back(index // 6 - 1, 1)
-
-        @pl.when((index < DOWN_DONE) & (_rem(index, 6) == 0))
+                rights[DH_AT + FF * half + SIXTH * part + block] = (dact[half, :, cols] * slope).astype(jnp.bfloat16)
+
+        @pl.when((index > 0) & (index <= DOWN_DONE) & (_rem(index, SIXTH) == 0))
+        def _():
+            bend_back(index // SIXTH - 1, 1)
+
+        @pl.when((index < DOWN_DONE) & (_rem(index, SIXTH) == 0))
         def _():
             dact[ALL] = jnp.zeros_like(dact)
-            hidden_load(pair, index // 6, 0).start()
+            hidden_load(pair, index // SIXTH, 0).start()
 
         @pl.when(index < DOWN_DONE)
         def _():
             for role, half in torus.sides:
-                dact[half] += _dot_rhs_t(rights[_rem(index, 6)], weights(role))
-
-        @pl.when((index < DOWN_DONE) & (_rem(index, 6) == 5))
-        def _():
-            bend_back(index // 6, 0)
-            hidden_load(pair, index // 6, 1).start()
+                dact[half] += _dot_rhs_t(rights[_rem(index, SIXTH)], weights(role))
+
+        @pl.when((index < DOWN_DONE) & (_rem(index, SIXTH) == 5))
+        def _():
+            bend_back(index // SIXTH, 0)
+            hidden_load(pair, index // SIXTH, 1).start()
 
         @pl.when(index == DOWN_DONE - 1)
         def _():
@@ -526,7 +536,7 @@
                 key, value = k_buf[:, _at(HEAD * half, HEAD)], v_buf[:, _at(HEAD * half, HEAD)]
                 d_q = []
                 for head in TWO:
-                    query = q_buf[:, _at(3 * COLS * half + COLS * (index - UP_DONE) + HEAD * head, HEAD)]
+                    query = q_buf[:, _at(STAGES * COLS * half + COLS * (index - UP_DONE) + HEAD * head, HEAD)]
                     d_head = d_o[:, HEAD * head:HEAD * head + HEAD]
                     prob = _probs(query, key, causal)
                     d_prob = _dot_rhs_t(d_head, value)
@@ -559,7 +569,10 @@
             def _():
                 finish(pair - 1, ["a"])
             result = (lefts[GRAD].astype(jnp.float32) + _rms_back(x_buf[ALL], dnorm[ALL])).astype(jnp.bfloat16)
-            dx_ref[ALL] = result
+
+            @pl.when(pair == 0)
+            def _():
+                x_out(result)
             for block in SIX:
                 rights[block] = result[:, COLS * block:COLS * block + COLS]
 
@@ -573,11 +586,11 @@
         lead = _rem(chunk, sums[0].shape[0])
         quarter = third // RING
         for role, half in torus.sides[::-1]:
-            left = jnp.where(index < DOWN_DONE, 3 * half + index // 6,
+            left = jnp.where(index < DOWN_DONE, STAGES * half + index // SIXTH,
                              jnp.where(index < UP_DONE, NORM_MLP, jnp.where(index < O_DONE, GRAD, NORM_ATTN)))
-            right = jnp.where(index < DOWN_DONE, _rem(index, 6),
+            right = jnp.where(index < DOWN_DONE, _rem(index, SIXTH),
                               jnp.where(index < UP_DONE, DH_AT + FF * half + index - DOWN_DONE,
-                                        jnp.where(index < O_DONE, O_AT + 3 * half + index - UP_DONE,
+                                        jnp.where(index < O_DONE, O_AT + STAGES * half + index - UP_DONE,
                                                   QKV_AT + QKV * half + index - O_DONE)))
             for z in range(RING):
                 part = _dot_lhs_t(lefts[left, :, quarter * z:quarter * z + quarter], rights[right])
@@ -615,7 +628,7 @@
             return sums[0][(lead,) + _block(color, 0, position) + (_rows(color), cols)]
         return sums[stage][(lead, color) + _block(color, stage, position) + (EVERY, cols)]
 
-    left_cols, right_cols, every = slice(0, COLS // 2), slice(COLS // 2, COLS), slice(0, COLS)
+    left_cols, right_cols, every = slice(0, WIDE), slice(WIDE, COLS), slice(0, COLS)
 
     def store_halves(stage, chunk):
         slot = _rem(chunk, RING)
@@ -679,18 +692,19 @@
 
     return [(0, fetch), (2 * LAG, functools.partial(middle, 0)), (LAG, open_first),
             (3 * LAG, functools.partial(turn, 0)), (4 * LAG, functools.partial(middle, 1)),
-            (5 * LAG, functools.partial(turn, 1)), (6 * LAG, functools.partial(middle, 2)),
+            (5 * LAG, functools.partial(turn, 1)), (SIXTH * LAG, functools.partial(middle, 2)),
             (7 * LAG, functools.partial(turn, 2)), (1, consume), (0, multiply)]
 
 
-def train_kernel(n_layers, x_ref, g_ref, rows_ref, down_ref, y_ref, dx_ref, rows_out, out, *refs):
+def train_kernel(n_layers, x_ref, g_ref, rows_ref, down_ref, y_ref, dx_ref, rows_hbm, down_hbm, *refs):
     saved, refs = refs[:9], refs[9:]
+    (rows_out, out), refs = refs[:2], refs[2:]
     (wbuf, peer, shard, twin, state, lefts, rights, q_buf, k_buf, v_buf, hid_out_buf, acc, hid_in_buf, dact, x_buf,
      dk_acc, dv_acc, away), refs = refs[:18], refs[18:]
     sums, half_bufs, full_bufs, refs = refs[:3], refs[3:9], refs[9:15], refs[15:]
     half_bufs = [half_bufs[2 * stage:2 * stage + 2] for stage in COLORS]
     full_bufs = [full_bufs[2 * stage:2 * stage + 2] for stage in COLORS]
-    forward_sems, backward_sems, (swap_sem, credit) = refs[:8], refs[8:16], refs[16:]
+    forward_sems, backward_sems, (swap_sem, end_sem, credit) = refs[:8], refs[8:16], refs[16:]
     torus = Torus(credit)
     core = torus.core
     n_chunks = n_layers * PER_HALF
@@ -701,34 +715,63 @@
                               backward_sems[0].at[3]).start()
     torus.meet()
     fill.wait()
-    pltpu.make_async_copy(rights.at[0:6], rights.at[0:6], backward_sems[0].at[3]).wait()
+    pltpu.make_async_copy(rights.at[:DH_AT], rights.at[:DH_AT], backward_sems[0].at[3]).wait()
+    def y_copy():
+        return pltpu.make_async_copy(state, y_ref, forward_sems[5].at[9])
+
+    def x_out(result):
+        y_copy().wait()
+        state[ALL] = result
+        pltpu.make_async_copy(state, dx_ref, forward_sems[5].at[9]).start()
+
     forward = forward_steps(torus, n_layers, x_ref, rows_ref, down_ref, y_ref, saved, wbuf, peer, shard, twin, state, lefts,
                             rights, q_buf, k_buf, v_buf, hid_out_buf, acc, *forward_sems)
-    backward = backward_steps(torus, n_layers, g_ref, x_ref, dx_ref, saved, out, wbuf, lefts, rights, hid_in_buf, dact, acc,
+    backward = backward_steps(torus, n_layers, x_ref, x_out, saved, out, wbuf, lefts, rights, hid_in_buf, dact, acc,
                               q_buf, k_buf, v_buf, x_buf, dk_acc, dv_acc, sums, half_bufs, full_bufs,
                               *backward_sems)
     turn_at = n_chunks
     backward = [(lag + turn_at, step) for lag, step in backward]
     n_ticks = turn_at + n_chunks + 7 * LAG
-    half_rows = ROWS // 2
     tail = 2
 
     def hand_over(layer, part):
         cols = _at(part * FIFTH, FIFTH)
         both = out[layer, :, cols]
-        low, high = both[:half_rows], both[half_rows:]
+        low, high = both[:HALF_ROWS], both[HALF_ROWS:]
         rows_out[core, layer, :, cols] = jnp.where(core == 0, low, high)
         away[layer, :, cols] = jnp.where(core == 0, high, low)
-        torus.remote(away.at[layer, :, cols], rows_out.at[core, layer, :, cols], swap_sem.at[0], swap_sem.at[1],
-                     torus.sibling).start()
+        torus.remote(away.at[layer, :, cols], rows_out.at[core, layer, :, cols], swap_sem.at[0, layer],
+                     swap_sem.at[1, layer], torus.sibling).start()
+
+    def down_result(layer):
+        return pltpu.make_async_copy(out.at[layer, :, UP_END:], down_hbm.at[layer], end_sem.at[0, layer])
+
+    def rows_result(layer):
+        return pltpu.make_async_copy(rows_out.at[:, layer], rows_hbm.at[:, layer], end_sem.at[1, layer])
+
+    def rows_meet(layer):
+        swap = torus.remote(away.at[layer], rows_out.at[core, layer], swap_sem.at[0, layer], swap_sem.at[1, layer],
+                            torus.sibling)
+        swap.wait_send()
+        swap.wait_recv()
+        rows_result(layer).start()
 
     def hand_on(now):
-        for layer in range(1, n_layers):
+        for layer in range(n_layers):
             begin = turn_at + (n_layers - layer) * PER_HALF + 8 * LAG
 
-            @pl.when((now >= begin) & (now < begin + 5))
-            def _(layer=layer, begin=begin):
-                hand_over(layer, now - begin)
+            @pl.when(now == begin - UP_BLOCKS)
+            def _(layer=layer):
+                down_result(layer).start()
+
+            if layer > 0:
+                @pl.when((now >= begin) & (now < begin + 5))
+                def _(layer=layer, begin=begin):
+                    hand_over(layer, now - begin)
+
+                @pl.when(now == begin + 8)
+                def _(layer=layer):
+                    rows_meet(layer)
 
         @pl.when(now >= n_ticks - 5 + tail)
         def _():
@@ -737,45 +780,46 @@
     torus.run(backward[:1] + forward + backward[1:], n_chunks, n_ticks, hand_on)
     for part in range(tail):
         hand_over(0, part)
-    swap = torus.remote(away, rows_out.at[core], swap_sem.at[0], swap_sem.at[1], torus.sibling)
-    swap.wait_send()
-    swap.wait_recv()
-    pltpu.make_async_copy(state, y_ref, forward_sems[5].at[9]).wait()
+    rows_meet(0)
+    for layer in range(n_layers):
+        _all_done([down_result(layer), rows_result(layer)])
+    pltpu.make_async_copy(state, dx_ref, forward_sems[5].at[9]).wait()
 
 
 def train_stack(x_loc, g_loc, rows, down):
     n_layers = down.shape[0]
     seq, width = x_loc.shape
     bf16, f32 = jnp.bfloat16, jnp.float32
-    half = COLS // 2
+    half = WIDE
     chunk = CUBE + (ROWS, COLS)
     shape = jax.ShapeDtypeStruct
     hbm = pl.BlockSpec(memory_space=pl.ANY)
     vmem = pl.BlockSpec(memory_space=pltpu.VMEM)
     dma = pltpu.SemaphoreType.DMA
     saved = (shape((2 * n_layers - 1, seq, width), bf16), shape((n_layers,) + CUBE + (ROWS, PER_HALF * COLS), bf16),
-             shape((n_layers, 3, 2, seq, width), f32), shape((n_layers, 6, seq, width), bf16),
+             shape((n_layers, 3, 2, seq, width), f32), shape((n_layers, SIXTH, seq, width), bf16),
              shape((n_layers, 2, seq, width), bf16), shape((n_layers, seq, width), bf16),
              shape((n_layers, seq, 2 * HEAD), bf16), shape((n_layers, seq, 2 * HEAD), bf16),
-             shape((n_layers, 6, seq, COLS), bf16))
+             shape((n_layers, SIXTH, seq, COLS), bf16))
     scratch = [pltpu.VMEM(full, kind) for full, kind in (
+        ((2, n_layers, HALF_ROWS, UP_END), f32), ((n_layers, ROWS, PER_HALF * COLS), f32),
         ((GATHER_SLOTS + 6,) + chunk, bf16), ((RING,) + chunk, bf16), ((n_layers, ROWS, PER_HALF * COLS), bf16),
         (rows.shape[1:], bf16), ((seq, width), bf16), ((9, seq, width), bf16), ((56, seq, COLS), bf16),
-        ((seq, 6 * COLS), bf16), ((seq, 2 * HEAD), bf16), ((seq, 2 * HEAD), bf16), ((2, 2, seq, COLS), f32),
+        ((seq, SIXTH * COLS), bf16), ((seq, 2 * HEAD), bf16), ((seq, 2 * HEAD), bf16), ((2, 2, seq, COLS), f32),
         ((seq, width), f32), ((seq, width), f32), ((2, seq, width), f32), ((seq, width), bf16),
-        ((2, seq, HEAD), f32), ((2, seq, HEAD), f32), ((n_layers, ROWS // 2, UP_END), f32), ((6,) + chunk, f32),
+        ((2, seq, HEAD), f32), ((2, seq, HEAD), f32), ((n_layers, HALF_ROWS, UP_END), f32), ((6,) + chunk, f32),
         ((5, 3, RING, RING, TILE, COLS), f32), ((5, 3, RING, TILE, COLS), f32))]
     for cols in (half, COLS):
         for size in ((RING, RING), (RING,), ()):
             scratch += [pltpu.VMEM((RING, 3, 2) + size + (TILE, cols), bf16)] * 2
-    scratch += [dma((6, RING)), dma((6, RING)), dma((RING,)), dma((RING,)), dma((RING,)), dma((10,)), dma((2, 2)), dma((2,))]
-    scratch += [dma((10,)), dma((2,)), dma((SLOTS,)), dma((SLOTS,)), dma((RING,)), dma((RING,)), dma((6, RING)),
-                dma((6, RING)), dma((2,)), pltpu.SemaphoreType.REGULAR((7,))]
+    scratch += [dma((SIXTH, RING)), dma((SIXTH, RING)), dma((RING,)), dma((RING,)), dma((RING,)), dma((10,)), dma((2, 2)), dma((2,))]
+    scratch += [dma((10,)), dma((2,)), dma((SLOTS,)), dma((SLOTS,)), dma((RING,)), dma((RING,)), dma((SIXTH, RING)),
+                dma((SIXTH, RING)), dma((2, n_layers)), dma((2, n_layers)), pltpu.SemaphoreType.REGULAR((7,))]
     return pl.pallas_call(
         functools.partial(train_kernel, n_layers), name="train_stack",
-        out_shape=(shape((seq, width), bf16), shape((seq, width), bf16), shape((2, n_layers, ROWS // 2, UP_END), f32),
-                   shape((n_layers, ROWS, PER_HALF * COLS), f32)) + saved,
-        in_specs=[hbm, hbm, vmem, vmem], out_specs=(hbm,) + (vmem,) * 3 + (hbm,) * len(saved), scratch_shapes=scratch,
+        out_shape=(shape((seq, width), bf16), shape((seq, width), bf16), shape((2, n_layers, HALF_ROWS, UP_END), f32),
+                   shape(down.shape, f32)) + saved,
+        in_specs=[hbm, hbm, vmem, vmem], out_specs=(hbm,) * (4 + len(saved)), scratch_shapes=scratch,
         compiler_params=pltpu.CompilerParams(collective_id=0, has_side_effects=True, vmem_limit_bytes=VMEM_LIMIT),
     )(x_loc, g_loc, rows, down)[:4]
 
@@ -788,7 +832,7 @@
     for half in TWO:
         for part in COLORS:
             for chip in range(chips):
-                packed = chips * ROWS * (3 * half + part) + ROWS * chip
+                packed = chips * ROWS * (STAGES * half + part) + ROWS * chip
                 plain = block * (2 * chip + half) + ROWS * part
                 pair = (packed, plain) if packed_first else (plain, packed)
                 moves.append(pair + (min(ROWS, block - ROWS * part),))
@@ -819,103 +863,129 @@
     return slice(size * index, size * index + size)
 
 
-def pack_kernel(chips, q_ref, k_ref, v_ref, o_ref, up_ref, down_ref, rows_out, down_out, wide):
-    rows, layers, cols = up_ref.shape
+def _moved(pairs, sems):
+    copies = [pltpu.make_async_copy(source, target, sems.at[order]) for order, (source, target) in enumerate(pairs)]
+    for copy in copies:
+        copy.start()
+    return copies
+
+
+def _all_done(copies):
+    for copy in copies:
+        copy.wait()
+
+
+def _head_spots(heads):
+    return [[(head, 0, heads * half + head) for head in range(heads)]
+            + [(heads + 2 + head, 3, heads * half + head) for head in range(heads)] for half in TWO]
+
+
+def pack_kernel(chips, *refs):
+    sources, (rows_hbm, down_hbm), arrays, refs = refs[:6], refs[6:8], refs[8:14], refs[14:]
+    rows_out, down_out, wide, in_sems, out_sems = refs
+    k_ref, v_ref, up_ref, down_ref = arrays[1], arrays[2], arrays[4], arrays[5]
+    rows, layers, _ = up_ref.shape
     block, _, width = down_ref.shape
-    heads = q_ref.shape[1] // 2
-    for half in TWO:
+    heads = arrays[0].shape[1] // 2
+    half_f = STAGES * chips * ROWS
+    inward = _moved(zip(sources, arrays), in_sems)
+    _all_done(inward[:QKV])
+    for half, spots in enumerate(_head_spots(heads)):
+        for at, which, head in spots:
+            rows_out[half, :, :, _span(at, LANES)] = jnp.swapaxes(
+                arrays[which][:, head].astype(jnp.float32), 0, 1).astype(jnp.bfloat16)
         for layer in range(layers):
-            for at, ref in ((0, q_ref), (heads + 2, o_ref)):
-                for head in range(heads):
-                    rows_out[half, layer, :, _span(at + head, LANES)] = ref[
-                        :, heads * half + head].astype(jnp.float32)[:, layer].astype(jnp.bfloat16)
             for at, ref in ((heads, k_ref), (heads + 1, v_ref)):
                 rows_out[half, layer, :, _span(at, LANES)] = ref[layer].astype(
                     jnp.float32)[:, half].astype(jnp.bfloat16)
-    for tile in range(cols // LANES):
-        both = up_ref[:, :, _span(tile, LANES)].astype(jnp.float32)
-        for layer in range(layers):
-            wide[layer, :, _span(tile, LANES)] = both[:, layer]
+    inward[QKV].wait()
+    wide[ALL] = jnp.swapaxes(up_ref[ALL].astype(jnp.float32), 0, 1)
     lane = lax.broadcasted_iota(jnp.int32, (layers, rows, LANES), 2)
-    half_f = 3 * chips * ROWS
-    for index, tile in enumerate(_pieces(_moves(chips, block, True), 2 * half_f)):
-        value = _gather_tile(lambda source: wide[:, :, _span(source, LANES)], tile, lane)
-        half, at = divmod(LANES * index, half_f)
-        if at >= 2 * chips * ROWS:
-            position = lax.rem(lane + LANES * index % ROWS, ROWS)
-            value = jnp.where(position < block - 2 * ROWS, value, 0.0)
-        start = ATTN * COLS + at
-        rows_out[half, :, :, start:start + LANES] = value.astype(jnp.bfloat16)
+    tiles = _pieces(_moves(chips, block, True), 2 * half_f)
+    outward = []
+    for half in TWO:
+        for index in range(half_f // LANES):
+            tile = tiles[half * (half_f // LANES) + index]
+            value = _gather_tile(lambda source: wide[:, :, _span(source, LANES)], tile, lane)
+            if LANES * index >= 2 * chips * ROWS:
+                position = lax.rem(lane + LANES * index % ROWS, ROWS)
+                value = jnp.where(position < block - 2 * ROWS, value, 0.0)
+            rows_out[half, :, :, _span(2 * ATTN + index, LANES)] = value.astype(jnp.bfloat16)
+        outward += _moved([(rows_out.at[half], rows_hbm.at[half])], out_sems.at[half:half + 1])
+    inward[5].wait()
     for part in COLORS:
         used = min(ROWS, block - ROWS * part)
-        value = down_ref[ROWS * part:ROWS * part + used].astype(jnp.float32)
+        both = jnp.swapaxes(down_ref[ROWS * part:ROWS * part + used].astype(jnp.float32), 0, 1)
         for layer in range(layers):
-            one = value[:, layer]
+            one = both[layer]
             if used < ROWS:
                 one = jnp.concatenate([one, jnp.zeros((ROWS - used, width), jnp.float32)], axis=0)
             down_out[layer, :, _span(part, width)] = one.astype(jnp.bfloat16)
+    _all_done(outward + _moved([(down_out, down_hbm)], out_sems.at[2:3]))
+
+
+def _bounced(kernel, name, inputs, outs, arrays, n_sems):
+    hbm = pl.BlockSpec(memory_space=pl.ANY)
+    scratch = [pltpu.VMEM(array.shape, array.dtype) for array in arrays]
+    return pl.pallas_call(
+        kernel, name=name, out_shape=tuple(outs), in_specs=[hbm] * len(inputs), out_specs=(hbm,) * len(outs),
+        scratch_shapes=scratch + [pltpu.SemaphoreType.DMA((size,)) for size in n_sems],
+        compiler_params=pltpu.CompilerParams(vmem_limit_bytes=VMEM_LIMIT))(*inputs)
 
 
 def pack_weights(w_q, w_k, w_v, w_o, w_up, w_down, chips):
     layers, rows = w_up.shape[:2]
-    width = w_down.shape[2]
-    vmem = pl.BlockSpec(memory_space=pltpu.VMEM)
     shape = jax.ShapeDtypeStruct
-    return pl.pallas_call(
-        functools.partial(pack_kernel, chips), name="pack_weights",
-        out_shape=(shape((2, layers, rows, UP_END), jnp.bfloat16), shape((layers, ROWS, 3 * width), jnp.bfloat16)),
-        in_specs=[vmem] * 6, out_specs=(vmem,) * 2,
-        scratch_shapes=[pltpu.VMEM(w_up.shape, jnp.float32)],
-        compiler_params=pltpu.CompilerParams(vmem_limit_bytes=VMEM_LIMIT),
-    )(w_q.transpose(1, 2, 0, 3), w_k, w_v, w_o.transpose(1, 2, 0, 3), w_up.transpose(1, 0, 2),
-      w_down.transpose(1, 0, 2))
-
-
-def unpack_kernel(chips, rows_ref, down_ref, y_ref, dx_ref, q_out, k_out, v_out, o_out, up_out, down_out, y_out,
-                  dx_out):
+    inputs = [w_q.transpose(1, 2, 0, 3), w_k, w_v, w_o.transpose(1, 2, 0, 3), w_up.transpose(1, 0, 2),
+              w_down.transpose(1, 0, 2)]
+    outs = [shape((2, layers, rows, UP_END), jnp.bfloat16), shape((layers, ROWS, 3 * w_down.shape[2]), jnp.bfloat16)]
+    return _bounced(functools.partial(pack_kernel, chips), "pack_weights", inputs, outs,
+                    inputs + outs + [shape(w_up.shape, jnp.float32)], (6, 3))
+
+
+def unpack_kernel(chips, *refs):
+    sources, results, arrays, (in_sems, out_sems) = refs[:4], refs[4:12], refs[12:22], refs[22:]
+    rows_ref, down_ref, q_out, k_out, v_out, o_out, up_out, down_out = arrays[:2] + arrays[4:]
     rows, layers, cols = up_out.shape
     block, _, width = down_out.shape
     heads = q_out.shape[1] // 2
-    for half in TWO:
+    inward = _moved(zip(sources, arrays), in_sems)
+    inward[0].wait()
+    for half, spots in enumerate(_head_spots(heads)):
+        for at, which, head in spots:
+            (q_out, o_out)[which // 3][:, head] = jnp.swapaxes(rows_ref[half, :, :, _span(at, LANES)], 0, 1)
         for layer in range(layers):
-            for at, ref in ((0, q_out), (heads + 2, o_out)):
-                for head in range(heads):
-                    ref[:, heads * half + head, layer, :] = rows_ref[half, layer, :, _span(at + head, LANES)]
             for at, ref in ((heads, k_out), (heads + 1, v_out)):
                 ref[layer, :, half, :] = rows_ref[half, layer, :, _span(at, LANES)]
+    outward = _moved(zip((q_out, k_out, v_out, o_out), results), out_sems)
     lane = lax.broadcasted_iota(jnp.int32, (layers, rows, LANES), 2)
-    half_f = 3 * chips * ROWS
+    per_half = STAGES * chips * ROWS // LANES
 
     def load(source):
-        half, at = divmod(LANES * source, half_f)
-        return rows_ref[half, :, :, ATTN * COLS + at:ATTN * COLS + at + LANES]
+        half, tile = divmod(source, per_half)
+        return rows_ref[half, :, :, _span(2 * ATTN + tile, LANES)]
 
     for index, tile in enumerate(_pieces(_moves(chips, block, False), cols)):
-        value = _gather_tile(load, tile, lane)
-        for layer in range(layers):
-            up_out[:, layer, _span(index, LANES)] = value[layer]
+        up_out[:, :, _span(index, LANES)] = jnp.swapaxes(_gather_tile(load, tile, lane), 0, 1)
+    _all_done(inward[1:])
+    outward += _moved(zip((up_out,) + arrays[2:4], results[4:5] + results[6:]), out_sems.at[QKV:])
     for part in COLORS:
         used = min(ROWS, block - ROWS * part)
         for layer in range(layers):
-            down_out[ROWS * part:ROWS * part + used, layer, :] = down_ref[layer, :used, UP_END + width * part:UP_END + width * part + width]
-    y_out[ALL] = y_ref[ALL]
-    dx_out[ALL] = dx_ref[ALL]
+            down_out[ROWS * part:ROWS * part + used, layer, :] = down_ref[layer, :used, _span(part, width)]
+    _all_done(outward + _moved([(down_out, results[5])], out_sems.at[ATTN:]))
 
 
 def unpack_grads(row_grad, down_grad, y_loc, grad_x, shapes, chips):
-    vmem = pl.BlockSpec(memory_space=pltpu.VMEM)
     q_shape, k_shape, _, _, up_shape, down_shape = shapes
     layers, rows, heads, head_dim = q_shape
+    shape = jax.ShapeDtypeStruct
     turned = [(rows, heads, layers, head_dim), k_shape, k_shape, (rows, heads, layers, head_dim),
               (rows, layers, up_shape[2]), (down_shape[1], layers, down_shape[2])]
-    shape = jax.ShapeDtypeStruct
-    outs = pl.pallas_call(
-        functools.partial(unpack_kernel, chips), name="unpack_grads",
-        out_shape=tuple(shape(full, jnp.float32) for full in turned) + tuple(
-            shape(value.shape, value.dtype) for value in (y_loc, grad_x)),
-        in_specs=[vmem] * 4, out_specs=(vmem,) * 8,
-        compiler_params=pltpu.CompilerParams(vmem_limit_bytes=VMEM_LIMIT),
-    )(row_grad, down_grad, y_loc, grad_x)
+    turned = [shape(full, jnp.float32) for full in turned]
+    inputs = [row_grad, down_grad, y_loc, grad_x]
+    outs = _bounced(functools.partial(unpack_kernel, chips), "unpack_grads", inputs,
+                    turned + [shape(value.shape, value.dtype) for value in (y_loc, grad_x)], inputs + turned, (4, 8))
     d_q, d_k, d_v, d_o, d_up, d_down, y_out, dx_out = outs
     return (y_out[None], dx_out[None], d_q.transpose(2, 0, 1, 3), d_k, d_v, d_o.transpose(2, 0, 1, 3),
             d_up.transpose(1, 0, 2), d_down.transpose(1, 0, 2))

time: 534 us -> 530 us (level)
  no operation moved by 1% of the time
where the time goes in v10:
time: 530 us
  Pallas kernels  529 us (100%)
    pallas_call x1, Pallas kernels, train_stack(): pl.pallas_call(functools.partial(train_kernel, n_layers), name='train_sta...  521 us

profile of v10, /device:TPU:1, one launch (start us, length us, event | category | flops | bytes accessed | tf_op | source)
XLA Modules:
  0.0 529.9 jit_solution(14977896939793890468)
XLA Ops:
  0.6 3.4 pack_weights.1
  4.1 520.5 %train_stack.1 = (bf16[192,1536]{1,0:T(8,128)(2,1)}, bf16[192,1536]{1,0:T(8,128)(2,1)}, f32[2,2,12,6400]{3,2,1,0:T(8,128)}, f32[2,24,4608]{2,1,0:T(8,128)}, bf16...) custom-call(bf16[192,1536]{1,0:T(8,128)(2,1)} %bitcast.12, ...), custom_call_target="tpu_custom_call" | custom-call | tf_op jit(solution)/shard_map/train_stack/pallas_call | solution.py:818
  524.6 5.4 %unpack_grads.1 = (f32[12,12,2,128]{3,2,1,0:T(2,128)}, f32[2,12,2,128]{3,2,1,0:T(2,128)}, f32[2,12,2,128]{3,2,1,0:T(2,128)}, f32[12,12,2,128]{3,2,1,0:T(2,128)},...) custom-call(f32[2,2,12,6400]{3,2,1,0:T(8,128)} %get-tuple-element.24.re, ...), custom_call_target="tpu_custom_call" | custom-call | tf_op jit(solution)/shard_map/unpack_grads/pallas_call | solution.py:930

commit v11 on v10

--- a/solution.py
+++ b/solution.py
@@ -80,7 +80,17 @@
 
 
 def _causal(seq):
-    return (lax.broadcasted_iota(jnp.int32, (seq, seq), 0) >= lax.broadcasted_iota(jnp.int32, (seq, seq), 1))
+    return (lax.rem(lax.broadcasted_iota(jnp.int32, (2 * seq, seq), 0), seq)
+            >= lax.broadcasted_iota(jnp.int32, (2 * seq, seq), 1))
+
+
+def _under(block):
+    return jnp.concatenate([block[:, :HEAD], block[:, HEAD:]], axis=0)
+
+
+def _beside(stacked):
+    seq = stacked.shape[0] // 2
+    return jnp.concatenate([stacked[:seq], stacked[seq:]], axis=1)
 
 
 def _probs(query, key, causal):
@@ -156,12 +166,22 @@
     seq = state.shape[0]
     third = CHIPS * ROWS
     last = n_layers - 1
-    swap = torus.remote(rows_ref.at[1 - core], twin, twin_sem.at[0], twin_sem.at[1], torus.sibling)
-    swap.start()
-    swap.wait_send()
-    swap.wait_recv()
+    pieces = [(0, EVERY, slice(0, FIFTH)), (0, EVERY, slice(FIFTH, None))] + [
+        (layer, EVERY, EVERY) for layer in range(1, n_layers)]
+    swaps = [torus.remote(rows_ref.at[(1 - core,) + piece], twin.at[piece], twin_sem.at[0, order], twin_sem.at[1, order],
+                          torus.sibling) for order, piece in enumerate(pieces)]
+    for swap in swaps:
+        swap.start()
+    swaps[0].wait_send()
+    swaps[0].wait_recv()
 
     def assemble(chunk):
+        @pl.when(chunk == 1)
+        def _():
+            for swap in swaps[1:]:
+                swap.wait_send()
+                swap.wait_recv()
+
         @pl.when(chunk < 5 * n_layers)
         def _():
             layer, part = chunk // 5, _rem(chunk, 5)
@@ -303,12 +323,9 @@
             causal = _causal(seq)
             for role, half in torus.sides:
                 key, value = k_buf[:, _at(HEAD * half, HEAD)], v_buf[:, _at(HEAD * half, HEAD)]
-                outs = []
-                for head in TWO:
-                    at = _at(STAGES * COLS * half + COLS * (index - QKV) + HEAD * head, HEAD)
-                    prob = _probs(q_buf[:, at], key, causal)
-                    outs.append(_dot(prob.astype(jnp.bfloat16), value).astype(jnp.bfloat16))
-                block = jnp.concatenate(outs, axis=1)
+                query = _under(q_buf[:, _at(STAGES * COLS * half + COLS * (index - QKV), COLS)])
+                prob = _probs(query, key, causal).astype(jnp.bfloat16)
+                block = _beside(_dot(prob, value).astype(jnp.bfloat16))
                 rights[O_AT + STAGES * half + index - QKV] = block
                 acc[ALL] += _dot_rhs_t(block, weights(role))
 
@@ -534,18 +551,15 @@
             for role, half in torus.sides:
                 d_o = _dot(lefts[GRAD], weights(role)).astype(jnp.bfloat16)
                 key, value = k_buf[:, _at(HEAD * half, HEAD)], v_buf[:, _at(HEAD * half, HEAD)]
-                d_q = []
-                for head in TWO:
-                    query = q_buf[:, _at(STAGES * COLS * half + COLS * (index - UP_DONE) + HEAD * head, HEAD)]
-                    d_head = d_o[:, HEAD * head:HEAD * head + HEAD]
-                    prob = _probs(query, key, causal)
-                    d_prob = _dot_rhs_t(d_head, value)
-                    dv_acc[half] += _dot_lhs_t(prob.astype(jnp.bfloat16), d_head)
-                    d_score = prob * (d_prob - jnp.sum(prob * d_prob, axis=-1, keepdims=True))
-                    d_score = (d_score * (HEAD ** -0.5)).astype(jnp.bfloat16)
-                    d_q.append(_dot(d_score, key).astype(jnp.bfloat16))
-                    dk_acc[half] += _dot_lhs_t(d_score, query)
-                rights[QKV_AT + QKV * half + index - UP_DONE] = jnp.concatenate(d_q, axis=1)
+                query = _under(q_buf[:, _at(STAGES * COLS * half + COLS * (index - UP_DONE), COLS)])
+                d_heads = _under(d_o)
+                prob = _probs(query, key, causal)
+                d_prob = _dot_rhs_t(d_heads, value)
+                dv_acc[half] += _dot_lhs_t(prob.astype(jnp.bfloat16), d_heads)
+                d_score = prob * (d_prob - jnp.sum(prob * d_prob, axis=-1, keepdims=True))
+                d_score = (d_score * (HEAD ** -0.5)).astype(jnp.bfloat16)
+                rights[QKV_AT + QKV * half + index - UP_DONE] = _beside(_dot(d_score, key).astype(jnp.bfloat16))
+                dk_acc[half] += _dot_lhs_t(d_score, query)
 
         @pl.when(index == O_DONE - 1)
         def _():
@@ -732,8 +746,6 @@
     turn_at = n_chunks
     backward = [(lag + turn_at, step) for lag, step in backward]
     n_ticks = turn_at + n_chunks + 7 * LAG
-    tail = 2
-
     def hand_over(layer, part):
         cols = _at(part * FIFTH, FIFTH)
         both = out[layer, :, cols]
@@ -773,13 +785,12 @@
                 def _(layer=layer):
                     rows_meet(layer)
 
-        @pl.when(now >= n_ticks - 5 + tail)
-        def _():
-            hand_over(0, now - n_ticks + 5)
+        @pl.when((now >= n_ticks - ATTN) & (now < n_ticks - ATTN + QKV))
+        def _():
+            hand_over(0, n_ticks - STAGES - now)
 
     torus.run(backward[:1] + forward + backward[1:], n_chunks, n_ticks, hand_on)
-    for part in range(tail):
-        hand_over(0, part)
+    hand_over(0, 0)
     rows_meet(0)
     for layer in range(n_layers):
         _all_done([down_result(layer), rows_result(layer)])
@@ -812,7 +823,7 @@
     for cols in (half, COLS):
         for size in ((RING, RING), (RING,), ()):
             scratch += [pltpu.VMEM((RING, 3, 2) + size + (TILE, cols), bf16)] * 2
-    scratch += [dma((SIXTH, RING)), dma((SIXTH, RING)), dma((RING,)), dma((RING,)), dma((RING,)), dma((10,)), dma((2, 2)), dma((2,))]
+    scratch += [dma((SIXTH, RING)), dma((SIXTH, RING)), dma((RING,)), dma((RING,)), dma((RING,)), dma((10,)), dma((2, 2)), dma((2, n_layers + 1))]
     scratch += [dma((10,)), dma((2,)), dma((SLOTS,)), dma((SLOTS,)), dma((RING,)), dma((RING,)), dma((SIXTH, RING)),
                 dma((SIXTH, RING)), dma((2, n_layers)), dma((2, n_layers)), pltpu.SemaphoreType.REGULAR((7,))]
     return pl.pallas_call(
@@ -949,31 +960,34 @@
     rows, layers, cols = up_out.shape
     block, _, width = down_out.shape
     heads = q_out.shape[1] // 2
-    inward = _moved(zip(sources, arrays), in_sems)
+    order = (1, 0, 2, 3)
+    inward = _moved([(sources[which], arrays[which]) for which in order], in_sems)
     inward[0].wait()
+    for part in COLORS:
+        used = min(ROWS, block - ROWS * part)
+        for layer in range(layers):
+            down_out[ROWS * part:ROWS * part + used, layer, :] = down_ref[layer, :used, _span(part, width)]
+    inward[1].wait()
+    outward = _moved([(down_out, results[5])], out_sems)
+    lane = lax.broadcasted_iota(jnp.int32, (layers, rows, LANES), 2)
+    per_half = STAGES * chips * ROWS // LANES
+
+    def load(source):
+        half, tile = divmod(source, per_half)
+        return rows_ref[half, :, :, _span(2 * ATTN + tile, LANES)]
+
+    _all_done(inward[2:])
+    outward += _moved(zip(arrays[2:4], results[6:]), out_sems.at[1:])
+    for index, tile in enumerate(_pieces(_moves(chips, block, False), cols)):
+        up_out[:, :, _span(index, LANES)] = jnp.swapaxes(_gather_tile(load, tile, lane), 0, 1)
+    outward += _moved([(up_out, results[4])], out_sems.at[STAGES:])
     for half, spots in enumerate(_head_spots(heads)):
         for at, which, head in spots:
             (q_out, o_out)[which // 3][:, head] = jnp.swapaxes(rows_ref[half, :, :, _span(at, LANES)], 0, 1)
         for layer in range(layers):
             for at, ref in ((heads, k_out), (heads + 1, v_out)):
                 ref[layer, :, half, :] = rows_ref[half, layer, :, _span(at, LANES)]
-    outward = _moved(zip((q_out, k_out, v_out, o_out), results), out_sems)
-    lane = lax.broadcasted_iota(jnp.int32, (layers, rows, LANES), 2)
-    per_half = STAGES * chips * ROWS // LANES
-
-    def load(source):
-        half, tile = divmod(source, per_half)
-        return rows_ref[half, :, :, _span(2 * ATTN + tile, LANES)]
-
-    for index, tile in enumerate(_pieces(_moves(chips, block, False), cols)):
-        up_out[:, :, _span(index, LANES)] = jnp.swapaxes(_gather_tile(load, tile, lane), 0, 1)
-    _all_done(inward[1:])
-    outward += _moved(zip((up_out,) + arrays[2:4], results[4:5] + results[6:]), out_sems.at[QKV:])
-    for part in COLORS:
-        used = min(ROWS, block - ROWS * part)
-        for layer in range(layers):
-            down_out[ROWS * part:ROWS * part + used, layer, :] = down_ref[layer, :used, _span(part, width)]
-    _all_done(outward + _moved([(down_out, results[5])], out_sems.at[ATTN:]))
+    _all_done(outward + _moved(zip((q_out, k_out, v_out, o_out), results), out_sems.at[QKV:]))
 
 
 def unpack_grads(row_grad, down_grad, y_loc, grad_x, shapes, chips):

time: 530 us -> 524 us (0.989)
    pallas_call x1, Pallas kernels: 521 us -> 515 us  [train_stack(): pl.pallas_call(functools.partial(train_kernel, n_layers), name='train_sta...]
where the time goes in v11:
time: 524 us
  Pallas kernels  524 us (100%)
    pallas_call x1, Pallas kernels, train_stack(): pl.pallas_call(functools.partial(train_kernel, n_layers), name='train_sta...  515 us

profile of v11, /device:TPU:1, one launch (start us, length us, event | category | flops | bytes accessed | tf_op | source)
XLA Modules:
  0.0 524.2 jit_solution(13790696295475363900)
XLA Ops:
  0.6 3.4 pack_weights.1
  4.1 514.8 %train_stack.1 = (bf16[192,1536]{1,0:T(8,128)(2,1)}, bf16[192,1536]{1,0:T(8,128)(2,1)}, f32[2,2,12,6400]{3,2,1,0:T(8,128)}, f32[2,24,4608]{2,1,0:T(8,128)}, bf16...) custom-call(bf16[192,1536]{1,0:T(8,128)(2,1)} %bitcast.12, ...), custom_call_target="tpu_custom_call" | custom-call | tf_op jit(solution)/shard_map/train_stack/pallas_call | solution.py:829
  518.9 5.3 %unpack_grads.1 = (f32[12,12,2,128]{3,2,1,0:T(2,128)}, f32[2,12,2,128]{3,2,1,0:T(2,128)}, f32[2,12,2,128]{3,2,1,0:T(2,128)}, f32[12,12,2,128]{3,2,1,0:T(2,128)},...) custom-call(f32[2,2,12,6400]{3,2,1,0:T(8,128)} %get-tuple-element.24.re, ...), custom_call_target="tpu_custom_call" | custom-call | tf_op jit(solution)/shard_map/unpack_grads/pallas_call | solution.py:941

commit v12 on v11

--- a/solution.py
+++ b/solution.py
@@ -47,6 +47,10 @@
 
 
 FIFTH = UP_END // 5
+GELU_A = 0.7978845608028654
+GELU_B = GELU_A * 0.044715
+GELU_C = 0.5 * GELU_A
+GELU_D = 1.5 * GELU_B
 GATHER_SLOTS = SIXTH * LAG + RING
 
 
@@ -321,13 +325,14 @@
         @pl.when((index >= QKV) & (index < ATTN))
         def _():
             causal = _causal(seq)
+            queries = [_under(q_buf[:, _at(STAGES * COLS * half + COLS * (index - QKV), COLS)]) for _, half in torus.sides]
+            probs = [_probs(queries[role], k_buf[:, _at(HEAD * half, HEAD)], causal).astype(jnp.bfloat16)
+                     for role, half in torus.sides]
+            blocks = [_beside(_dot(probs[role], v_buf[:, _at(HEAD * half, HEAD)]).astype(jnp.bfloat16))
+                      for role, half in torus.sides]
+            acc[ALL] += sum(_dot_rhs_t(blocks[role], weights(role)) for role in TWO)
             for role, half in torus.sides:
-                key, value = k_buf[:, _at(HEAD * half, HEAD)], v_buf[:, _at(HEAD * half, HEAD)]
-                query = _under(q_buf[:, _at(STAGES * COLS * half + COLS * (index - QKV), COLS)])
-                prob = _probs(query, key, causal).astype(jnp.bfloat16)
-                block = _beside(_dot(prob, value).astype(jnp.bfloat16))
-                rights[O_AT + STAGES * half + index - QKV] = block
-                acc[ALL] += _dot_rhs_t(block, weights(role))
+                rights[O_AT + STAGES * half + index - QKV] = blocks[role]
 
         @pl.when(index == ATTN - 1)
         def _():
@@ -485,9 +490,9 @@
             for block in SIX:
                 cols = slice(COLS * block, COLS * block + COLS)
                 hidden = hid_buf[:, cols]
-                bend = jnp.tanh(0.7978845608028654 * (hidden + 0.044715 * (hidden * hidden * hidden)))
-                slope = 0.5 * (1.0 + bend) + 0.5 * hidden * (1.0 - bend * bend) * (
-                    0.7978845608028654 * (1.0 + 0.134145 * (hidden * hidden)))
+                square = hidden * hidden
+                bend = jnp.tanh(hidden * (GELU_A + GELU_B * square))
+                slope = (0.5 + 0.5 * bend) + (hidden * (1.0 - bend * bend)) * (GELU_C + GELU_D * square)
                 rights[DH_AT + FF * half + SIXTH * part + block] = (dact[half, :, cols] * slope).astype(jnp.bfloat16)
 
         @pl.when((index > 0) & (index <= DOWN_DONE) & (_rem(index, SIXTH) == 0))
@@ -501,8 +506,9 @@
 
         @pl.when(index < DOWN_DONE)
         def _():
+            products = [_dot_rhs_t(rights[_rem(index, SIXTH)], weights(role)) for role in TWO]
             for role, half in torus.sides:
-                dact[half] += _dot_rhs_t(rights[_rem(index, SIXTH)], weights(role))
+                dact[half] += products[role]
 
         @pl.when((index < DOWN_DONE) & (_rem(index, SIXTH) == 5))
         def _():
@@ -548,18 +554,23 @@
         @pl.when((index >= UP_DONE) & (index < O_DONE))
         def _():
             causal = _causal(seq)
+            keys = [k_buf[:, _at(HEAD * half, HEAD)] for _, half in torus.sides]
+            values = [v_buf[:, _at(HEAD * half, HEAD)] for _, half in torus.sides]
+            queries = [_under(q_buf[:, _at(STAGES * COLS * half + COLS * (index - UP_DONE), COLS)])
+                       for _, half in torus.sides]
+            probs = [_probs(queries[role], keys[role], causal) for role in TWO]
+            d_heads = [_under(_dot(lefts[GRAD], weights(role)).astype(jnp.bfloat16)) for role in TWO]
+            d_probs = [_dot_rhs_t(d_heads[role], values[role]) for role in TWO]
+            d_scores = [probs[role] * (d_probs[role] - jnp.sum(probs[role] * d_probs[role], axis=-1, keepdims=True))
+                        for role in TWO]
+            d_scores = [(d_score * (HEAD ** -0.5)).astype(jnp.bfloat16) for d_score in d_scores]
+            d_v = [_dot_lhs_t(probs[role].astype(jnp.bfloat16), d_heads[role]) for role in TWO]
+            d_k = [_dot_lhs_t(d_scores[role], queries[role]) for role in TWO]
+            d_q = [_beside(_dot(d_scores[role], keys[role]).astype(jnp.bfloat16)) for role in TWO]
             for role, half in torus.sides:
-                d_o = _dot(lefts[GRAD], weights(role)).astype(jnp.bfloat16)
-                key, value = k_buf[:, _at(HEAD * half, HEAD)], v_buf[:, _at(HEAD * half, HEAD)]
-                query = _under(q_buf[:, _at(STAGES * COLS * half + COLS * (index - UP_DONE), COLS)])
-                d_heads = _under(d_o)
-                prob = _probs(query, key, causal)
-                d_prob = _dot_rhs_t(d_heads, value)
-                dv_acc[half] += _dot_lhs_t(prob.astype(jnp.bfloat16), d_heads)
-                d_score = prob * (d_prob - jnp.sum(prob * d_prob, axis=-1, keepdims=True))
-                d_score = (d_score * (HEAD ** -0.5)).astype(jnp.bfloat16)
-                rights[QKV_AT + QKV * half + index - UP_DONE] = _beside(_dot(d_score, key).astype(jnp.bfloat16))
-                dk_acc[half] += _dot_lhs_t(d_score, query)
+                dv_acc[half] += d_v[role]
+                dk_acc[half] += d_k[role]
+                rights[QKV_AT + QKV * half + index - UP_DONE] = d_q[role]
 
         @pl.when(index == O_DONE - 1)
         def _():

time: 524 us -> 522 us (level)
  no operation moved by 1% of the time
where the time goes in v12:
time: 522 us
  Pallas kernels  522 us (100%)
    pallas_call x1, Pallas kernels, train_stack(): pl.pallas_call(functools.partial(train_kernel, n_layers), name='train_sta...  513 us

profile of v12, /device:TPU:1, one launch (start us, length us, event | category | flops | bytes accessed | tf_op | source)
XLA Modules:
  0.0 522.2 jit_solution(3472301609578583680)
XLA Ops:
  0.6 3.4 pack_weights.1
  4.1 512.9 %train_stack.1 = (bf16[192,1536]{1,0:T(8,128)(2,1)}, bf16[192,1536]{1,0:T(8,128)(2,1)}, f32[2,2,12,6400]{3,2,1,0:T(8,128)}, f32[2,24,4608]{2,1,0:T(8,128)}, bf16...) custom-call(bf16[192,1536]{1,0:T(8,128)(2,1)} %bitcast.12, ...), custom_call_target="tpu_custom_call" | custom-call | tf_op jit(solution)/shard_map/train_stack/pallas_call | solution.py:840
  516.9 5.3 %unpack_grads.1 = (f32[12,12,2,128]{3,2,1,0:T(2,128)}, f32[2,12,2,128]{3,2,1,0:T(2,128)}, f32[2,12,2,128]{3,2,1,0:T(2,128)}, f32[12,12,2,128]{3,2,1,0:T(2,128)},...) custom-call(f32[2,2,12,6400]{3,2,1,0:T(8,128)} %get-tuple-element.24.re, ...), custom_call_target="tpu_custom_call" | custom-call | tf_op jit(solution)/shard_map/unpack_grads/pallas_call | solution.py:952

commit v13 on v12

--- a/solution.py
+++ b/solution.py
@@ -51,7 +51,9 @@
 GELU_B = GELU_A * 0.044715
 GELU_C = 0.5 * GELU_A
 GELU_D = 1.5 * GELU_B
-GATHER_SLOTS = SIXTH * LAG + RING
+AHEAD = 7
+GATHER_SLOTS = 22
+MANY = 16
 
 
 def _rows(color):
@@ -144,10 +146,23 @@
                 for _, _, mine in self.partners:
                     pl.semaphore_wait(self.credit.at[mine], 1)
 
-            for lag, action in steps:
-                @pl.when((now >= lag) & (now < lag + n_chunks))
-                def _(lag=lag, action=action):
-                    action(now - lag)
+            for lag, action, early in steps:
+                beat = now - lag
+                if not early:
+                    @pl.when((beat >= 0) & (beat < n_chunks))
+                    def _(beat=beat, action=action):
+                        action(beat)
+                    continue
+                double = beat < AHEAD
+
+                @pl.when((beat >= 0) & (beat < n_chunks - AHEAD))
+                def _(beat=beat, double=double, action=action):
+                    first = jnp.where(double, 2 * beat, beat + AHEAD)
+
+                    def one(order, inner):
+                        action(first + order)
+                        return inner
+                    lax.fori_loop(0, jnp.where(double, 2, 1), one, 0)
             after(now)
 
             @pl.when(now < n_ticks - 2)
@@ -210,7 +225,7 @@
     halves = (slice(0, WIDE), slice(WIDE, COLS))
 
     def send_own(stage, chunk):
-        slot, sem = _rem(chunk, slots), _rem(chunk, RING)
+        slot, sem = _rem(chunk, slots), _rem(chunk, MANY)
         for color in COLORS:
             dim = ORDERS[color][stage]
             here = spot(slot, color, stage, place[dim], slice(0, COLS))
@@ -222,7 +237,7 @@
                              {dim: near[way][dim]}).start()
 
     def send_far(stage, chunk):
-        slot, sem = _rem(chunk, slots), _rem(chunk, RING)
+        slot, sem = _rem(chunk, slots), _rem(chunk, MANY)
         for color in COLORS:
             dim = ORDERS[color][stage]
             for way in TWO:
@@ -231,7 +246,7 @@
                              {dim: near[way][dim]}).start()
 
     def arrived(part, chunk):
-        slot, sem = _rem(chunk, slots), _rem(chunk, RING)
+        slot, sem = _rem(chunk, slots), _rem(chunk, MANY)
         count = slice(0, 2) if part % 2 == 0 else 0
         block = wbuf.at[(slot,) + (0,) * (2 - part // 2) + (count,)]
         whole = torus.remote(block, block, ring_send.at[part, sem], ring_recv.at[part, sem], torus.sibling)
@@ -393,9 +408,9 @@
 
         keep_copy(chunk).wait()
 
-    steps = [(0, assemble), (0, enter)]
-    steps += [((part + 1) * LAG, functools.partial(pass_on, part)) for part in range(5)]
-    return steps + [(ready, exchange), (ready + 1, compute)]
+    steps = [(0, assemble, False), (0, enter, True)]
+    steps += [((part + 1) * LAG, functools.partial(pass_on, part), part < STAGES) for part in range(5)]
+    return steps + [(ready, exchange, False), (ready + 1, compute, False)]
 
 
 def backward_steps(torus, n_layers, x_ref, x_out, saved, out, wbuf, lefts, rights, hid_buf, dact, dnorm, q_buf,
@@ -408,17 +423,17 @@
     last = n_layers - 1
 
     def mine_slot(chunk):
-        return GATHER_SLOTS + _rem(chunk, 2)
+        return GATHER_SLOTS - 2 + _rem(chunk, 2)
 
     def out_slot(chunk):
-        return GATHER_SLOTS + 2 + _rem(chunk, 2)
+        return _rem(chunk, 2)
 
     def their_slot(chunk):
-        return 7 + _rem(chunk, SLOTS)
+        return 5 + _rem(chunk, SLOTS)
 
     def peer_slot(chunk):
         order = _rem(chunk, RING)
-        return jnp.where(order == 0, 6, jnp.where(order == 3, 10, GATHER_SLOTS + 3 + order))
+        return jnp.where(order == 3, 8, 2 + order)
 
     def pair_of(chunk):
         return last - chunk // PER_HALF
@@ -755,7 +770,7 @@
                               q_buf, k_buf, v_buf, x_buf, dk_acc, dv_acc, sums, half_bufs, full_bufs,
                               *backward_sems)
     turn_at = n_chunks
-    backward = [(lag + turn_at, step) for lag, step in backward]
+    backward = [(lag + turn_at, step, False) for lag, step in backward]
     n_ticks = turn_at + n_chunks + 7 * LAG
     def hand_over(layer, part):
         cols = _at(part * FIFTH, FIFTH)
@@ -825,7 +840,7 @@
              shape((n_layers, SIXTH, seq, COLS), bf16))
     scratch = [pltpu.VMEM(full, kind) for full, kind in (
         ((2, n_layers, HALF_ROWS, UP_END), f32), ((n_layers, ROWS, PER_HALF * COLS), f32),
-        ((GATHER_SLOTS + 6,) + chunk, bf16), ((RING,) + chunk, bf16), ((n_layers, ROWS, PER_HALF * COLS), bf16),
+        ((GATHER_SLOTS,) + chunk, bf16), ((RING,) + chunk, bf16), ((n_layers, ROWS, PER_HALF * COLS), bf16),
         (rows.shape[1:], bf16), ((seq, width), bf16), ((9, seq, width), bf16), ((56, seq, COLS), bf16),
         ((seq, SIXTH * COLS), bf16), ((seq, 2 * HEAD), bf16), ((seq, 2 * HEAD), bf16), ((2, 2, seq, COLS), f32),
         ((seq, width), f32), ((seq, width), f32), ((2, seq, width), f32), ((seq, width), bf16),
@@ -834,7 +849,7 @@
     for cols in (half, COLS):
         for size in ((RING, RING), (RING,), ()):
             scratch += [pltpu.VMEM((RING, 3, 2) + size + (TILE, cols), bf16)] * 2
-    scratch += [dma((SIXTH, RING)), dma((SIXTH, RING)), dma((RING,)), dma((RING,)), dma((RING,)), dma((10,)), dma((2, 2)), dma((2, n_layers + 1))]
+    scratch += [dma((SIXTH, MANY)), dma((SIXTH, MANY)), dma((RING,)), dma((RING,)), dma((RING,)), dma((10,)), dma((2, 2)), dma((2, n_layers + 1))]
     scratch += [dma((10,)), dma((2,)), dma((SLOTS,)), dma((SLOTS,)), dma((RING,)), dma((RING,)), dma((SIXTH, RING)),
                 dma((SIXTH, RING)), dma((2, n_layers)), dma((2, n_layers)), pltpu.SemaphoreType.REGULAR((7,))]
     return pl.pallas_call(
@@ -966,20 +981,27 @@
 
 
 def unpack_kernel(chips, *refs):
-    sources, results, arrays, (in_sems, out_sems) = refs[:4], refs[4:12], refs[12:22], refs[22:]
-    rows_ref, down_ref, q_out, k_out, v_out, o_out, up_out, down_out = arrays[:2] + arrays[4:]
+    sources, results, arrays, (in_sems, out_sems, down_sems) = refs[:4], refs[4:12], refs[12:23], refs[23:]
+    rows_ref, down_ref, q_out, k_out, v_out, o_out, up_out, down_out = arrays[:2] + arrays[4:10]
+    short = arrays[10]
     rows, layers, cols = up_out.shape
     block, _, width = down_out.shape
     heads = q_out.shape[1] // 2
     order = (1, 0, 2, 3)
     inward = _moved([(sources[which], arrays[which]) for which in order], in_sems)
     inward[0].wait()
+    pairs = []
     for part in COLORS:
         used = min(ROWS, block - ROWS * part)
         for layer in range(layers):
-            down_out[ROWS * part:ROWS * part + used, layer, :] = down_ref[layer, :used, _span(part, width)]
+            source = down_ref.at[layer, :, _span(part, width)]
+            if used < ROWS:
+                short[layer] = down_ref[layer, :used, _span(part, width)]
+                source = short.at[layer]
+            pairs.append((source,
+                          results[5].at[ROWS * part:ROWS * part + used, layer, :]))
+    outward = _moved(pairs, down_sems)
     inward[1].wait()
-    outward = _moved([(down_out, results[5])], out_sems)
     lane = lax.broadcasted_iota(jnp.int32, (layers, rows, LANES), 2)
     per_half = STAGES * chips * ROWS // LANES
 
@@ -1010,7 +1032,7 @@
     turned = [shape(full, jnp.float32) for full in turned]
     inputs = [row_grad, down_grad, y_loc, grad_x]
     outs = _bounced(functools.partial(unpack_kernel, chips), "unpack_grads", inputs,
-                    turned + [shape(value.shape, value.dtype) for value in (y_loc, grad_x)], inputs + turned, (4, 8))
+                    turned + [shape(value.shape, value.dtype) for value in (y_loc, grad_x)], inputs + turned + [shape((layers, down_shape[1] - 2 * ROWS, down_shape[2]), jnp.float32)], (4, 8, 6))
     d_q, d_k, d_v, d_o, d_up, d_down, y_out, dx_out = outs
     return (y_out[None], dx_out[None], d_q.transpose(2, 0, 1, 3), d_k, d_v, d_o.transpose(2, 0, 1, 3),
             d_up.transpose(1, 0, 2), d_down.transpose(1, 0, 2))

time: 522 us -> 525 us (level)
  no operation moved by 1% of the time
where the time goes in v13:
time: 525 us; the launch traced here: 524 us
  Pallas kernels  524 us (100%)
    pallas_call x1, Pallas kernels, train_stack(): pl.pallas_call(functools.partial(train_kernel, n_layers), name='train_sta...  515 us

profile of v13, /device:TPU:1, one launch (start us, length us, event | category | flops | bytes accessed | tf_op | source)
XLA Modules:
  0.0 524.5 jit_solution(8522470676978881280)
XLA Ops:
  0.6 3.4 pack_weights.1
  4.1 514.9 %train_stack.1 = (bf16[192,1536]{1,0:T(8,128)(2,1)}, bf16[192,1536]{1,0:T(8,128)(2,1)}, f32[2,2,12,6400]{3,2,1,0:T(8,128)}, f32[2,24,4608]{2,1,0:T(8,128)}, bf16...) custom-call(bf16[192,1536]{1,0:T(8,128)(2,1)} %bitcast.12, ...), custom_call_target="tpu_custom_call" | custom-call | tf_op jit(solution)/shard_map/train_stack/pallas_call | solution.py:855
  519.0 5.3 %unpack_grads.1 = (f32[12,12,2,128]{3,2,1,0:T(2,128)}, f32[2,12,2,128]{3,2,1,0:T(2,128)}, f32[2,12,2,128]{3,2,1,0:T(2,128)}, f32[12,12,2,128]{3,2,1,0:T(2,128)},...) custom-call(f32[2,2,12,6400]{3,2,1,0:T(8,128)} %get-tuple-element.24.re, ...), custom_call_target="tpu_custom_call" | custom-call | tf_op jit(solution)/shard_map/unpack_grads/pallas_call | solution.py:967

commit v14 on v12

--- a/solution.py
+++ b/solution.py
@@ -721,9 +721,9 @@
             (7 * LAG, functools.partial(turn, 2)), (1, consume), (0, multiply)]
 
 
-def train_kernel(n_layers, x_ref, g_ref, rows_ref, down_ref, y_ref, dx_ref, rows_hbm, down_hbm, *refs):
+def train_kernel(n_layers, x_ref, g_ref, rows_in, down_in, y_ref, dx_ref, rows_hbm, down_hbm, *refs):
     saved, refs = refs[:9], refs[9:]
-    (rows_out, out), refs = refs[:2], refs[2:]
+    (rows_ref, down_ref, rows_out, out), refs = refs[:4], refs[4:]
     (wbuf, peer, shard, twin, state, lefts, rights, q_buf, k_buf, v_buf, hid_out_buf, acc, hid_in_buf, dact, x_buf,
      dk_acc, dv_acc, away), refs = refs[:18], refs[18:]
     sums, half_bufs, full_bufs, refs = refs[:3], refs[3:9], refs[9:15], refs[15:]
@@ -733,12 +733,14 @@
     torus = Torus(credit)
     core = torus.core
     n_chunks = n_layers * PER_HALF
+    inward = _moved([(rows_in, rows_ref), (down_in, down_ref)], backward_sems[0])
     fill = pltpu.make_async_copy(x_ref, state, forward_sems[5].at[9])
     fill.start()
     for block in SIX:
         pltpu.make_async_copy(g_ref.at[:, COLS * block:COLS * block + COLS], rights.at[block],
                               backward_sems[0].at[3]).start()
     torus.meet()
+    _all_done(inward)
     fill.wait()
     pltpu.make_async_copy(rights.at[:DH_AT], rights.at[:DH_AT], backward_sems[0].at[3]).wait()
     def y_copy():
@@ -824,6 +826,7 @@
              shape((n_layers, seq, 2 * HEAD), bf16), shape((n_layers, seq, 2 * HEAD), bf16),
              shape((n_layers, SIXTH, seq, COLS), bf16))
     scratch = [pltpu.VMEM(full, kind) for full, kind in (
+        (rows.shape, bf16), (down.shape, bf16),
         ((2, n_layers, HALF_ROWS, UP_END), f32), ((n_layers, ROWS, PER_HALF * COLS), f32),
         ((GATHER_SLOTS + 6,) + chunk, bf16), ((RING,) + chunk, bf16), ((n_layers, ROWS, PER_HALF * COLS), bf16),
         (rows.shape[1:], bf16), ((seq, width), bf16), ((9, seq, width), bf16), ((56, seq, COLS), bf16),
@@ -841,7 +844,7 @@
         functools.partial(train_kernel, n_layers), name="train_stack",
         out_shape=(shape((seq, width), bf16), shape((seq, width), bf16), shape((2, n_layers, HALF_ROWS, UP_END), f32),
                    shape(down.shape, f32)) + saved,
-        in_specs=[hbm, hbm, vmem, vmem], out_specs=(hbm,) * (4 + len(saved)), scratch_shapes=scratch,
+        in_specs=[hbm] * 4, out_specs=(hbm,) * (4 + len(saved)), scratch_shapes=scratch,
         compiler_params=pltpu.CompilerParams(collective_id=0, has_side_effects=True, vmem_limit_bytes=VMEM_LIMIT),
     )(x_loc, g_loc, rows, down)[:4]
 
@@ -971,8 +974,7 @@
     rows, layers, cols = up_out.shape
     block, _, width = down_out.shape
     heads = q_out.shape[1] // 2
-    order = (1, 0, 2, 3)
-    inward = _moved([(sources[which], arrays[which]) for which in order], in_sems)
+    inward = _moved([(sources[which], arrays[which]) for which in (1, 0)], in_sems)
     inward[0].wait()
     for part in COLORS:
         used = min(ROWS, block - ROWS * part)
@@ -987,11 +989,11 @@
         half, tile = divmod(source, per_half)
         return rows_ref[half, :, :, _span(2 * ATTN + tile, LANES)]
 
-    _all_done(inward[2:])
-    outward += _moved(zip(arrays[2:4], results[6:]), out_sems.at[1:])
+    through = _moved(zip(sources[2:], arrays[2:4]), in_sems.at[2:])
     for index, tile in enumerate(_pieces(_moves(chips, block, False), cols)):
         up_out[:, :, _span(index, LANES)] = jnp.swapaxes(_gather_tile(load, tile, lane), 0, 1)
-    outward += _moved([(up_out, results[4])], out_sems.at[STAGES:])
+    _all_done(through)
+    outward += _moved(zip(arrays[2:4] + (up_out,), results[6:] + results[4:5]), out_sems.at[1:])
     for half, spots in enumerate(_head_spots(heads)):
         for at, which, head in spots:
             (q_out, o_out)[which // 3][:, head] = jnp.swapaxes(rows_ref[half, :, :, _span(at, LANES)], 0, 1)

time: 522 us -> 523 us (level)
  no operation moved by 1% of the time
where the time goes in v14:
time: 523 us
  Pallas kernels  522 us (100%)
    pallas_call x1, Pallas kernels, train_stack(): pl.pallas_call(functools.partial(train_kernel, n_layers), name='train_sta...  512 us

profile of v14, /device:TPU:1, one launch (start us, length us, event | category | flops | bytes accessed | tf_op | source)
XLA Modules:
  0.0 522.8 jit_solution(16369299194187581070)
XLA Ops:
  0.6 3.4 pack_weights.1
  4.1 512.0 %train_stack.1 = (bf16[192,1536]{1,0:T(8,128)(2,1)}, bf16[192,1536]{1,0:T(8,128)(2,1)}, f32[2,2,12,6400]{3,2,1,0:T(8,128)}, f32[2,24,4608]{2,1,0:T(8,128)}, bf16...) custom-call(bf16[192,1536]{1,0:T(8,128)(2,1)} %bitcast.12, ...), custom_call_target="tpu_custom_call" | custom-call | tf_op jit(solution)/shard_map/train_stack/pallas_call | solution.py:843
  516.0 6.8 %unpack_grads.1 = (f32[12,12,2,128]{3,2,1,0:T(2,128)}, f32[2,12,2,128]{3,2,1,0:T(2,128)}, f32[2,12,2,128]{3,2,1,0:T(2,128)}, f32[12,12,2,128]{3,2,1,0:T(2,128)},...) custom-call(f32[2,2,12,6400]{3,2,1,0:T(8,128)} %get-tuple-element.24.re, ...), custom_call_target="tpu_custom_call" | custom-call | tf_op jit(solution)/shard_map/unpack_grads/pallas_call | solution.py:955

commit v15 on v14

--- a/solution.py
+++ b/solution.py
@@ -974,7 +974,8 @@
     rows, layers, cols = up_out.shape
     block, _, width = down_out.shape
     heads = q_out.shape[1] // 2
-    inward = _moved([(sources[which], arrays[which]) for which in (1, 0)], in_sems)
+    order = (1, 0, 2, 3)
+    inward = _moved([(sources[which], arrays[which]) for which in order], in_sems)
     inward[0].wait()
     for part in COLORS:
         used = min(ROWS, block - ROWS * part)
@@ -989,11 +990,11 @@
         half, tile = divmod(source, per_half)
         return rows_ref[half, :, :, _span(2 * ATTN + tile, LANES)]
 
-    through = _moved(zip(sources[2:], arrays[2:4]), in_sems.at[2:])
+    _all_done(inward[2:])
+    outward += _moved(zip(arrays[2:4], results[6:]), out_sems.at[1:])
     for index, tile in enumerate(_pieces(_moves(chips, block, False), cols)):
         up_out[:, :, _span(index, LANES)] = jnp.swapaxes(_gather_tile(load, tile, lane), 0, 1)
-    _all_done(through)
-    outward += _moved(zip(arrays[2:4] + (up_out,), results[6:] + results[4:5]), out_sems.at[1:])
+    outward += _moved([(up_out, results[4])], out_sems.at[STAGES:])
     for half, spots in enumerate(_head_spots(heads)):
         for at, which, head in spots:
             (q_out, o_out)[which // 3][:, head] = jnp.swapaxes(rows_ref[half, :, :, _span(at, LANES)], 0, 1)

time: 523 us -> 521 us (level)
  no operation moved by 1% of the time
where the time goes in v15:
time: 521 us
  Pallas kernels  521 us (100%)
    pallas_call x1, Pallas kernels, train_stack(): pl.pallas_call(functools.partial(train_kernel, n_layers), name='train_sta...  512 us

profile of v15, /device:TPU:1, one launch (start us, length us, event | category | flops | bytes accessed | tf_op | source)
XLA Modules:
  0.0 521.3 jit_solution(6858769532367987233)
XLA Ops:
  0.6 3.4 pack_weights.1
  4.1 512.0 %train_stack.1 = (bf16[192,1536]{1,0:T(8,128)(2,1)}, bf16[192,1536]{1,0:T(8,128)(2,1)}, f32[2,2,12,6400]{3,2,1,0:T(8,128)}, f32[2,24,4608]{2,1,0:T(8,128)}, bf16...) custom-call(bf16[192,1536]{1,0:T(8,128)(2,1)} %bitcast.12, ...), custom_call_target="tpu_custom_call" | custom-call | tf_op jit(solution)/shard_map/train_stack/pallas_call | solution.py:843
  516.0 5.3 %unpack_grads.1 = (f32[12,12,2,128]{3,2,1,0:T(2,128)}, f32[2,12,2,128]{3,2,1,0:T(2,128)}, f32[2,12,2,128]{3,2,1,0:T(2,128)}, f32[12,12,2,128]{3,2,1,0:T(2,128)},...) custom-call(f32[2,2,12,6400]{3,2,1,0:T(8,128)} %get-tuple-element.24.re, ...), custom_call_target="tpu_custom_call" | custom-call | tf_op jit(solution)/shard_map/unpack_grads/pallas_call | solution.py:955
